TPU v7x, 512 devices: a whole 4x8x8 slice. The times are simulated.
512 devices in a mesh: section: 4 (over x_hi, core), seq: 128 (over z, y, x_lo).
Axes of the slice: x: 4 (x_hi: 2, x_lo: 2; x = x_hi * 2 + x_lo), y: 8, z: 8, core: 2. Of those that a mesh axis runs over, the one named last changes fastest.
Arguments:
- hidden: bfloat16 [2, 16384, 2688], P(None, 'seq'), may hold values from -6 to 6
- lengths: int32 [2], replicated, may hold values from 8192 to 16384, as said below
- reward_pos: int32 [2], replicated, may hold values from 8064 to 16383, as said below
- in_gain: bfloat16 [2688], P('seq'), may hold values from 0.099609375 to 1.8984375
- w_query: bfloat16 [2688, 2048], P('seq', 'section'), may hold values from -0.077151675 to 0.077151675
- w_key: bfloat16 [2688, 1024], P('seq', 'section'), may hold values from -0.077151675 to 0.077151675
- w_value: bfloat16 [2688, 1024], P('seq', 'section'), may hold values from -0.125 to 0.125
- query_gain: float32 [128], replicated, may hold values from 0.6 to 7
- key_gain: float32 [128], replicated, may hold values from 0.6 to 7
- w_out: bfloat16 [2048, 2688], P('section', 'seq'), may hold values from -0.125 to 0.125
- post_gain: bfloat16 [2688], P('seq'), may hold values from 0.099609375 to 1.8984375
- final_gain: bfloat16 [2688], P('seq'), may hold values from 0.099609375 to 1.8984375
- value_head: bfloat16 [2688], P('seq'), may hold values from -0.125 to 0.125
Outputs:
- token_values: float32 [2, 16384], P(None, 'seq')
- reward: float32 [2], replicated
Inputs may be any that keep to these rules, and one draw needn't show every extreme that they name: `lengths`: in every draw at least one micro-batch has all 16384 tokens valid. reward_pos[m] lies among the last 128 valid tokens of micro-batch m.
All inputs are finite; a program needn't handle non-finite values.
Results may differ from a plain program's by a relative error of at most 0.01.
Values may be sent and summed in bfloat16 or wider, within the bound.
No kernel may reach another device: no remote copies, remote signals or barrier semaphores. Data moves between devices by JAX's collectives and lax.ppermute only.
A program may use at most 64 MiB of HBM per device.

v0:
```python
import functools
import math

import jax
import jax.numpy as jnp
from jax import lax
from jax.sharding import Mesh
from jax.sharding import PartitionSpec as P

HD = 128
GROUP = 2
WINDOW = 1024
SEQ = ("seq_0", "seq_1", "seq_2")


norm_eps = 1e-06
query_scale = 168.0 ** (-0.5)
rope_base = 10000.0


def passed_along(array, axis, by):
    devices = lax.axis_size(axis)
    pairs = [(i, i + by) for i in range(devices) if 0 <= i + by < devices]
    return lax.ppermute(array, axis, pairs)


def sent_together(arrays, axis, dim, along):
    widths = [math.prod(a.shape[along:]) for a in arrays]
    both = jnp.concatenate(
        [a.reshape(*a.shape[:along], w) for a, w in zip(arrays, widths)], axis=along
    )
    whole = lax.all_gather(both, axis, axis=dim, tiled=True)
    tiles = jnp.split(whole, [sum(widths[:k]) for k in range(1, len(widths))], axis=along)
    return tuple((b.reshape(*whole.shape[:along], *a.shape[along:]) for a, b in zip(arrays, tiles)))


def laid_out(tiles, dim):
    tiles = jnp.moveaxis(tiles, 0, dim)
    lengths = tiles.shape
    return tiles.reshape(*lengths[:dim], lengths[dim] * lengths[dim + 1], *lengths[dim + 2 :])


def stacked_from(array, axes, turns):
    tiles = array[None]
    for k in turns:
        tiles = lax.all_gather(tiles, axes[k], axis=0, tiled=True)
    held = [lax.axis_size(axes[k]) for k in reversed(turns)]
    tiles = tiles.reshape(*held, *array.shape)
    turned = sorted(range(len(turns)), key=lambda place: turns[len(turns) - 1 - place])
    return tiles.transpose(*turned, *range(len(turns), tiles.ndim)).reshape(-1, *array.shape)


def whole_of(array, axes, turns, dim):
    return laid_out(stacked_from(array, axes, turns), dim)


def in_blocks(array, dim, devices):
    before, after = (array.shape[:dim], array.shape[dim + 1 :])
    return jnp.moveaxis(array.reshape(*before, devices, -1, *after), dim, 0)


def sent_and_summed(array, axis, dim):
    tiles = in_blocks(array, dim, lax.axis_size(axis))
    arrived = lax.all_to_all(tiles, axis, split_axis=0, concat_axis=0, tiled=True)
    return arrived.sum(axis=0)


def sent_to_all(array, axis):
    devices = lax.axis_size(axis)
    return lax.all_to_all(
        jnp.broadcast_to(array[None], (devices, *array.shape)), axis, 0, 0, tiled=True
    )


def taken_together(array, axis):
    everything = sent_to_all(array, axis)
    return jnp.sum(everything, axis=0)


def by_axis(array, axes):
    return functools.reduce(lax.psum, axes, array)


def rms_scale(values, gain_vec):
    return (
        values * lax.rsqrt(jnp.mean(values * values, axis=-1, keepdims=True) + norm_eps) * gain_vec
    )


def rotate_pairs(head_rows, positions):
    half_width = head_rows.shape[-1] // 2
    frequency = rope_base ** (
        -jnp.arange(half_width, dtype=jnp.float32) * 2.0 / head_rows.shape[-1]
    )
    angles = positions.astype(jnp.float32)[:, None] * frequency[None, :]
    target = (angles.shape[0],) + (1,) * (head_rows.ndim - 2) + (half_width,)
    cosine = jnp.cos(angles).reshape(target)
    sine_part = jnp.sin(angles).reshape(target)
    front_half = head_rows[..., :half_width]
    back_half = head_rows[..., half_width:]
    return jnp.concatenate(
        [front_half * cosine - back_half * sine_part, back_half * cosine + front_half * sine_part],
        axis=-1,
    )


def window_blocks(packed, tok_dev):
    block_count = WINDOW // tok_dev + 1
    blocks_held = [packed]
    while len(blocks_held) < block_count:
        take_count = min(len(blocks_held), block_count - len(blocks_held))
        arrived = passed_along(jnp.stack(blocks_held[:take_count]), SEQ, len(blocks_held))
        blocks_held = blocks_held + [arrived[offset] for offset in range(take_count)]
    return jnp.concatenate(blocks_held[::-1], axis=1)


def window_attention(queries, keys_all, values_all, query_pos, key_pos):
    scores = jnp.einsum("qhgd,khd->hgqk", queries, keys_all, preferred_element_type=jnp.float32)
    allowed = (
        (key_pos[None, :] <= query_pos[:, None])
        & (key_pos[None, :] > query_pos[:, None] - WINDOW)
        & (key_pos[None, :] >= 0)
    )
    scores = jnp.where(allowed[None, None], scores, -1e30)
    row_top = jnp.max(scores, axis=-1, keepdims=True)
    exponent = jnp.exp(scores - row_top)
    attn_weights = (exponent / jnp.sum(exponent, axis=-1, keepdims=True)).astype(jnp.bfloat16)
    mixed_heads = jnp.einsum(
        "hgqk,khd->qhgd", attn_weights, values_all, preferred_element_type=jnp.float32
    )
    return mixed_heads.astype(jnp.bfloat16)


def local(
    hidden,
    lengths,
    reward_pos,
    in_gain,
    w_query,
    w_key,
    w_value,
    query_gain,
    key_gain,
    w_out,
    post_gain,
    final_gain,
    value_head,
):
    micro_count, tok_dev, width = hidden.shape
    row_count = micro_count * tok_dev
    qwidth = w_query.shape[1]
    kwidth = w_key.shape[1]
    heads_here = kwidth // HD
    widened = hidden.reshape(row_count, width).astype(jnp.float32)
    inverse = lax.rsqrt(jnp.mean(widened * widened, axis=-1, keepdims=True) + norm_eps)
    seq_pos = lax.axis_index(SEQ) * tok_dev + jnp.arange(tok_dev, dtype=jnp.int32)
    positions = jnp.tile(seq_pos, micro_count)
    gain_piece, query_piece, key_piece, value_piece, post_piece, final_piece, head_piece = (
        sent_together(
            (in_gain, w_query, w_key, w_value, post_gain, final_gain, value_head), SEQ, 0, 1
        )
    )
    normed = (widened * inverse * gain_piece.astype(jnp.float32)).astype(jnp.bfloat16)
    query_acc = jnp.dot(normed, query_piece, preferred_element_type=jnp.float32)
    key_acc = jnp.dot(normed, key_piece, preferred_element_type=jnp.float32)
    value_acc = jnp.dot(normed, value_piece, preferred_element_type=jnp.float32)
    post_full = post_piece.astype(jnp.float32)
    final_full = final_piece.astype(jnp.float32)
    head_full = head_piece.astype(jnp.float32)
    folded = (query_acc, key_acc, value_acc, post_full, final_full, head_full)
    queries = folded[0].reshape(row_count, heads_here, GROUP, HD)
    queries = (rotate_pairs(rms_scale(queries, query_gain), positions) * query_scale).astype(
        jnp.bfloat16
    )
    keys_new = folded[1].reshape(row_count, heads_here, HD)
    keys_new = (
        rotate_pairs(rms_scale(keys_new, key_gain), positions)
        .astype(jnp.bfloat16)
        .reshape(row_count, kwidth)
    )
    vals_new = folded[2].astype(jnp.bfloat16)
    packed = jnp.concatenate([keys_new, vals_new], axis=1).reshape(micro_count, tok_dev, 2 * kwidth)
    window_rows = window_blocks(packed, tok_dev)
    key_pos = seq_pos[0] - WINDOW + jnp.arange(WINDOW + tok_dev, dtype=jnp.int32)
    mixed_list = []
    for micro_id in range(micro_count):
        block_queries = queries[micro_id * tok_dev : (micro_id + 1) * tok_dev]
        keys_all = window_rows[micro_id, :, :kwidth].reshape(-1, heads_here, HD)
        values_all = window_rows[micro_id, :, kwidth:].reshape(-1, heads_here, HD)
        mixed_list.append(
            window_attention(block_queries, keys_all, values_all, seq_pos, key_pos).reshape(
                tok_dev, qwidth
            )
        )
    mixed_all = jnp.concatenate(mixed_list, axis=0)
    branch = jnp.dot(
        mixed_all, whole_of(w_out, SEQ, (2, 0, 1), 1), preferred_element_type=jnp.float32
    )
    post_full, final_full, head_full = (folded[3], folded[4], folded[5])
    share_width = width // lax.axis_size("section")
    offset = lax.axis_index("section") * share_width
    share = sent_and_summed(branch, "section", 1)
    branch_sq = taken_together(jnp.sum(share * share, axis=1), "section")
    share_scale = lax.rsqrt(branch_sq / width + norm_eps)[:, None]
    post_share = lax.dynamic_slice_in_dim(post_full, offset, share_width, 0)
    updated = (
        lax.dynamic_slice_in_dim(widened, offset, share_width, 1) + share * share_scale * post_share
    ).astype(jnp.bfloat16)
    updated_wide = updated.astype(jnp.float32)
    residual_sq = taken_together(jnp.sum(updated_wide * updated_wide, axis=1), "section")
    final_share = lax.dynamic_slice_in_dim(final_full, offset, share_width, 0)
    last_rows = (
        updated_wide * lax.rsqrt(residual_sq / width + norm_eps)[:, None] * final_share
    ).astype(jnp.bfloat16)
    head_share = lax.dynamic_slice_in_dim(head_full, offset, share_width, 0).astype(jnp.bfloat16)
    raw_values = taken_together(
        jnp.dot(last_rows, head_share, preferred_element_type=jnp.float32), "section"
    )
    raw_values = raw_values.reshape(micro_count, tok_dev)
    token_values = jnp.where(seq_pos[None, :] < lengths[:, None], raw_values, 0.0)
    partial_value = jnp.sum(
        jnp.where(seq_pos[None, :] == reward_pos[:, None], token_values, 0.0), axis=1
    )
    reward = by_axis(partial_value, SEQ)
    return (token_values, reward)


def solution(mesh):
    torus = Mesh(
        mesh.devices.reshape(mesh.shape["section"], 8, 8, 2), ("section", "seq_0", "seq_1", "seq_2")
    )
    in_specs = (
        P(None, SEQ, None),
        P(),
        P(),
        P(SEQ),
        P(SEQ, "section"),
        P(SEQ, "section"),
        P(SEQ, "section"),
        P(),
        P(),
        P("section", SEQ),
        P(SEQ),
        P(SEQ),
        P(SEQ),
    )
    out_specs = (P(None, SEQ), P())
    return jax.shard_map(local, mesh=torus, in_specs=in_specs, out_specs=out_specs, check_vma=False)
```

profile of v0, /device:TPU:2, one launch (start us, length us, event | category | flops | bytes accessed | tf_op | source)
XLA Modules:
  0.0 885.2 jit_solution(14072104166463112967)
XLA Ops:
  11.8 8.6 all-gather
  20.5 28.0 %all_gather.14 = bf16[16,512,21]{1,2,0:T(8,128)(2,1)S(1)} all-gather(bf16[2,512,21]{1,2,0:T(8,128)(2,1)S(1)} %copy.153), channel_id=1, replica_groups=mesh['section'=4,'seq_0'=8,'seq_1'=8,'seq_2'=2] {'seq_0'}, dimensions={0}, use_global_device_ids=true | all-gather | bytes 387072 | tf_op jit(solution)/shard_map/all_gather | solution.py:46
  53.6 558.3 %all-gather.7.cloned.1.call-done = bf16[128,21,1028]{2,1,0:T(8,128)(2,1)} async-done(((bf16[1,21,1028]{2,1,0:T(8,128)(2,1)}), bf16[128,21,1028]{2,1,0:T(8,128)(2,1)}) %all-gather.7.cloned.1.call-update) | async-done | bytes 5526544 | tf_op jit(solution)/shard_map/all_gather | solution.py:32
  611.9 9.2 %reshape.390 = bf16[2688,1028]{1,0:T(8,128)(2,1)} reshape(bf16[128,21,1028]{2,1,0:T(8,128)(2,1)} %all-gather.7.cloned.1.call-done) | data formatting | bytes 11053056
  621.1 3.3 slice_bitcast_fusion.1
  641.2 17.0 %all-gather.5.cloned.1.call-done = bf16[128,512,21]{1,0,2:T(8,128)(2,1)} async-done(((bf16[16,512,21]{1,0,2:T(8,128)(2,1)}), bf16[128,512,21]{1,0,2:T(8,128)(2,1)}) %all-gather.5.cloned.1.call-update) | async-done | bytes 2752528 | tf_op jit(solution)/shard_map/all_gather | solution.py:46
  658.2 6.5 reshape.382
  664.8 6.4 copy.155
  671.1 5.4 reshape.384
  680.2 5.0 slice_bitcast_fusion
  686.8 4.5 collective-permute-start
  692.9 4.5 copy.144
  702.5 5.0 collective-permute-start.3
  709.5 37.9 %collective-permute-done.3 = bf16[4,2,128,512]{2,3,1,0:T(8,128)(2,1)S(1)} collective-permute-done((bf16[4,2,128,512]{2,3,1,0:T(8,128)(2,1)S(1)}, bf16[4,2,128,512]{2,3,1,0:T(8,128)(2,1)S(1)}, u32[]{:S(2)}, u32[]{:S(2)}) %collective-permute-start.3) | collective-permute-done | bytes 1048608 | tf_op jit(solution)/shard_map/ppermute | solution.py:24
  761.5 4.2 convolution_bitcast_fusion.2
  765.7 4.6 all-to-all-start
  770.3 3.5 fusion.68
  774.0 30.6 %all-to-all-done = f32[4,256,672]{1,2,0:T(8,128)} async-done(((f32[4,256,672]{1,2,0:T(8,128)}), f32[4,256,672]{1,2,0:T(8,128)}, u32[]{:S(2)}, u32[]{:S(2)}) %all-to-all-start) | async-done | bytes 2752544 | tf_op jit(solution)/shard_map/all_to_all | solution.py:64
  811.7 4.2 all-to-all-done.1
  821.7 4.2 all-to-all-done.2
  827.2 7.6 all_to_all.23
  835.6 21.5 %psum.21 = f32[2]{0:T(128)S(1)} all-reduce(f32[2]{0:T(128)S(1)} %get-tuple-element.2), channel_id=1, replica_groups=mesh['section'=4,'seq_0'=8,'seq_1'=8,'seq_2'=2] {'seq_0'}, use_global_device_ids=true, to_apply=%region_14.15 | all-reduce | flops 2 | bytes 16 | tf_op jit(solution)/shard_map/psum | solution.py:81
  857.2 15.8 %psum.22 = f32[2]{0:T(128)S(1)} all-reduce(f32[2]{0:T(128)S(1)} %psum.21), channel_id=1, replica_groups=mesh['section'=4,'seq_0'=8,'seq_1'=8,'seq_2'=2] {'seq_1'}, use_global_device_ids=true, to_apply=%region_15.16 | all-reduce | flops 2 | bytes 16 | tf_op jit(solution)/shard_map/psum | solution.py:81
  872.9 5.4 psum.23
  (126 shorter events, 69.1 us)
Async XLA Ops:
  7.2 604.7 %all-gather.7.cloned.1.call-start = ((), (), s32[]{:S(2)}) async-start(), calls=%async_computation.5 | async-start | bytes 7133184 | tf_op jit(solution)/shard_map/all_gather | solution.py:32
  11.8 646.4 %all-gather.5.cloned.1.call-start = ((), (), s32[]{:S(2)}) async-start(), calls=%async_computation.4 | async-start | bytes 3096576 | tf_op jit(solution)/shard_map/all_gather | solution.py:46
  53.6 578.4 %copy-start.8 = (f32[256,64]{0,1:T(8,128)}, f32[256,64]{0,1:T(8,128)S(1)}, u32[]{:S(2)}) copy-start(f32[256,64]{0,1:T(8,128)S(1)} %get-tuple-element.17) | copy-start | bytes 196612
  53.6 578.4 %copy-start.10 = (f32[256,64]{0,1:T(8,128)}, f32[256,64]{0,1:T(8,128)S(1)}, u32[]{:S(2)}) copy-start(f32[256,64]{0,1:T(8,128)S(1)} %get-tuple-element.18) | copy-start | bytes 196612
  627.0 4.3 copy-start.5
  628.5 3.4 copy-start.16
  632.2 44.4 %copy-start = (bf16[1,2,128,256]{2,3,1,0:T(8,128)(2,1)}, bf16[1,2,128,256]{2,3,1,0:T(8,128)(2,1)S(1)}, u32[]{:S(2)}) copy-start(bf16[1,2,128,256]{2,3,1,0:T(8,128)(2,1)S(1)} %copy.140) | copy-start | bytes 393220
  635.9 40.6 %copy-start.2 = (bf16[1,2,128,256]{2,3,1,0:T(8,128)(2,1)}, bf16[1,2,128,256]{2,3,1,0:T(8,128)(2,1)S(1)}, u32[]{:S(2)}) copy-start(bf16[1,2,128,256]{2,3,1,0:T(8,128)(2,1)S(1)} %copy.141) | copy-start | bytes 393220
  635.9 28.8 %copy-start.14 = (bf16[1,2,128,512]{2,3,1,0:T(8,128)(2,1)}, bf16[1,2,128,512]{2,3,1,0:T(8,128)(2,1)S(1)}, u32[]{:S(2)}) copy-start(bf16[1,2,128,512]{2,3,1,0:T(8,128)(2,1)S(1)} %pad_maximum_fusion.2) | copy-start | bytes 786436
  636.0 40.6 %collective-permute-start.1 = (bf16[1,2,128,512]{2,3,1,0:T(8,128)(2,1)S(1)}, bf16[1,2,128,512]{2,3,1,0:T(8,128)(2,1)S(1)}, u32[]{:S(2)}, u32[]{:S(2)}) collective-permute-start(bf16[1,2,128,512]{2,3,1,0:T(8,128)(2,1)S(1)} %pad_maximum_fusion.2), channel_id=1, source_target_pairs={{0,1},{1,2},{2,3},{3,4},{4,5},{5,6},{6,7},{7,8},{8,9},{9,10},{10,1... | collective-permute-start | bytes 786440 | tf_op jit(solution)/shard_map/ppermute | solution.py:24
  677.4 25.0 %collective-permute-start.2 = (bf16[2,2,128,512]{2,3,1,0:T(8,128)(2,1)}, bf16[2,2,128,512]{2,3,1,0:T(8,128)(2,1)S(1)}, u32[]{:S(2)}, u32[]{:S(2)}) collective-permute-start(bf16[2,2,128,512]{2,3,1,0:T(8,128)(2,1)} %pad_maximum_fusion.1), channel_id=1, source_target_pairs={{0,2},{1,3},{2,4},{3,5},{4,6},{5,7},{6,8},{7,9},{8,10},{9,11},{10,... | collective-permute-start | bytes 1572872 | tf_op jit(solution)/shard_map/ppermute | solution.py:24
  686.8 21.7 %collective-permute-start = (bf16[1,2,128,512]{2,3,1,0:T(8,128)(2,1)}, bf16[1,2,128,512]{2,3,1,0:T(8,128)(2,1)}, u32[]{:S(2)}, u32[]{:S(2)}) collective-permute-start(bf16[1,2,128,512]{2,3,1,0:T(8,128)(2,1)} %copy-done.14), channel_id=1, source_target_pairs={{0,8},{1,9},{2,10},{3,11},{4,12},{5,13},{6,14},{7,15},{8,16},{9,17... | collective-permute-start | bytes 786440 | tf_op jit(solution)/shard_map/ppermute | solution.py:24
  699.1 3.2 copy-start.3
  699.1 8.4 copy-start.17
  702.3 5.3 copy-start.9
  702.3 5.3 copy-start.11
  702.5 44.9 %collective-permute-start.3 = (bf16[4,2,128,512]{2,3,1,0:T(8,128)(2,1)S(1)}, bf16[4,2,128,512]{2,3,1,0:T(8,128)(2,1)S(1)}, u32[]{:S(2)}, u32[]{:S(2)}) collective-permute-start(bf16[4,2,128,512]{2,3,1,0:T(8,128)(2,1)S(1)} %pad_maximum_fusion), channel_id=1, source_target_pairs={{0,4},{1,5},{2,6},{3,7},{4,8},{5,9},{6,10},{7,11},{8,12},{9,13},{1... | collective-permute-start | bytes 3145736 | tf_op jit(solution)/shard_map/ppermute | solution.py:24
  707.8 40.1 %copy-start.12 = (bf16[2,128,256]{1,2,0:T(8,128)(2,1)S(1)}, bf16[2,128,256]{1,2,0:T(8,128)(2,1)}, u32[]{:S(2)}) copy-start(bf16[2,128,256]{1,2,0:T(8,128)(2,1)} %copy.142) | copy-start | bytes 393220
  707.8 40.1 %copy-start.13 = (bf16[2,128,256]{1,2,0:T(8,128)(2,1)S(1)}, bf16[2,128,256]{1,2,0:T(8,128)(2,1)}, u32[]{:S(2)}) copy-start(bf16[2,128,256]{1,2,0:T(8,128)(2,1)} %copy.143) | copy-start | bytes 393220
  765.7 38.8 %all-to-all-start = ((f32[4,256,672]{1,2,0:T(8,128)}), f32[4,256,672]{1,2,0:T(8,128)}, u32[]{:S(2)}, u32[]{:S(2)}) async-start(f32[4,256,672]{1,2,0:T(8,128)} %convolution_bitcast_fusion.2), calls=%async_computation | async-start | bytes 5505024 | tf_op jit(solution)/shard_map/all_to_all | solution.py:64
  806.6 28.2 %copy-start.18 = (s32[2]{0:T(128)S(1)}, s32[2]{0:T(128)}, u32[]{:S(2)}) copy-start(s32[2]{0:T(128)} %param.15) | copy-start | bytes 28
  806.6 28.2 %copy-start.19 = (s32[2]{0:T(128)S(1)}, s32[2]{0:T(128)}, u32[]{:S(2)}) copy-start(s32[2]{0:T(128)} %param.14) | copy-start | bytes 28
  807.3 8.5 all-to-all-start.1
  817.4 8.5 all-to-all-start.2
  (5 other events, 9.4 us)
Sparse Core Ops, SparseCore 0:
  11.9 599.9 all-gather.6
  614.0 44.1 all-gather.4
where the time goes:
time: 887 us; the launch traced here: 885 us
  waiting for transfers between devices  652 us (74%)
  blocking collectives  87 us (10%)
  local copies, waits for them, and re-layouts  66.1 us (7%)
  starting transfers between devices  26.7 us (3%)
  matrix products  22.5 us (3%)
  other arithmetic  16.2 us (2%)
  between operations  14.6 us (2%)
    all_gather x1, waiting for transfers between devices, sent_together(): whole = lax.all_gather(both, axis, axis=dim, tiled=True)  558 us
    psum x3, blocking collectives, by_axis(): return functools.reduce(lax.psum, axes, array)  42.8 us
    ppermute x4, waiting for transfers between devices, passed_along(): return lax.ppermute(array, axis, pairs)  37.9 us
    all_gather x2, blocking collectives, stacked_from(): tiles = lax.all_gather(tiles, axes[k], axis=0, tiled=True)  36.6 us
    all_to_all x1, waiting for transfers between devices, sent_and_summed(): lax.all_to_all(tiles, axis, split_axis=0, concat_axis=0, tiled=True)  30.6 us
  transfers between devices with their start and end apart: 9, of which 6 were waited for; matrix products, arithmetic and copies ran while one was open for 8% of the time, Pallas kernels for 0%

commit v1 on v0

v1 whole, which is shorter than its diff:
```python
import jax
import jax.numpy as jnp
import numpy as np
from jax import lax
from jax.experimental import pallas as pl
from jax.experimental.pallas import tpu as pltpu
from jax.sharding import Mesh
from jax.sharding import PartitionSpec as P

HD = 128
GROUP = 2
WINDOW = 1024
NORM_EPS = 1e-06
QUERY_SCALE = 168.0 ** (-0.5)
ROPE_BASE = 10000.0
SIZES = (2, 2, 8, 8, 2)
AXES = ("xh", "core", "z", "y", "xl")
SECTION = ("xh", "core")
SEQ = ("z", "y", "xl")
RING_X = ("xh", "xl")
NT = (((1,), (1,)), ((), ()))


def pairs_of(source_of):
    out = []
    for there in np.ndindex(*SIZES):
        here = source_of(*there)
        if here is not None:
            out.append(
                (int(np.ravel_multi_index(here, SIZES)), int(np.ravel_multi_index(there, SIZES)))
            )
    return out


def row_source(xh, c, z, y, l):
    return (xh, l, z, (8 * c + y) // 2, y % 2)


def out_source(xh, c, z, y, l):
    s, o = divmod(2 * z + c, 4)
    q = 32 * (2 * xh + l) + 8 * o + y
    return (s // 2, s % 2, q // 16, (q % 16) // 2, q % 2)


def other_half(xh, c, z, y, l):
    return (xh, c, z, y, 1 - l)


def block_before(xh, c, z, y, l):
    block = 8 * z + y - 1
    return None if block < 0 else (xh, c, block // 8, block % 8, l)


def moved(array, source_of):
    return lax.ppermute(array, AXES, pairs_of(source_of))


def told_to_all(array, axes):
    n = lax.axis_size(axes)
    return lax.all_to_all(jnp.broadcast_to(array[None], (n, *array.shape)), axes, 0, 0, tiled=True)


def project_kernel(first, h_ref, w_ref, gain_ref, cos_ref, sin_ref, out_ref, inv_ref):
    j = pl.program_id(0)

    @pl.when(j == 0)
    def _():
        wide = h_ref[...].astype(jnp.float32)
        inv_ref[...] = lax.rsqrt(jnp.mean(wide * wide, axis=1, keepdims=True) + NORM_EPS)

    acc = jnp.dot(h_ref[...], w_ref[...], preferred_element_type=jnp.float32) * inv_ref[...]

    @pl.when(j + first < 6)
    def _():
        unit = acc * lax.rsqrt(jnp.mean(acc * acc, axis=1, keepdims=True) + NORM_EPS)
        unit = unit * gain_ref[0]
        turned = pltpu.roll(unit, HD // 2, 1)
        out_ref[...] = (unit * cos_ref[...] + turned * sin_ref[...]).astype(jnp.bfloat16)

    @pl.when(j + first >= 6)
    def _():
        out_ref[...] = acc.astype(jnp.bfloat16)


def project(h, weights, gains, cos, sin, first):
    rows, width = h.shape
    whole = lambda *shape: pl.BlockSpec(shape, lambda j: (0,) * len(shape))
    return pl.pallas_call(
        lambda *refs: project_kernel(first, *refs),
        grid=(4,),
        in_specs=[
            whole(rows, width),
            pl.BlockSpec((width, HD), lambda j: (0, j + first)),
            pl.BlockSpec((1, 1, HD), lambda j: (j + first, 0, 0)),
            whole(rows, HD),
            whole(rows, HD),
        ],
        out_specs=pl.BlockSpec((rows, HD), lambda j: (0, j)),
        out_shape=jax.ShapeDtypeStruct((rows, 4 * HD), jnp.bfloat16),
        scratch_shapes=[pltpu.VMEM((rows, 1), jnp.float32)],
        name="project",
    )(h, weights, gains, cos, sin)


def attend_kernel(block_ref, q_ref, *refs):
    keys, vals, out_ref = refs[:5], refs[5:10], refs[10]
    rows = q_ref.shape[0]
    block = block_ref[0]
    query = lax.broadcasted_iota(jnp.int32, (rows, rows), 0)
    key = lax.broadcasted_iota(jnp.int32, (rows, rows), 1)
    for g in range(GROUP):
        q = q_ref[:, g * HD : (g + 1) * HD]
        scores = []
        for back in range(5):
            s = lax.dot_general(q, keys[back][...], NT, preferred_element_type=jnp.float32)
            if back == 0:
                s = jnp.where(key <= query, s, -1e30)
            elif back == 4:
                s = jnp.where((key > query) & (block >= 4), s, -1e30)
            else:
                s = jnp.where(block >= back, s, -1e30)
            scores.append(s)
        top = jnp.max(scores[0], axis=1, keepdims=True)
        for s in scores[1:]:
            top = jnp.maximum(top, jnp.max(s, axis=1, keepdims=True))
        total, mixed = 0.0, 0.0
        for s, v in zip(scores, vals):
            e = jnp.exp(s - top)
            total = total + jnp.sum(e, axis=1, keepdims=True)
            mixed = mixed + jnp.dot(
                e.astype(jnp.bfloat16), v[...], preferred_element_type=jnp.float32
            )
        out_ref[:, g * HD : (g + 1) * HD] = (mixed / total).astype(jnp.bfloat16)


def attend(block, q, held):
    rows = q.shape[0]
    part = lambda at: pl.BlockSpec((rows, HD), lambda h, b: (0, h + at))
    wide = pl.BlockSpec((rows, GROUP * HD), lambda h, b: (0, h))
    return pl.pallas_call(
        attend_kernel,
        grid_spec=pltpu.PrefetchScalarGridSpec(
            num_scalar_prefetch=1,
            grid=(2,),
            in_specs=[wide] + [part(0)] * 5 + [part(2)] * 5,
            out_specs=wide,
        ),
        out_shape=jax.ShapeDtypeStruct(q.shape, jnp.bfloat16),
        name="attend",
    )(block, q, *held, *held)


def sums_kernel(mixed_ref, w_ref, h_ref, out_ref):
    @pl.when(pl.program_id(0) == 0)
    def _():
        out_ref[...] = jnp.zeros_like(out_ref)

    width = mixed_ref.shape[2]
    branch = 0.0
    for s in range(4):
        branch = branch + lax.dot_general(
            w_ref[s, 0, :, :width], mixed_ref[s], NT, preferred_element_type=jnp.float32
        )
    gains = w_ref[0, 0, :, width:].astype(jnp.float32)
    post, final, head = gains[:, 0:1], gains[:, 1:2], gains[:, 2:3]
    read = final * head
    hidden = h_ref[0].astype(jnp.float32)
    scaled = branch * post
    for k, term in enumerate(
        (
            branch * branch,
            scaled * scaled,
            hidden * scaled,
            scaled * read,
            hidden * read,
            hidden * hidden,
        )
    ):
        out_ref[k : k + 1, :] += jnp.sum(term, axis=0, keepdims=True)


def token_sums(mixed, weights, h_share):
    rows = mixed.shape[1]
    _, parts, depth, wide = weights.shape
    return pl.pallas_call(
        sums_kernel,
        grid=(parts,),
        in_specs=[
            pl.BlockSpec(mixed.shape, lambda o: (0, 0, 0)),
            pl.BlockSpec((4, 1, depth, wide), lambda o: (0, o, 0, 0)),
            pl.BlockSpec((1, depth, rows), lambda o: (o, 0, 0)),
        ],
        out_specs=pl.BlockSpec((8, rows), lambda o: (0, 0)),
        out_shape=jax.ShapeDtypeStruct((8, rows), jnp.float32),
        name="token_sums",
    )(mixed, weights, h_share)


def local(
    hidden,
    lengths,
    reward_pos,
    in_gain,
    w_query,
    w_key,
    w_value,
    query_gain,
    key_gain,
    w_out,
    post_gain,
    final_gain,
    value_head,
):
    _, tok_dev, width = hidden.shape
    shard = in_gain.shape[0]
    rows = 2 * tok_dev
    block = 8 * lax.axis_index("z") + lax.axis_index("y")
    core, half = lax.axis_index("core"), lax.axis_index("xl")
    place = 2 * lax.axis_index("xh") + half

    projections = jnp.concatenate([w_query, w_key, w_value], axis=1).astype(jnp.float32)
    projections = (projections * in_gain.astype(jnp.float32)[:, None]).astype(jnp.bfloat16)
    octet = told_to_all(moved(projections, row_source), "y").reshape(8 * shard, -1)
    weights = lax.all_gather(octet, ("z", "core"), axis=0, tiled=True)

    extra = jnp.stack([post_gain, final_gain, value_head], axis=1)
    out_shard = jnp.concatenate(
        [w_out.T, extra, jnp.zeros((shard, HD - 3), jnp.bfloat16)], axis=1
    )
    out_octet = told_to_all(moved(out_shard, out_source), "y").reshape(8 * shard, -1)
    out_weights = lax.all_gather(out_octet, ("z", "core"), axis=0, tiled=True)
    out_weights = out_weights.reshape(4, 4, 8 * shard, -1)

    mine = lax.dynamic_index_in_dim(hidden, core, 0, keepdims=False)
    theirs = moved(mine, other_half)
    h = jnp.concatenate(
        [jnp.where(half == 0, mine, theirs), jnp.where(half == 0, theirs, mine)], axis=0
    )
    h_share = lax.dynamic_slice_in_dim(h, place * (width // 4), width // 4, 1)
    h_share = h_share.T.reshape(4, 8 * shard, rows)

    pos = block * rows + jnp.arange(rows, dtype=jnp.int32)
    frequency = ROPE_BASE ** (-jnp.arange(HD // 2, dtype=jnp.float32) * 2.0 / HD)
    angles = pos.astype(jnp.float32)[:, None] * frequency[None, :]
    cos, sin = jnp.cos(angles), jnp.sin(angles)
    cos = jnp.concatenate([cos, cos], axis=1)
    sin = jnp.concatenate([-sin, sin], axis=1)
    gains = jnp.stack([query_gain * QUERY_SCALE] * 4 + [key_gain] * 4)[:, None, :]

    kv = project(h, weights, gains, cos, sin, 4)
    held = [kv]
    for _ in range(WINDOW // rows):
        held.append(moved(held[-1], block_before))
    q = project(h, weights, gains, cos, sin, 0)
    mixed = attend(block[None], q, held)

    everyone = told_to_all(mixed, RING_X)
    sums = token_sums(everyone, out_weights, h_share)
    sums = told_to_all(sums, ("xh", "xl", "core")).reshape(4, 2, 8, rows).sum(axis=0)
    branch_sq, scaled_sq, cross, read_branch, read_hidden, hidden_sq = (
        sums[:, k] for k in range(6)
    )
    scale = lax.rsqrt(branch_sq / width + NORM_EPS)
    residual_sq = hidden_sq + scale * (2.0 * cross + scale * scaled_sq)
    residual_sq = jnp.maximum(residual_sq, 0.0)
    values = (read_hidden + scale * read_branch) * lax.rsqrt(residual_sq / width + NORM_EPS)
    values = jnp.where(pos[None, :] < lengths[:, None], values, 0.0)
    token_values = lax.dynamic_slice_in_dim(values, half * tok_dev, tok_dev, 1)
    reward = jnp.sum(jnp.where(pos[None, :] == reward_pos[:, None], values, 0.0), axis=1)
    for axis in ("y", "z"):
        reward = told_to_all(reward, axis).sum(axis=0)
    return token_values, reward


def solution(mesh):
    torus = Mesh(mesh.devices.reshape(SIZES), AXES)
    in_specs = (
        P(None, SEQ, None),
        P(),
        P(),
        P(SEQ),
        P(SEQ, SECTION),
        P(SEQ, SECTION),
        P(SEQ, SECTION),
        P(),
        P(),
        P(SECTION, SEQ),
        P(SEQ),
        P(SEQ),
        P(SEQ),
    )
    out_specs = (P(None, SEQ), P())
    return jax.shard_map(local, mesh=torus, in_specs=in_specs, out_specs=out_specs, check_vma=False)
```

time: 887 us -> 213 us (0.24)
  waiting for transfers between devices: 652 us -> 69.2 us
  local copies, waits for them, and re-layouts: 66.1 us -> 10.6 us
  blocking collectives: 87 us -> 38.7 us
  starting transfers between devices: 26.7 us -> 52.4 us
  matrix products: 22.5 us -> 0 us
  Pallas kernels: 0 us -> 21.4 us
  other arithmetic: 16.2 us -> 5.18 us
    all_gather x2, waiting for transfers between devices: 575 us -> 7.05 us  [the longest x1 4.81 us: local(): weights = lax.all_gather(octet, ('z', 'core'), axis=0, tiled=True)]
    psum x3 -> x0, blocking collectives: 42.8 us -> none  [by_axis(): return functools.reduce(lax.psum, axes, array)]
    all_gather x2 -> x0, blocking collectives: 36.6 us -> none  [stacked_from(): tiles = lax.all_gather(tiles, axes[k], axis=0, tiled=True)]
    all_to_all x1 -> x2, blocking collectives: 7.63 us -> 38.7 us  [told_to_all(): lax.all_to_all(jnp.broadcast_to(array[None], (n, *array.shape)), axes, 0,...]
    pallas_call x0 -> x4, Pallas kernels: none -> 21.4 us  [the longest x2 11.8 us: project(): pl.pallas_call(lambda *refs: project_kernel(first, *refs), grid=(4,), in_...]
    dot_general x7 -> x0, matrix products: 18.6 us -> none  [the longest x2 6.26 us: window_attention(): jnp.einsum('hgqk,khd->qhgd', attn_weights, values_all, preferred_element_...]
    all_to_all x3 -> x4, starting transfers between devices: 11.1 us -> 28.4 us  [told_to_all(): lax.all_to_all(jnp.broadcast_to(array[None], (n, *array.shape)), axes, 0,...]
    dot_general x4 -> x0, local copies, waits for them, and re-layouts: 15.4 us -> none  [the longest x2 9.58 us: local(): query_acc = jnp.dot(normed, query_piece, preferred_element_type=jnp.float32)]
  transfers between devices with their start and end apart: 9 -> 13, of which waited for: 6 -> 12; matrix products, arithmetic and copies ran while one was open for 8% -> 4% of each run, Pallas kernels for 0% -> 8%
where the time goes in v1:
time: 213 us; the launch traced here: 212 us
  waiting for transfers between devices  69.2 us (32%)
  starting transfers between devices  52.4 us (25%)
  blocking collectives  38.7 us (18%)
  Pallas kernels  21.4 us (10%)
  between operations  14.3 us (7%)
  local copies, waits for them, and re-layouts  10.6 us (5%)
  other arithmetic  5.18 us (2%)
    all_to_all x2, blocking collectives, told_to_all(): lax.all_to_all(jnp.broadcast_to(array[None], (n, *array.shape)), axes, 0,...  38.7 us
    ppermute x7, waiting for transfers between devices, moved(): return lax.ppermute(array, AXES, pairs_of(source_of))  35 us
    all_to_all x4, starting transfers between devices, told_to_all(): lax.all_to_all(jnp.broadcast_to(array[None], (n, *array.shape)), axes, 0,...  28.4 us
    all_to_all x4, waiting for transfers between devices, told_to_all(): lax.all_to_all(jnp.broadcast_to(array[None], (n, *array.shape)), axes, 0,...  27.1 us
    ppermute x7, starting transfers between devices, moved(): return lax.ppermute(array, AXES, pairs_of(source_of))  24 us
    pallas_call x2, Pallas kernels, project(): pl.pallas_call(lambda *refs: project_kernel(first, *refs), grid=(4,), in_...  11.8 us
    pallas_call x1, Pallas kernels, token_sums(): pl.pallas_call(sums_kernel, grid=(parts,), in_specs=[pl.BlockSpec(mixed.s...  5.01 us
    all_gather x1, waiting for transfers between devices, local(): weights = lax.all_gather(octet, ('z', 'core'), axis=0, tiled=True)  4.81 us
  transfers between devices with their start and end apart: 13, of which 12 were waited for; matrix products, arithmetic and copies ran while one was open for 4% of the time, Pallas kernels for 8%

profile of v1, /device:TPU:2, one launch (start us, length us, event | category | flops | bytes accessed | tf_op | source)
XLA Modules:
  0.0 211.8 jit_solution(14044625334019333259)
XLA Ops:
  8.8 3.4 %collective-permute-start.1 = (bf16[21,1024]{1,0:T(8,128)(2,1)S(1)}, bf16[21,1024]{1,0:T(8,128)(2,1)S(1)}, u32[]{:S(2)}, u32[]{:S(2)}) collective-permute-start(bf16[21,1024]{1,0:T(8,128)(2,1)S(1)} %multiply_convert_fusion), channel_id=1, source_target_pairs={{0,0},{128,1},{1,2},{129,3},{2,4},{130,5},{3,6},{131,7},{4,8},{132... | collective-permute-start | bytes 129032 | tf_op jit(solution)/shard_map/ppermute | solution.py:55
  14.2 23.0 %all_to_all.32 = bf16[8,21,1024]{2,1,0:T(8,128)(2,1)S(1)} all-to-all(bf16[8,21,1024]{2,1,0:T(8,128)(2,1)S(1)} %broadcast_in_dim.21), channel_id=1, replica_groups=mesh['xh'=2,'core'=2,'z'=8,'y'=8,'xl'=2] {'y'}, dimensions={0} | all-to-all | bytes 688128 | tf_op jit(solution)/shard_map/all_to_all | solution.py:60
  40.7 5.6 %collective-permute-done.6 = bf16[21,640]{1,0:T(8,128)(2,1)S(1)} collective-permute-done((bf16[21,640]{1,0:T(8,128)(2,1)S(1)}, bf16[21,640]{1,0:T(8,128)(2,1)S(1)}, u32[]{:S(2)}, u32[]{:S(2)}) %collective-permute-start.6) | collective-permute-done | bytes 26912 | tf_op jit(solution)/shard_map/ppermute | solution.py:55
  46.4 15.7 %all_to_all.33 = bf16[8,21,640]{2,1,0:T(8,128)(2,1)S(1)} all-to-all(bf16[8,21,640]{2,1,0:T(8,128)(2,1)S(1)} %broadcast_in_dim.26), channel_id=1, replica_groups=mesh['xh'=2,'core'=2,'z'=8,'y'=8,'xl'=2] {'y'}, dimensions={0} | all-to-all | bytes 430080 | tf_op jit(solution)/shard_map/all_to_all | solution.py:60
  67.0 11.8 %collective-permute-done = bf16[128,2688]{1,0:T(8,128)(2,1)S(1)} collective-permute-done((bf16[128,2688]{1,0:T(8,128)(2,1)S(1)}, bf16[128,2688]{1,0:T(8,128)(2,1)S(1)}, u32[]{:S(2)}, u32[]{:S(2)}) %collective-permute-start) | collective-permute-done | bytes 688160 | tf_op jit(solution)/shard_map/ppermute | solution.py:55
  80.1 4.8 %all-gather.3.cloned.1.call-done.refs_1_ = bf16[2688,1024]{1,0:T(8,128)(2,1)} async-done(((bf16[168,1024]{1,0:T(8,128)(2,1)}), bf16[2688,1024]{1,0:T(8,128)(2,1)}) %all-gather.3.cloned.1.call-update) | async-done | bytes 5505040 | tf_op jit(solution)/shard_map/all_gather | solution.py:224
  84.9 5.8 %project.3.refs_0_.refs_5_ = bf16[256,512]{1,0:T(8,128)(2,1)} custom-call(bf16[256,2688]{1,0:T(8,128)(2,1)} %pad_maximum_fusion.refs_0_, bf16[2688,1024]{1,0:T(8,128)(2,1)} %all-gather.3.cloned.1.call-done.refs_1_, f32[8,1,128]{2,1,0:T(1,128)} %bitcast.67, f32[256,128]{1,0:T(8,128)} %get-tuple-element.15.refs_3_, f32[256,128]{1,0:T(8,128)} %get-tuple-element.16.refs_4_), custom_call_target="tpu_custom_call" | custom-call | tf_op jit(solution)/shard_map/project/pallas_call | solution.py:88
  94.0 6.2 %collective-permute-done.2.refs_1_.refs_6_ = bf16[256,512]{1,0:T(8,128)(2,1)S(1)} collective-permute-done((bf16[256,512]{1,0:T(8,128)(2,1)}, bf16[256,512]{1,0:T(8,128)(2,1)S(1)}, u32[]{:S(2)}, u32[]{:S(2)}) %collective-permute-start.2) | collective-permute-done | bytes 262176 | tf_op jit(solution)/shard_map/ppermute | solution.py:55
  100.3 4.3 %collective-permute-start.3 = (bf16[256,512]{1,0:T(8,128)(2,1)S(1)}, bf16[256,512]{1,0:T(8,128)(2,1)S(1)}, u32[]{:S(2)}, u32[]{:S(2)}) collective-permute-start(bf16[256,512]{1,0:T(8,128)(2,1)S(1)} %collective-permute-done.2.refs_1_.refs_6_), channel_id=1, source_target_pairs={{0,2},{1,3},{2,4},{3,5},{4,6},{5,7},{6,8},{7,9},{8,10},{9,11},{10,... | collective-permute-start | bytes 786440 | tf_op jit(solution)/shard_map/ppermute | solution.py:55
  104.6 5.1 %collective-permute-done.3.refs_2_.refs_7_ = bf16[256,512]{1,0:T(8,128)(2,1)S(1)} collective-permute-done((bf16[256,512]{1,0:T(8,128)(2,1)S(1)}, bf16[256,512]{1,0:T(8,128)(2,1)S(1)}, u32[]{:S(2)}, u32[]{:S(2)}) %collective-permute-start.3) | collective-permute-done | bytes 262176 | tf_op jit(solution)/shard_map/ppermute | solution.py:55
  109.6 4.4 %collective-permute-start.4 = (bf16[256,512]{1,0:T(8,128)(2,1)S(1)}, bf16[256,512]{1,0:T(8,128)(2,1)S(1)}, u32[]{:S(2)}, u32[]{:S(2)}) collective-permute-start(bf16[256,512]{1,0:T(8,128)(2,1)S(1)} %collective-permute-done.3.refs_2_.refs_7_), channel_id=1, source_target_pairs={{0,2},{1,3},{2,4},{3,5},{4,6},{5,7},{6,8},{7,9},{8,10},{9,11},{10,... | collective-permute-start | bytes 786440 | tf_op jit(solution)/shard_map/ppermute | solution.py:55
  114.0 4.3 %collective-permute-done.4.refs_3_.refs_8_ = bf16[256,512]{1,0:T(8,128)(2,1)S(1)} collective-permute-done((bf16[256,512]{1,0:T(8,128)(2,1)S(1)}, bf16[256,512]{1,0:T(8,128)(2,1)S(1)}, u32[]{:S(2)}, u32[]{:S(2)}) %collective-permute-start.4) | collective-permute-done | bytes 262176 | tf_op jit(solution)/shard_map/ppermute | solution.py:55
  118.4 4.4 %collective-permute-start.5 = (bf16[256,512]{1,0:T(8,128)(2,1)S(1)}, bf16[256,512]{1,0:T(8,128)(2,1)S(1)}, u32[]{:S(2)}, u32[]{:S(2)}) collective-permute-start(bf16[256,512]{1,0:T(8,128)(2,1)S(1)} %collective-permute-done.4.refs_3_.refs_8_), channel_id=1, source_target_pairs={{0,2},{1,3},{2,4},{3,5},{4,6},{5,7},{6,8},{7,9},{8,10},{9,11},{10,... | collective-permute-start | bytes 786440 | tf_op jit(solution)/shard_map/ppermute | solution.py:55
  122.8 6.1 %project.2.q_ref = bf16[256,512]{1,0:T(8,128)(2,1)} custom-call(bf16[256,2688]{1,0:T(8,128)(2,1)} %pad_maximum_fusion.refs_0_, bf16[2688,1024]{1,0:T(8,128)(2,1)} %all-gather.3.cloned.1.call-done.refs_1_, f32[8,1,128]{2,1,0:T(1,128)} %bitcast.68, f32[256,128]{1,0:T(8,128)} %get-tuple-element.15.refs_3_, f32[256,128]{1,0:T(8,128)} %get-tuple-element.16.refs_4_), custom_call_target="tpu_custom_call" | custom-call | tf_op jit(solution)/shard_map/project/pallas_call | solution.py:88
  129.6 4.6 %attend.1 = bf16[256,512]{1,0:T(8,128)(2,1)} custom-call(s32[1]{0:T(128)} %bitcast.block_ref, bf16[256,512]{1,0:T(8,128)(2,1)} %project.2.q_ref, bf16[256,512]{1,0:T(8,128)(2,1)} %project.3.refs_0_.refs_5_, bf16[256,512]{1,0:T(8,128)(2,1)} %copy-done.2, bf16[256,512]{1,0:T(8,128)(2,1)} %copy-done.3, bf16[256,512]{1,0:T(8,128)(2,1)} %copy-done.4, ...), custom_call_target="tpu_custom_call" | custom-call | tf_op jit(solution)/shard_map/attend/pallas_call | solution.py:140
  136.2 4.7 %all-to-all-start.1 = ((bf16[4,256,512]{2,1,0:T(8,128)(2,1)}), bf16[4,256,512]{2,1,0:T(8,128)(2,1)S(1)}, u32[]{:S(2)}, u32[]{:S(2)}) async-start(bf16[4,256,512]{2,1,0:T(8,128)(2,1)} %broadcast_in_dim.23), calls=%async_computation.1 | async-start | bytes 2097152 | tf_op jit(solution)/shard_map/all_to_all | solution.py:60
  144.3 8.1 %all-to-all-done.1.mixed_ref = bf16[4,256,512]{2,1,0:T(8,128)(2,1)S(1)} async-done(((bf16[4,256,512]{2,1,0:T(8,128)(2,1)}), bf16[4,256,512]{2,1,0:T(8,128)(2,1)S(1)}, u32[]{:S(2)}, u32[]{:S(2)}) %all-to-all-start.1) | async-done | bytes 1048608 | tf_op jit(solution)/shard_map/all_to_all | solution.py:60
  153.3 5.0 %token_sums.1 = f32[8,256]{1,0:T(8,128)} custom-call(bf16[4,256,512]{2,1,0:T(8,128)(2,1)} %copy-done, bf16[4,4,168,640]{3,2,1,0:T(8,128)(2,1)} %bitcast.64, bf16[4,168,256]{2,1,0:T(8,128)(2,1)} %bitcast.65), custom_call_target="tpu_custom_call" | custom-call | tf_op jit(solution)/shard_map/token_sums/pallas_call | solution.py:185
  159.7 4.7 %all-to-all-start.3 = ((f32[8,8,256]{2,1,0:T(8,128)}), f32[8,8,256]{2,1,0:T(8,128)S(1)}, u32[]{:S(2)}, u32[]{:S(2)}) async-start(f32[8,8,256]{2,1,0:T(8,128)} %broadcast_in_dim.27), calls=%async_computation.3 | async-start | bytes 131072 | tf_op jit(solution)/shard_map/all_to_all | solution.py:60
  164.4 4.2 %all-to-all-done.3 = f32[8,8,256]{2,1,0:T(8,128)S(1)} async-done(((f32[8,8,256]{2,1,0:T(8,128)}), f32[8,8,256]{2,1,0:T(8,128)S(1)}, u32[]{:S(2)}, u32[]{:S(2)}) %all-to-all-start.3) | async-done | bytes 65568 | tf_op jit(solution)/shard_map/all_to_all | solution.py:60
  169.4 9.5 %all-to-all-start.4 = ((f32[8,1,2]{2,1,0:T(1,128)}), f32[8,1,2]{2,1,0:T(1,128)S(1)}, u32[]{:S(2)}, u32[]{:S(2)}) async-start(f32[8,1,2]{2,1,0:T(1,128)} %broadcast_in_dim.28), calls=%async_computation.4 | async-start | bytes 8192 | tf_op jit(solution)/shard_map/all_to_all | solution.py:60
  178.9 7.7 %all-to-all-done.4 = f32[8,1,2]{2,1,0:T(1,128)S(1)} async-done(((f32[8,1,2]{2,1,0:T(1,128)}), f32[8,1,2]{2,1,0:T(1,128)S(1)}, u32[]{:S(2)}, u32[]{:S(2)}) %all-to-all-start.4) | async-done | bytes 96 | tf_op jit(solution)/shard_map/all_to_all | solution.py:60
  187.2 9.5 %all-to-all-start.5 = ((f32[8,1,2]{2,1,0:T(1,128)}), f32[8,1,2]{2,1,0:T(1,128)S(1)}, u32[]{:S(2)}, u32[]{:S(2)}) async-start(f32[8,1,2]{2,1,0:T(1,128)} %broadcast_in_dim.29), calls=%async_computation.5 | async-start | bytes 8192 | tf_op jit(solution)/shard_map/all_to_all | solution.py:60
  197.3 7.1 %all-to-all-done.5 = f32[8,1,2]{2,1,0:T(1,128)S(1)} async-done(((f32[8,1,2]{2,1,0:T(1,128)}), f32[8,1,2]{2,1,0:T(1,128)S(1)}, u32[]{:S(2)}, u32[]{:S(2)}) %all-to-all-start.5) | async-done | bytes 96 | tf_op jit(solution)/shard_map/all_to_all | solution.py:60
  (71 shorter events, 27.5 us)
Async XLA Ops:
  7.2 31.0 %copy-start.10 = (bf16[21]{0:T(256)(128)(2,1)S(1)}, bf16[21]{0:T(256)(128)(2,1)}, u32[]{:S(2)}) copy-start(bf16[21]{0:T(256)(128)(2,1)} %param.23) | copy-start | bytes 130
  7.2 31.1 %copy-start.11 = (bf16[21]{0:T(256)(128)(2,1)S(1)}, bf16[21]{0:T(256)(128)(2,1)}, u32[]{:S(2)}) copy-start(bf16[21]{0:T(256)(128)(2,1)} %param.24) | copy-start | bytes 130
  7.2 31.2 %copy-start.12 = (bf16[21]{0:T(256)(128)(2,1)S(1)}, bf16[21]{0:T(256)(128)(2,1)}, u32[]{:S(2)}) copy-start(bf16[21]{0:T(256)(128)(2,1)} %param.25) | copy-start | bytes 130
  7.2 31.3 %copy-start.6 = (bf16[512,21]{0,1:T(8,128)(2,1)S(1)}, bf16[512,21]{0,1:T(8,128)(2,1)}, u32[]{:S(2)}) copy-start(bf16[512,21]{0,1:T(8,128)(2,1)} %param.22) | copy-start | bytes 64516
  7.2 77.7 %all-gather.3.cloned.1.call-start = ((), (), s32[]{:S(2)}) async-start(), calls=%async_computation.6 | async-start | bytes 5849088 | tf_op jit(solution)/shard_map/all_gather | solution.py:224
  8.8 5.4 %collective-permute-start.1 = (bf16[21,1024]{1,0:T(8,128)(2,1)S(1)}, bf16[21,1024]{1,0:T(8,128)(2,1)S(1)}, u32[]{:S(2)}, u32[]{:S(2)}) collective-permute-start(bf16[21,1024]{1,0:T(8,128)(2,1)S(1)} %multiply_convert_fusion), channel_id=1, source_target_pairs={{0,0},{128,1},{1,2},{129,3},{2,4},{130,5},{3,6},{131,7},{4,8},{132... | collective-permute-start | bytes 129032 | tf_op jit(solution)/shard_map/ppermute | solution.py:55
  37.2 25.7 %copy-start.1 = (bf16[2,128,2688]{2,1,0:T(8,128)(2,1)S(1)}, bf16[2,128,2688]{2,1,0:T(8,128)(2,1)}, u32[]{:S(2)}) copy-start(bf16[2,128,2688]{2,1,0:T(8,128)(2,1)} %param.13) | copy-start | bytes 4128772
  38.1 106.2 %all-gather.5.cloned.1.call-start = ((), (), s32[]{:S(2)}) async-start(), calls=%async_computation.7 | async-start | bytes 3655680 | tf_op jit(solution)/shard_map/all_gather | solution.py:231
  38.6 26.3 %copy-start.13 = (f32[128]{0:T(128)S(1)}, f32[128]{0:T(128)}, u32[]{:S(2)}) copy-start(f32[128]{0:T(128)} %param.20) | copy-start | bytes 1540
  38.6 26.3 %copy-start.7 = (f32[128]{0:T(128)S(1)}, f32[128]{0:T(128)}, u32[]{:S(2)}) copy-start(f32[128]{0:T(128)} %param.21) | copy-start | bytes 1540
  38.6 7.8 %collective-permute-start.6 = (bf16[21,640]{1,0:T(8,128)(2,1)S(1)}, bf16[21,640]{1,0:T(8,128)(2,1)S(1)}, u32[]{:S(2)}, u32[]{:S(2)}) collective-permute-start(bf16[21,640]{1,0:T(8,128)(2,1)S(1)} %concatenate.19), channel_id=1, source_target_pairs={{0,0},{32,1},{1,2},{33,3},{2,4},{34,5},{3,6},{35,7},{4,8},{36,9},{... | collective-permute-start | bytes 80648 | tf_op jit(solution)/shard_map/ppermute | solution.py:55
  63.0 15.8 %collective-permute-start = (bf16[128,2688]{1,0:T(8,128)(2,1)S(1)}, bf16[128,2688]{1,0:T(8,128)(2,1)S(1)}, u32[]{:S(2)}, u32[]{:S(2)}) collective-permute-start(bf16[128,2688]{1,0:T(8,128)(2,1)S(1)} %dynamic-slice_bitcast_fusion), channel_id=1, source_target_pairs={{1,0},{0,1},{3,2},{2,3},{5,4},{4,5},{7,6},{6,7},{9,8},{8,9},{11,10... | collective-permute-start | bytes 2064392 | tf_op jit(solution)/shard_map/ppermute | solution.py:55
  90.6 9.6 %collective-permute-start.2 = (bf16[256,512]{1,0:T(8,128)(2,1)}, bf16[256,512]{1,0:T(8,128)(2,1)S(1)}, u32[]{:S(2)}, u32[]{:S(2)}) collective-permute-start(bf16[256,512]{1,0:T(8,128)(2,1)} %project.3.refs_0_.refs_5_), channel_id=1, source_target_pairs={{0,2},{1,3},{2,4},{3,5},{4,6},{5,7},{6,8},{7,9},{8,10},{9,11},{10,... | collective-permute-start | bytes 786440 | tf_op jit(solution)/shard_map/ppermute | solution.py:55
  100.3 28.6 %copy-start.2 = (bf16[256,512]{1,0:T(8,128)(2,1)}, bf16[256,512]{1,0:T(8,128)(2,1)S(1)}, u32[]{:S(2)}) copy-start(bf16[256,512]{1,0:T(8,128)(2,1)S(1)} %collective-permute-done.2.refs_1_.refs_6_) | copy-start | bytes 786436
  100.3 9.4 %collective-permute-start.3 = (bf16[256,512]{1,0:T(8,128)(2,1)S(1)}, bf16[256,512]{1,0:T(8,128)(2,1)S(1)}, u32[]{:S(2)}, u32[]{:S(2)}) collective-permute-start(bf16[256,512]{1,0:T(8,128)(2,1)S(1)} %collective-permute-done.2.refs_1_.refs_6_), channel_id=1, source_target_pairs={{0,2},{1,3},{2,4},{3,5},{4,6},{5,7},{6,8},{7,9},{8,10},{9,11},{10,... | collective-permute-start | bytes 786440 | tf_op jit(solution)/shard_map/ppermute | solution.py:55
  109.6 19.2 %copy-start.3 = (bf16[256,512]{1,0:T(8,128)(2,1)}, bf16[256,512]{1,0:T(8,128)(2,1)S(1)}, u32[]{:S(2)}) copy-start(bf16[256,512]{1,0:T(8,128)(2,1)S(1)} %collective-permute-done.3.refs_2_.refs_7_) | copy-start | bytes 786436
  109.6 8.7 %collective-permute-start.4 = (bf16[256,512]{1,0:T(8,128)(2,1)S(1)}, bf16[256,512]{1,0:T(8,128)(2,1)S(1)}, u32[]{:S(2)}, u32[]{:S(2)}) collective-permute-start(bf16[256,512]{1,0:T(8,128)(2,1)S(1)} %collective-permute-done.3.refs_2_.refs_7_), channel_id=1, source_target_pairs={{0,2},{1,3},{2,4},{3,5},{4,6},{5,7},{6,8},{7,9},{8,10},{9,11},{10,... | collective-permute-start | bytes 786440 | tf_op jit(solution)/shard_map/ppermute | solution.py:55
  118.4 10.5 %collective-permute-start.5 = (bf16[256,512]{1,0:T(8,128)(2,1)S(1)}, bf16[256,512]{1,0:T(8,128)(2,1)S(1)}, u32[]{:S(2)}, u32[]{:S(2)}) collective-permute-start(bf16[256,512]{1,0:T(8,128)(2,1)S(1)} %collective-permute-done.4.refs_3_.refs_8_), channel_id=1, source_target_pairs={{0,2},{1,3},{2,4},{3,5},{4,6},{5,7},{6,8},{7,9},{8,10},{9,11},{10,... | collective-permute-start | bytes 786440 | tf_op jit(solution)/shard_map/ppermute | solution.py:55
  136.2 16.1 %all-to-all-start.1 = ((bf16[4,256,512]{2,1,0:T(8,128)(2,1)}), bf16[4,256,512]{2,1,0:T(8,128)(2,1)S(1)}, u32[]{:S(2)}, u32[]{:S(2)}) async-start(bf16[4,256,512]{2,1,0:T(8,128)(2,1)} %broadcast_in_dim.23), calls=%async_computation.1 | async-start | bytes 2097152 | tf_op jit(solution)/shard_map/all_to_all | solution.py:60
  153.3 15.3 %copy-start.8 = (s32[2]{0:T(128)S(1)}, s32[2]{0:T(128)}, u32[]{:S(2)}) copy-start(s32[2]{0:T(128)} %param.15) | copy-start | bytes 28
  153.3 15.3 %copy-start.9 = (s32[2]{0:T(128)S(1)}, s32[2]{0:T(128)}, u32[]{:S(2)}) copy-start(s32[2]{0:T(128)} %param.14) | copy-start | bytes 28
  159.7 8.9 %all-to-all-start.3 = ((f32[8,8,256]{2,1,0:T(8,128)}), f32[8,8,256]{2,1,0:T(8,128)S(1)}, u32[]{:S(2)}, u32[]{:S(2)}) async-start(f32[8,8,256]{2,1,0:T(8,128)} %broadcast_in_dim.27), calls=%async_computation.3 | async-start | bytes 131072 | tf_op jit(solution)/shard_map/all_to_all | solution.py:60
  169.4 17.2 %all-to-all-start.4 = ((f32[8,1,2]{2,1,0:T(1,128)}), f32[8,1,2]{2,1,0:T(1,128)S(1)}, u32[]{:S(2)}, u32[]{:S(2)}) async-start(f32[8,1,2]{2,1,0:T(1,128)} %broadcast_in_dim.28), calls=%async_computation.4 | async-start | bytes 8192 | tf_op jit(solution)/shard_map/all_to_all | solution.py:60
  187.2 17.2 %all-to-all-start.5 = ((f32[8,1,2]{2,1,0:T(1,128)}), f32[8,1,2]{2,1,0:T(1,128)S(1)}, u32[]{:S(2)}, u32[]{:S(2)}) async-start(f32[8,1,2]{2,1,0:T(1,128)} %broadcast_in_dim.29), calls=%async_computation.5 | async-start | bytes 8192 | tf_op jit(solution)/shard_map/all_to_all | solution.py:60
  (3 other events, 12.2 us)
Sparse Core Ops, SparseCore 0:
  38.2 46.6 all-gather.2
  87.0 57.2 all-gather.4

commit v2 on v1

v2 whole, which is shorter than its diff:
```python
import jax
import jax.numpy as jnp
import numpy as np
from jax import lax
from jax.experimental import pallas as pl
from jax.experimental.pallas import tpu as pltpu
from jax.sharding import Mesh
from jax.sharding import PartitionSpec as P


HD = 128
GROUP = 2
NORM_EPS = 1e-06
QUERY_SCALE = 168.0 ** (-0.5)
ROPE_BASE = 10000.0
SIZES = (2, 2, 8, 4, 2, 2)
AXES = ("xh", "core", "z", "yy", "p", "xl")
SECTION = ("xh", "core")
SEQ = ("z", "yy", "p", "xl")
AXIS_Y = ("yy", "p")
OCTANT = ("xh", "xl", "p")
NT = (((1,), (1,)), ((), ()))


def pairs_of(source_of):
    out = []
    for there in np.ndindex(*SIZES):
        here = source_of(*there)
        if here is not None:
            out.append(
                (int(np.ravel_multi_index(here, SIZES)), int(np.ravel_multi_index(there, SIZES)))
            )
    return out


def row_source(xh, c, z, yy, p, l):
    return (xh, l, z, 2 * c + yy // 2, yy % 2, p)


def out_source(xh, c, z, yy, p, l):
    s, o = divmod(2 * z + c, 4)
    q = 32 * (2 * xh + l) + 8 * o + 2 * yy + p
    return (s // 2, s % 2, q // 16, (q // 4) % 4, (q // 2) % 2, q % 2)


def beside(across_p, across_l):
    return lambda xh, c, z, yy, p, l: (xh, c, z, yy, p ^ across_p, l ^ across_l)


def block_before(xh, c, z, yy, p, l):
    block = 4 * z + yy - 1
    return None if block < 0 else (xh, c, block // 4, block % 4, p, l)


def moved(array, source_of):
    return lax.ppermute(array, AXES, pairs_of(source_of))


def told_to_all(array, axes):
    n = lax.axis_size(axes)
    return lax.all_to_all(jnp.broadcast_to(array[None], (n, *array.shape)), axes, 0, 0, tiled=True)


def exchanged(tiles, axes):
    return lax.all_to_all(tiles, axes, 0, 0, tiled=True)


def norm_kernel(order_ref, gain_ref, *refs):
    for k in range(4):
        wide = refs[k][...].astype(jnp.float32)
        inverse = lax.rsqrt(jnp.mean(wide * wide, axis=1, keepdims=True) + NORM_EPS)
        rows = wide.shape[0]
        at = pl.multiple_of(order_ref[k] * rows, rows)
        refs[4][pl.ds(at, rows), :] = (wide * inverse * gain_ref[...]).astype(jnp.bfloat16)


def normed_rows(order, gain, pieces):
    rows, width = pieces[0].shape
    vmem = pl.BlockSpec(memory_space=pltpu.VMEM)
    return pl.pallas_call(
        norm_kernel,
        in_specs=[pl.BlockSpec(memory_space=pltpu.SMEM)] + [vmem] * 5,
        out_specs=vmem,
        out_shape=jax.ShapeDtypeStruct((4 * rows, width), jnp.bfloat16),
        name="norm",
    )(order, gain, *pieces)


def project_kernel(turned_heads, rows_ref, w_ref, gain_ref, cos_ref, sin_ref, out_ref):
    acc = jnp.dot(rows_ref[...], w_ref[...], preferred_element_type=jnp.float32)

    def turn():
        unit = acc * lax.rsqrt(jnp.mean(acc * acc, axis=1, keepdims=True) + NORM_EPS)
        unit = unit * gain_ref[...]
        other = pltpu.roll(unit, HD // 2, 1)
        out_ref[...] = (unit * cos_ref[...] + other * sin_ref[...]).astype(jnp.bfloat16)

    if turned_heads == 2:
        turn()
    else:
        pl.when(pl.program_id(0) == 0)(turn)

        @pl.when(pl.program_id(0) == 1)
        def _():
            out_ref[...] = acc.astype(jnp.bfloat16)


def project(normed, weights, gain, cos, sin, first, turned_heads):
    rows, width = normed.shape
    vmem = pl.BlockSpec(memory_space=pltpu.VMEM)
    return pl.pallas_call(
        lambda *refs: project_kernel(turned_heads, *refs),
        grid=(2,),
        in_specs=[
            vmem,
            pl.BlockSpec((width, HD), lambda j: (0, j + first)),
            vmem,
            vmem,
            vmem,
        ],
        out_specs=pl.BlockSpec((rows, HD), lambda j: (0, j)),
        out_shape=jax.ShapeDtypeStruct((rows, 2 * HD), jnp.bfloat16),
        name="project",
    )(normed, weights, gain, cos, sin)


def attend_kernel(block_ref, q_ref, own_ref, back1_ref, back2_ref, out_ref):
    held = (back2_ref, back1_ref, own_ref)
    rows = q_ref.shape[0] // 2
    block = block_ref[0]
    query = lax.broadcasted_iota(jnp.int32, (rows, rows), 0)
    key = lax.broadcasted_iota(jnp.int32, (rows, rows), 1)
    for a in range(2):
        pieces = [
            held[i // 2][(i % 2) * rows : (i % 2 + 1) * rows, :] for i in range(a, a + 5)
        ]
        for g in range(GROUP):
            q = q_ref[a * rows : (a + 1) * rows, g * HD : (g + 1) * HD]
            scores = []
            for k, piece in enumerate(pieces):
                s = lax.dot_general(q, piece[:, :HD], NT, preferred_element_type=jnp.float32)
                there = 2 * block + (a + k - 4) >= 0
                if k == 4:
                    s = jnp.where(key <= query, s, -1e30)
                elif k == 0:
                    s = jnp.where((key > query) & there, s, -1e30)
                elif a + k < 4:
                    s = jnp.where(there, s, -1e30)
                scores.append(s)
            top = jnp.max(scores[0], axis=1, keepdims=True)
            for s in scores[1:]:
                top = jnp.maximum(top, jnp.max(s, axis=1, keepdims=True))
            total, mixed = 0.0, 0.0
            for s, piece in zip(scores, pieces):
                e = jnp.exp(s - top)
                total = total + jnp.sum(e, axis=1, keepdims=True)
                mixed = mixed + jnp.dot(
                    e.astype(jnp.bfloat16), piece[:, HD:], preferred_element_type=jnp.float32
                )
            mixed = (mixed / total).astype(jnp.bfloat16)
            for x in range(4):
                out_ref[2 * x + a, :, g * HD : (g + 1) * HD] = mixed


def attend(block, q, held):
    rows, wide = q.shape
    vmem = pl.BlockSpec(memory_space=pltpu.VMEM)
    return pl.pallas_call(
        attend_kernel,
        in_specs=[pl.BlockSpec(memory_space=pltpu.SMEM)] + [vmem] * 4,
        out_specs=vmem,
        out_shape=jax.ShapeDtypeStruct((8, rows // 2, wide), jnp.bfloat16),
        name="attend",
    )(block, q, *held)


def sums_kernel(mixed_ref, w_ref, gains_ref, h_ref, out_ref, sums_ref):
    o = pl.program_id(0)

    @pl.when(o == 0)
    def _():
        sums_ref[...] = jnp.zeros_like(sums_ref)

    wide = mixed_ref.shape[2]
    branch = 0.0
    for head in range(8):
        at = (head % 2) * wide
        branch = branch + lax.dot_general(
            w_ref[head // 2, 0, :, at : at + wide],
            mixed_ref[head],
            NT,
            preferred_element_type=jnp.float32,
        )
    gains = gains_ref[0]
    post, final, head = gains[:, 0:1], gains[:, 1:2], gains[:, 2:3]
    read = final * head
    hidden = h_ref[0].astype(jnp.float32)
    scaled = branch * post
    for k, term in enumerate(
        (
            branch * branch,
            scaled * scaled,
            hidden * scaled,
            scaled * read,
            hidden * read,
            hidden * hidden,
        )
    ):
        sums_ref[k : k + 1, :] += jnp.sum(term, axis=0, keepdims=True)

    @pl.when(o == pl.num_programs(0) - 1)
    def _():
        for k in range(out_ref.shape[0]):
            out_ref[k] = sums_ref[...]


def token_sums(mixed, weights, gains, h_share, copies):
    rows = mixed.shape[1]
    _, parts, depth, wide = weights.shape
    return pl.pallas_call(
        sums_kernel,
        grid=(parts,),
        in_specs=[
            pl.BlockSpec(memory_space=pltpu.VMEM),
            pl.BlockSpec((4, 1, depth, wide), lambda o: (0, o, 0, 0)),
            pl.BlockSpec((1, depth, 3), lambda o: (o, 0, 0)),
            pl.BlockSpec((1, depth, rows), lambda o: (o, 0, 0)),
        ],
        out_specs=pl.BlockSpec((copies, 8, rows), lambda o: (0, 0, 0)),
        out_shape=jax.ShapeDtypeStruct((copies, 8, rows), jnp.float32),
        scratch_shapes=[pltpu.VMEM((8, rows), jnp.float32)],
        name="token_sums",
    )(mixed, weights, gains, h_share)


def local(
    hidden,
    lengths,
    reward_pos,
    in_gain,
    w_query,
    w_key,
    w_value,
    query_gain,
    key_gain,
    w_out,
    post_gain,
    final_gain,
    value_head,
):
    _, tok_dev, width = hidden.shape
    shard = in_gain.shape[0]
    octet_rows = 8 * shard
    rows = 2 * tok_dev
    block = 4 * lax.axis_index("z") + lax.axis_index("yy")
    parity, half = lax.axis_index("p"), lax.axis_index("xl")
    place = 2 * lax.axis_index("xh") + half

    def with_row(tile, values):
        return jnp.concatenate([tile, jnp.pad(values, (0, 4 * HD - values.shape[0]))[None]], axis=0)

    heads = [
        with_row(
            jnp.concatenate(
                [
                    w_query[:, 2 * k * HD : 2 * (k + 1) * HD],
                    w_key[:, k * HD : (k + 1) * HD],
                    w_value[:, k * HD : (k + 1) * HD],
                ],
                axis=1,
            ),
            in_gain,
        )
        for k in range(2)
    ]
    out_shard = with_row(w_out.T, jnp.concatenate([post_gain, final_gain, value_head]))
    heads = moved(jnp.stack(heads), row_source)
    out_shard = moved(out_shard, out_source)
    tiles = jnp.concatenate(
        [jnp.tile(heads, (4, 1, 1)), jnp.broadcast_to(out_shard, (8, *out_shard.shape))], axis=2
    )
    octet = exchanged(tiles, AXIS_Y)
    gains = [octet[:, shard, at : at + shard] for at in (0, *range(4 * HD, 4 * HD + 3 * shard, shard))]
    gains = jnp.stack(gains).reshape(4, octet_rows)
    gains = jnp.pad(gains, ((0, 0), (0, 256 - octet_rows)))
    octet = octet[:, :shard].reshape(octet_rows, 8 * HD)
    weights = lax.all_gather(octet[:, : 4 * HD], ("z", "core"), axis=0, tiled=True)
    out_weights = lax.all_gather(octet[:, 4 * HD :], ("z", "core"), axis=0, tiled=True)
    out_weights = out_weights.reshape(4, 4, octet_rows, -1)
    gains = told_to_all(gains, ("z", "core"))
    gains = gains[:, :, :octet_rows].astype(jnp.float32)
    in_full = gains[:, 0].reshape(1, width)
    out_gains = gains[:4, 1:].swapaxes(1, 2)

    mine = lax.dynamic_index_in_dim(hidden, lax.axis_index("core"), 0, keepdims=False)
    near = moved(mine, beside(0, 1))
    far = moved(mine, beside(1, 0)), moved(mine, beside(1, 1))
    pieces = (mine, near, *far)
    order = jnp.stack(
        [
            2 * parity + half,
            2 * parity + 1 - half,
            2 - 2 * parity + half,
            2 - 2 * parity + 1 - half,
        ]
    )
    normed = normed_rows(order, in_full, pieces)
    h_share = jnp.concatenate(
        [jnp.where(half == 0, mine, near), jnp.where(half == 0, near, mine)], axis=0
    )
    h_share = lax.dynamic_slice_in_dim(h_share, place * (width // 4), width // 4, 1)
    h_share = h_share.T.reshape(4, octet_rows, rows)

    pos = block * 2 * rows + jnp.arange(2 * rows, dtype=jnp.int32)
    frequency = ROPE_BASE ** (-jnp.arange(HD // 2, dtype=jnp.float32) * 2.0 / HD)
    angles = pos.astype(jnp.float32)[:, None] * frequency[None, :]
    cos, sin = jnp.cos(angles), jnp.sin(angles)
    cos = jnp.concatenate([cos, cos], axis=1)
    sin = jnp.concatenate([-sin, sin], axis=1)

    held = [project(normed, weights, key_gain[None], cos, sin, 2, 1)]
    for _ in range(2):
        held.append(moved(held[-1], block_before))
    q = project(normed, weights, (query_gain * QUERY_SCALE)[None], cos, sin, 0, 2)
    mixed = exchanged(attend(block[None], q, held), OCTANT)

    sums = exchanged(token_sums(mixed, out_weights, out_gains, h_share, 16), OCTANT + ("core",))
    sums = sums.reshape(4, 2, 2, 8, rows).sum(axis=0)
    branch_sq, scaled_sq, cross, read_branch, read_hidden, hidden_sq = (
        sums[:, :, k] for k in range(6)
    )
    scale = lax.rsqrt(branch_sq / width + NORM_EPS)
    residual_sq = hidden_sq + scale * (2.0 * cross + scale * scaled_sq)
    residual_sq = jnp.maximum(residual_sq, 0.0)
    values = (read_hidden + scale * read_branch) * lax.rsqrt(residual_sq / width + NORM_EPS)
    pos = pos.reshape(2, 1, rows)
    values = jnp.where(pos < lengths[None, :, None], values, 0.0)
    reward = jnp.sum(jnp.where(pos == reward_pos[None, :, None], values, 0.0), axis=(0, 2))
    reward = told_to_all(reward, ("z", "yy")).sum(axis=0)
    token_values = lax.dynamic_index_in_dim(values, parity, 0, keepdims=False)
    token_values = lax.dynamic_slice_in_dim(token_values, half * tok_dev, tok_dev, 1)
    return token_values, reward


def solution(mesh):
    torus = Mesh(mesh.devices.reshape(SIZES), AXES)
    in_specs = (
        P(None, SEQ, None),
        P(),
        P(),
        P(SEQ),
        P(SEQ, SECTION),
        P(SEQ, SECTION),
        P(SEQ, SECTION),
        P(),
        P(),
        P(SECTION, SEQ),
        P(SEQ),
        P(SEQ),
        P(SEQ),
    )
    out_specs = (P(None, SEQ), P())

    return jax.shard_map(local, mesh=torus, in_specs=in_specs, out_specs=out_specs, check_vma=False)
```

time: 213 us -> 206 us (0.967)
  the two profiles are of different devices: /device:TPU:2 before, /device:TPU:1 now
where the time goes in v2:
time: 206 us
  starting transfers between devices  70.5 us (34%)
  waiting for transfers between devices  58.7 us (28%)
  Pallas kernels  24.2 us (12%)
  blocking collectives  21.4 us (10%)
  between operations  14.3 us (7%)
  local copies, waits for them, and re-layouts  10.6 us (5%)
  other arithmetic  5.83 us (3%)
    all_to_all x2, starting transfers between devices, told_to_all(): lax.all_to_all(jnp.broadcast_to(array[None], (n, *array.shape)), axes, 0,...  31.9 us
    ppermute x7, starting transfers between devices, moved(): return lax.ppermute(array, AXES, pairs_of(source_of))  28 us
    all_to_all x1, blocking collectives, exchanged(): return lax.all_to_all(tiles, axes, 0, 0, tiled=True)  21.4 us
    ppermute x7, waiting for transfers between devices, moved(): return lax.ppermute(array, AXES, pairs_of(source_of))  19.4 us
    all_to_all x2, waiting for transfers between devices, told_to_all(): lax.all_to_all(jnp.broadcast_to(array[None], (n, *array.shape)), axes, 0,...  17.2 us
    all_to_all x2, waiting for transfers between devices, exchanged(): return lax.all_to_all(tiles, axes, 0, 0, tiled=True)  14.4 us
    all_to_all x2, starting transfers between devices, exchanged(): return lax.all_to_all(tiles, axes, 0, 0, tiled=True)  10.6 us
    pallas_call x2, Pallas kernels, project(): pl.pallas_call(lambda *refs: project_kernel(turned_heads, *refs), grid=(2...  9.81 us
  transfers between devices with their start and end apart: 13, of which 9 were waited for; matrix products, arithmetic and copies ran while one was open for 5% of the time, Pallas kernels for 9%

profile of v2, /device:TPU:1, one launch (start us, length us, event | category | flops | bytes accessed | tf_op | source)
XLA Modules:
  0.0 205.6 jit_solution(4640428098782764883)
XLA Ops:
  9.4 4.5 %collective-permute-start = (bf16[2,22,512]{2,1,0:T(8,128)(2,1)S(1)}, bf16[2,22,512]{2,1,0:T(8,128)(2,1)S(1)}, u32[]{:S(2)}, u32[]{:S(2)}) collective-permute-start(bf16[2,22,512]{2,1,0:T(8,128)(2,1)S(1)} %pad_maximum_fusion.3), channel_id=1, source_target_pairs={{0,0},{128,1},{1,2},{129,3},{2,4},{130,5},{3,6},{131,7},{4,8},{132... | collective-permute-start | bytes 135176 | tf_op jit(solution)/shard_map/ppermute | solution.py:56
  15.4 3.3 %collective-permute-start.1 = (bf16[22,512]{1,0:T(8,128)(2,1)S(1)}, bf16[22,512]{1,0:T(8,128)(2,1)S(1)}, u32[]{:S(2)}, u32[]{:S(2)}) collective-permute-start(bf16[22,512]{1,0:T(8,128)(2,1)S(1)} %pad_maximum_fusion.6), channel_id=1, source_target_pairs={{0,0},{32,1},{1,2},{33,3},{2,4},{34,5},{3,6},{35,7},{4,8},{36,9},{... | collective-permute-start | bytes 67592 | tf_op jit(solution)/shard_map/ppermute | solution.py:56
  18.8 5.9 %collective-permute-done.1 = bf16[22,512]{1,0:T(8,128)(2,1)S(1)} collective-permute-done((bf16[22,512]{1,0:T(8,128)(2,1)S(1)}, bf16[22,512]{1,0:T(8,128)(2,1)S(1)}, u32[]{:S(2)}, u32[]{:S(2)}) %collective-permute-start.1) | collective-permute-done | bytes 22560 | tf_op jit(solution)/shard_map/ppermute | solution.py:56
  24.8 21.4 %all_to_all.26 = bf16[8,22,1024]{2,1,0:T(8,128)(2,1)S(1)} all-to-all(bf16[8,22,1024]{2,1,0:T(8,128)(2,1)S(1)} %pad_maximum_fusion), channel_id=1, replica_groups=mesh['xh'=2,'core'=2,'z'=8,'yy'=4,'p'=2,'xl'=2] {'yy','p'}, dimensions={0} | all-to-all | bytes 720896 | tf_op jit(solution)/shard_map/all_to_all | solution.py:65
  52.6 3.8 %collective-permute-start.4 = (bf16[128,2688]{1,0:T(8,128)(2,1)S(1)}, bf16[128,2688]{1,0:T(8,128)(2,1)}, u32[]{:S(2)}, u32[]{:S(2)}) collective-permute-start(bf16[128,2688]{1,0:T(8,128)(2,1)S(1)} %dynamic-slice_bitcast_fusion.refs_0_), channel_id=1, source_target_pairs={{3,0},{2,1},{1,2},{0,3},{7,4},{6,5},{5,6},{4,7},{11,8},{10,9},{9,1... | collective-permute-start | bytes 2064392 | tf_op jit(solution)/shard_map/ppermute | solution.py:56
  59.5 18.2 %all-to-all-start.1 = ((bf16[16,4,256]{2,1,0:T(4,128)(2,1)}), bf16[16,4,256]{2,1,0:T(4,128)(2,1)S(1)}, u32[]{:S(2)}, u32[]{:S(2)}) async-start(bf16[16,4,256]{2,1,0:T(4,128)(2,1)} %broadcast_in_dim.42), calls=%async_computation.1 | async-start | bytes 65536 | tf_op jit(solution)/shard_map/all_to_all | solution.py:61
  78.3 6.9 %all-to-all-done.1 = bf16[16,4,256]{2,1,0:T(4,128)(2,1)S(1)} async-done(((bf16[16,4,256]{2,1,0:T(4,128)(2,1)}), bf16[16,4,256]{2,1,0:T(4,128)(2,1)S(1)}, u32[]{:S(2)}, u32[]{:S(2)}) %all-to-all-start.1) | async-done | bytes 32800 | tf_op jit(solution)/shard_map/all_to_all | solution.py:61
  86.8 4.8 %norm.1.refs_0_ = bf16[512,2688]{1,0:T(8,128)(2,1)} custom-call(s32[4]{0:T(128)} %pad_add_fusion.order_ref, f32[1,2688]{1,0:T(1,128)} %reshape_squeeze.3.gain_ref, bf16[128,2688]{1,0:T(8,128)(2,1)} %copy-done.3, bf16[128,2688]{1,0:T(8,128)(2,1)} %copy-done.1, bf16[128,2688]{1,0:T(8,128)(2,1)} %collective-permute-done.3.refs_2_, ...), custom_call_target="tpu_custom_call" | custom-call | tf_op jit(solution)/shard_map/norm/pallas_call | solution.py:80
  91.6 3.3 %all-gather.3.cloned.1.call-done.refs_1_ = bf16[2688,512]{1,0:T(8,128)(2,1)} async-done(((bf16[168,512]{1,0:T(8,128)(2,1)}), bf16[2688,512]{1,0:T(8,128)(2,1)}) %all-gather.3.cloned.1.call-update) | async-done | bytes 2752528 | tf_op jit(solution)/shard_map/all_gather | solution.py:287
  94.9 4.8 %project.3.own_ref = bf16[512,256]{1,0:T(8,128)(2,1)} custom-call(bf16[512,2688]{1,0:T(8,128)(2,1)} %norm.1.refs_0_, bf16[2688,512]{1,0:T(8,128)(2,1)} %all-gather.3.cloned.1.call-done.refs_1_, f32[1,128]{1,0:T(1,128)} %bitcast.80, f32[512,128]{1,0:T(8,128)} %get-tuple-element.31.refs_3_, f32[512,128]{1,0:T(8,128)} %get-tuple-element.32.refs_4_), custom_call_target="tpu_custom_call" | custom-call | tf_op jit(solution)/shard_map/project/pallas_call | solution.py:111
  99.7 3.9 %collective-permute-start.5 = (bf16[512,256]{1,0:T(8,128)(2,1)}, bf16[512,256]{1,0:T(8,128)(2,1)S(1)}, u32[]{:S(2)}, u32[]{:S(2)}) collective-permute-start(bf16[512,256]{1,0:T(8,128)(2,1)} %project.3.own_ref), channel_id=1, source_target_pairs={{0,4},{1,5},{2,6},{3,7},{4,8},{5,9},{6,10},{7,11},{8,12},{9,13},{1... | collective-permute-start | bytes 786440 | tf_op jit(solution)/shard_map/ppermute | solution.py:56
  103.6 9.5 %collective-permute-done.5.back1_ref = bf16[512,256]{1,0:T(8,128)(2,1)S(1)} collective-permute-done((bf16[512,256]{1,0:T(8,128)(2,1)}, bf16[512,256]{1,0:T(8,128)(2,1)S(1)}, u32[]{:S(2)}, u32[]{:S(2)}) %collective-permute-start.5) | collective-permute-done | bytes 262176 | tf_op jit(solution)/shard_map/ppermute | solution.py:56
  113.1 7.9 %collective-permute-start.6 = (bf16[512,256]{1,0:T(8,128)(2,1)S(1)}, bf16[512,256]{1,0:T(8,128)(2,1)S(1)}, u32[]{:S(2)}, u32[]{:S(2)}) collective-permute-start(bf16[512,256]{1,0:T(8,128)(2,1)S(1)} %collective-permute-done.5.back1_ref), channel_id=1, source_target_pairs={{0,4},{1,5},{2,6},{3,7},{4,8},{5,9},{6,10},{7,11},{8,12},{9,13},{1... | collective-permute-start | bytes 786440 | tf_op jit(solution)/shard_map/ppermute | solution.py:56
  121.5 5.0 %project.2.q_ref = bf16[512,256]{1,0:T(8,128)(2,1)} custom-call(bf16[512,2688]{1,0:T(8,128)(2,1)} %norm.1.refs_0_, bf16[2688,512]{1,0:T(8,128)(2,1)} %all-gather.3.cloned.1.call-done.refs_1_, f32[1,128]{1,0:T(1,128)} %multiply_bitcast_fusion.refs_2_, f32[512,128]{1,0:T(8,128)} %get-tuple-element.31.refs_3_, f32[512,128]{1,0:T(8,128)} %get-tuple-element.32.refs_4_), custom_call_target="tpu_custom_call" | custom-call | tf_op jit(solution)/shard_map/project/pallas_call | solution.py:111
  126.5 4.0 %collective-permute-done.6.back2_ref = bf16[512,256]{1,0:T(8,128)(2,1)S(1)} collective-permute-done((bf16[512,256]{1,0:T(8,128)(2,1)S(1)}, bf16[512,256]{1,0:T(8,128)(2,1)S(1)}, u32[]{:S(2)}, u32[]{:S(2)}) %collective-permute-start.6) | collective-permute-done | bytes 262176 | tf_op jit(solution)/shard_map/ppermute | solution.py:56
  131.1 4.6 %attend.1 = bf16[8,256,256]{2,1,0:T(8,128)(2,1)} custom-call(s32[1]{0:T(128)} %bitcast.block_ref, bf16[512,256]{1,0:T(8,128)(2,1)} %project.2.q_ref, bf16[512,256]{1,0:T(8,128)(2,1)} %project.3.own_ref, bf16[512,256]{1,0:T(8,128)(2,1)} %copy-done.5, bf16[512,256]{1,0:T(8,128)(2,1)} %copy-done.6), custom_call_target="tpu_custom_call" | custom-call | tf_op jit(solution)/shard_map/attend/pallas_call | solution.py:168
  135.8 4.7 %all-to-all-start.2 = ((bf16[8,256,256]{2,1,0:T(8,128)(2,1)}), bf16[8,256,256]{2,1,0:T(8,128)(2,1)S(1)}, u32[]{:S(2)}, u32[]{:S(2)}) async-start(bf16[8,256,256]{2,1,0:T(8,128)(2,1)} %attend.1), calls=%async_computation.2 | async-start | bytes 2097152 | tf_op jit(solution)/shard_map/all_to_all | solution.py:65
  142.6 3.7 %all-gather.5.cloned.1.call-done = bf16[2688,512]{1,0:T(8,128)(2,1)} async-done(((bf16[168,512]{1,0:T(8,128)(2,1)}), bf16[2688,512]{1,0:T(8,128)(2,1)}) %all-gather.5.cloned.1.call-update) | async-done | bytes 2752528 | tf_op jit(solution)/shard_map/all_gather | solution.py:288
  146.4 8.2 %all-to-all-done.2.mixed_ref = bf16[8,256,256]{2,1,0:T(8,128)(2,1)S(1)} async-done(((bf16[8,256,256]{2,1,0:T(8,128)(2,1)}), bf16[8,256,256]{2,1,0:T(8,128)(2,1)S(1)}, u32[]{:S(2)}, u32[]{:S(2)}) %all-to-all-start.2) | async-done | bytes 1048608 | tf_op jit(solution)/shard_map/all_to_all | solution.py:65
  155.5 5.0 %token_sums.1 = f32[16,8,256]{2,1,0:T(8,128)} custom-call(bf16[8,256,256]{2,1,0:T(8,128)(2,1)} %copy-done, bf16[4,4,168,512]{3,2,1,0:T(8,128)(2,1)} %bitcast.73, f32[4,168,3]{2,1,0:T(8,128)} %bitcast.76, bf16[4,168,256]{2,1,0:T(8,128)(2,1)} %bitcast.75), custom_call_target="tpu_custom_call" | custom-call | tf_op jit(solution)/shard_map/token_sums/pallas_call | solution.py:220
  160.5 5.9 %all-to-all-start.3 = ((f32[16,8,256]{2,1,0:T(8,128)}), f32[16,8,256]{2,1,0:T(8,128)S(1)}, u32[]{:S(2)}, u32[]{:S(2)}) async-start(f32[16,8,256]{2,1,0:T(8,128)} %token_sums.1), calls=%async_computation.3 | async-start | bytes 262144 | tf_op jit(solution)/shard_map/all_to_all | solution.py:65
  166.4 6.2 %all-to-all-done.3 = f32[16,8,256]{2,1,0:T(8,128)S(1)} async-done(((f32[16,8,256]{2,1,0:T(8,128)}), f32[16,8,256]{2,1,0:T(8,128)S(1)}, u32[]{:S(2)}, u32[]{:S(2)}) %all-to-all-start.3) | async-done | bytes 131104 | tf_op jit(solution)/shard_map/all_to_all | solution.py:65
  173.5 13.7 %all-to-all-start.4 = ((f32[32,1,2]{2,1,0:T(1,128)}), f32[32,1,2]{2,1,0:T(1,128)S(1)}, u32[]{:S(2)}, u32[]{:S(2)}) async-start(f32[32,1,2]{2,1,0:T(1,128)} %broadcast_in_dim.45), calls=%async_computation.4 | async-start | bytes 32768 | tf_op jit(solution)/shard_map/all_to_all | solution.py:61
  187.9 10.4 %all-to-all-done.4 = f32[32,1,2]{2,1,0:T(1,128)S(1)} async-done(((f32[32,1,2]{2,1,0:T(1,128)}), f32[32,1,2]{2,1,0:T(1,128)S(1)}, u32[]{:S(2)}, u32[]{:S(2)}) %all-to-all-start.4) | async-done | bytes 288 | tf_op jit(solution)/shard_map/all_to_all | solution.py:61
  (73 shorter events, 21.8 us)
Async XLA Ops:
  7.2 87.7 %all-gather.3.cloned.1.call-start = ((), (), s32[]{:S(2)}) async-start(), calls=%async_computation.5 | async-start | bytes 2924544 | tf_op jit(solution)/shard_map/all_gather | solution.py:287
  9.4 15.3 %collective-permute-start = (bf16[2,22,512]{2,1,0:T(8,128)(2,1)S(1)}, bf16[2,22,512]{2,1,0:T(8,128)(2,1)S(1)}, u32[]{:S(2)}, u32[]{:S(2)}) collective-permute-start(bf16[2,22,512]{2,1,0:T(8,128)(2,1)S(1)} %pad_maximum_fusion.3), channel_id=1, source_target_pairs={{0,0},{128,1},{1,2},{129,3},{2,4},{130,5},{3,6},{131,7},{4,8},{132... | collective-permute-start | bytes 135176 | tf_op jit(solution)/shard_map/ppermute | solution.py:56
  15.4 9.3 %collective-permute-start.1 = (bf16[22,512]{1,0:T(8,128)(2,1)S(1)}, bf16[22,512]{1,0:T(8,128)(2,1)S(1)}, u32[]{:S(2)}, u32[]{:S(2)}) collective-permute-start(bf16[22,512]{1,0:T(8,128)(2,1)S(1)} %pad_maximum_fusion.6), channel_id=1, source_target_pairs={{0,0},{32,1},{1,2},{33,3},{2,4},{34,5},{3,6},{35,7},{4,8},{36,9},{... | collective-permute-start | bytes 67592 | tf_op jit(solution)/shard_map/ppermute | solution.py:56
  24.8 23.1 %copy-start.4 = (bf16[2,128,2688]{2,1,0:T(8,128)(2,1)S(1)}, bf16[2,128,2688]{2,1,0:T(8,128)(2,1)}, u32[]{:S(2)}) copy-start(bf16[2,128,2688]{2,1,0:T(8,128)(2,1)} %param.13) | copy-start | bytes 4128772
  47.2 99.2 %all-gather.5.cloned.1.call-start = ((), (), s32[]{:S(2)}) async-start(), calls=%async_computation.6 | async-start | bytes 2924544 | tf_op jit(solution)/shard_map/all_gather | solution.py:288
  48.0 37.9 %copy-start.3 = (bf16[128,2688]{1,0:T(8,128)(2,1)}, bf16[128,2688]{1,0:T(8,128)(2,1)S(1)}, u32[]{:S(2)}) copy-start(bf16[128,2688]{1,0:T(8,128)(2,1)S(1)} %dynamic-slice_bitcast_fusion.refs_0_) | copy-start | bytes 2064388
  48.0 37.9 %collective-permute-start.2 = (bf16[128,2688]{1,0:T(8,128)(2,1)S(1)}, bf16[128,2688]{1,0:T(8,128)(2,1)S(1)}, u32[]{:S(2)}, u32[]{:S(2)}) collective-permute-start(bf16[128,2688]{1,0:T(8,128)(2,1)S(1)} %dynamic-slice_bitcast_fusion.refs_0_), channel_id=1, source_target_pairs={{1,0},{0,1},{3,2},{2,3},{5,4},{4,5},{7,6},{6,7},{9,8},{8,9},{11,10... | collective-permute-start | bytes 2064392 | tf_op jit(solution)/shard_map/ppermute | solution.py:56
  50.7 35.2 %collective-permute-start.3 = (bf16[128,2688]{1,0:T(8,128)(2,1)S(1)}, bf16[128,2688]{1,0:T(8,128)(2,1)}, u32[]{:S(2)}, u32[]{:S(2)}) collective-permute-start(bf16[128,2688]{1,0:T(8,128)(2,1)S(1)} %dynamic-slice_bitcast_fusion.refs_0_), channel_id=1, source_target_pairs={{2,0},{3,1},{0,2},{1,3},{6,4},{7,5},{4,6},{5,7},{10,8},{11,9},{8,1... | collective-permute-start | bytes 2064392 | tf_op jit(solution)/shard_map/ppermute | solution.py:56
  52.6 33.3 %collective-permute-start.4 = (bf16[128,2688]{1,0:T(8,128)(2,1)S(1)}, bf16[128,2688]{1,0:T(8,128)(2,1)}, u32[]{:S(2)}, u32[]{:S(2)}) collective-permute-start(bf16[128,2688]{1,0:T(8,128)(2,1)S(1)} %dynamic-slice_bitcast_fusion.refs_0_), channel_id=1, source_target_pairs={{3,0},{2,1},{1,2},{0,3},{7,4},{6,5},{5,6},{4,7},{11,8},{10,9},{9,1... | collective-permute-start | bytes 2064392 | tf_op jit(solution)/shard_map/ppermute | solution.py:56
  59.5 25.6 %all-to-all-start.1 = ((bf16[16,4,256]{2,1,0:T(4,128)(2,1)}), bf16[16,4,256]{2,1,0:T(4,128)(2,1)S(1)}, u32[]{:S(2)}, u32[]{:S(2)}) async-start(bf16[16,4,256]{2,1,0:T(4,128)(2,1)} %broadcast_in_dim.42), calls=%async_computation.1 | async-start | bytes 65536 | tf_op jit(solution)/shard_map/all_to_all | solution.py:61
  85.9 0.9 copy-start.1
  94.9 26.1 %copy-start.9 = (f32[128]{0:T(128)S(1)}, f32[128]{0:T(128)}, u32[]{:S(2)}) copy-start(f32[128]{0:T(128)} %param.20) | copy-start | bytes 1540
  99.7 13.4 %collective-permute-start.5 = (bf16[512,256]{1,0:T(8,128)(2,1)}, bf16[512,256]{1,0:T(8,128)(2,1)S(1)}, u32[]{:S(2)}, u32[]{:S(2)}) collective-permute-start(bf16[512,256]{1,0:T(8,128)(2,1)} %project.3.own_ref), channel_id=1, source_target_pairs={{0,4},{1,5},{2,6},{3,7},{4,8},{5,9},{6,10},{7,11},{8,12},{9,13},{1... | collective-permute-start | bytes 786440 | tf_op jit(solution)/shard_map/ppermute | solution.py:56
  113.1 13.4 %copy-start.5 = (bf16[512,256]{1,0:T(8,128)(2,1)}, bf16[512,256]{1,0:T(8,128)(2,1)S(1)}, u32[]{:S(2)}) copy-start(bf16[512,256]{1,0:T(8,128)(2,1)S(1)} %collective-permute-done.5.back1_ref) | copy-start | bytes 786436
  113.1 17.4 %collective-permute-start.6 = (bf16[512,256]{1,0:T(8,128)(2,1)S(1)}, bf16[512,256]{1,0:T(8,128)(2,1)S(1)}, u32[]{:S(2)}, u32[]{:S(2)}) collective-permute-start(bf16[512,256]{1,0:T(8,128)(2,1)S(1)} %collective-permute-done.5.back1_ref), channel_id=1, source_target_pairs={{0,4},{1,5},{2,6},{3,7},{4,8},{5,9},{6,10},{7,11},{8,12},{9,13},{1... | collective-permute-start | bytes 786440 | tf_op jit(solution)/shard_map/ppermute | solution.py:56
  130.5 0.7 copy-start.6
  135.7 4.7 %copy-start.2 = (bf16[128,2688]{1,0:T(8,128)(2,1)S(1)}, bf16[128,2688]{1,0:T(8,128)(2,1)}, u32[]{:S(2)}) copy-start(bf16[128,2688]{1,0:T(8,128)(2,1)} %copy-done.1) | copy-start | bytes 2064388
  135.8 18.8 %all-to-all-start.2 = ((bf16[8,256,256]{2,1,0:T(8,128)(2,1)}), bf16[8,256,256]{2,1,0:T(8,128)(2,1)S(1)}, u32[]{:S(2)}, u32[]{:S(2)}) async-start(bf16[8,256,256]{2,1,0:T(8,128)(2,1)} %attend.1), calls=%async_computation.2 | async-start | bytes 2097152 | tf_op jit(solution)/shard_map/all_to_all | solution.py:65
  154.5 1.0 copy-start
  155.5 17.1 %copy-start.7 = (s32[2]{0:T(128)S(1)}, s32[2]{0:T(128)}, u32[]{:S(2)}) copy-start(s32[2]{0:T(128)} %param.15) | copy-start | bytes 28
  155.5 17.1 %copy-start.8 = (s32[2]{0:T(128)S(1)}, s32[2]{0:T(128)}, u32[]{:S(2)}) copy-start(s32[2]{0:T(128)} %param.14) | copy-start | bytes 28
  160.5 12.1 %all-to-all-start.3 = ((f32[16,8,256]{2,1,0:T(8,128)}), f32[16,8,256]{2,1,0:T(8,128)S(1)}, u32[]{:S(2)}, u32[]{:S(2)}) async-start(f32[16,8,256]{2,1,0:T(8,128)} %token_sums.1), calls=%async_computation.3 | async-start | bytes 262144 | tf_op jit(solution)/shard_map/all_to_all | solution.py:65
  173.5 24.8 %all-to-all-start.4 = ((f32[32,1,2]{2,1,0:T(1,128)}), f32[32,1,2]{2,1,0:T(1,128)S(1)}, u32[]{:S(2)}, u32[]{:S(2)}) async-start(f32[32,1,2]{2,1,0:T(1,128)} %broadcast_in_dim.45), calls=%async_computation.4 | async-start | bytes 32768 | tf_op jit(solution)/shard_map/all_to_all | solution.py:61
Sparse Core Ops, SparseCore 0:
  47.3 47.5 all-gather.2
  97.0 49.3 all-gather.4

commit v3 on v2

--- a/solution.py
+++ b/solution.py
@@ -65,13 +65,21 @@
     return lax.all_to_all(tiles, axes, 0, 0, tiled=True)
 
 
+def rms_rows(piece, gain):
+    wide = piece.astype(jnp.float32)
+    inverse = lax.rsqrt(jnp.mean(wide * wide, axis=1, keepdims=True) + NORM_EPS)
+    return (wide * inverse * gain).astype(jnp.bfloat16)
+
+
 def norm_kernel(order_ref, gain_ref, *refs):
+    out_ref = refs[3]
     for k in range(4):
-        wide = refs[k][...].astype(jnp.float32)
-        inverse = lax.rsqrt(jnp.mean(wide * wide, axis=1, keepdims=True) + NORM_EPS)
-        rows = wide.shape[0]
+        rows = refs[0].shape[0]
         at = pl.multiple_of(order_ref[k] * rows, rows)
-        refs[4][pl.ds(at, rows), :] = (wide * inverse * gain_ref[...]).astype(jnp.bfloat16)
+        if k < 3:
+            out_ref[pl.ds(at, rows), :] = rms_rows(refs[k][...], gain_ref[...])
+        else:
+            out_ref[pl.ds(at, rows), :] = jnp.zeros((rows, out_ref.shape[1]), jnp.bfloat16)
 
 
 def normed_rows(order, gain, pieces):
@@ -79,102 +87,145 @@
     vmem = pl.BlockSpec(memory_space=pltpu.VMEM)
     return pl.pallas_call(
         norm_kernel,
-        in_specs=[pl.BlockSpec(memory_space=pltpu.SMEM)] + [vmem] * 5,
+        in_specs=[pl.BlockSpec(memory_space=pltpu.SMEM)] + [vmem] * 4,
         out_specs=vmem,
         out_shape=jax.ShapeDtypeStruct((4 * rows, width), jnp.bfloat16),
         name="norm",
     )(order, gain, *pieces)
 
 
-def project_kernel(turned_heads, rows_ref, w_ref, gain_ref, cos_ref, sin_ref, out_ref):
+def project_kernel(turns, order_ref, rows_ref, last_ref, in_gain_ref, w_ref, *refs):
+    gain_ref, cos_ref, sin_ref = refs[:3]
+    outs, normed_ref = refs[3:-1], refs[-1]
+    j = pl.program_id(0)
+    rows = last_ref.shape[0]
+    at = pl.multiple_of(order_ref[3] * rows, rows)
+
+    @pl.when(j == 0)
+    def _():
+        normed_ref[...] = rms_rows(last_ref[...], in_gain_ref[...])
+
     acc = jnp.dot(rows_ref[...], w_ref[...], preferred_element_type=jnp.float32)
-
-    def turn():
-        unit = acc * lax.rsqrt(jnp.mean(acc * acc, axis=1, keepdims=True) + NORM_EPS)
+    last = jnp.dot(normed_ref[...], w_ref[...], preferred_element_type=jnp.float32)
+
+    def turned(tile, cos, sin):
+        unit = tile * lax.rsqrt(jnp.mean(tile * tile, axis=1, keepdims=True) + NORM_EPS)
         unit = unit * gain_ref[...]
-        other = pltpu.roll(unit, HD // 2, 1)
-        out_ref[...] = (unit * cos_ref[...] + other * sin_ref[...]).astype(jnp.bfloat16)
-
-    if turned_heads == 2:
-        turn()
+        return unit * cos + pltpu.roll(unit, HD // 2, 1) * sin
+
+    def store(out_ref, turn):
+        if turn:
+            out_ref[...] = turned(acc, cos_ref[...], sin_ref[...]).astype(jnp.bfloat16)
+            there = turned(last, cos_ref[pl.ds(at, rows), :], sin_ref[pl.ds(at, rows), :])
+        else:
+            out_ref[...] = acc.astype(jnp.bfloat16)
+            there = last
+        out_ref[pl.ds(at, rows), :] = there.astype(jnp.bfloat16)
+
+    if len(outs) == 1:
+        store(outs[0], True)
     else:
-        pl.when(pl.program_id(0) == 0)(turn)
-
-        @pl.when(pl.program_id(0) == 1)
-        def _():
-            out_ref[...] = acc.astype(jnp.bfloat16)
-
-
-def project(normed, weights, gain, cos, sin, first, turned_heads):
+        for k in range(2):
+            pl.when(j == k)(lambda k=k: store(outs[k], turns[k]))
+
+
+def project(order, normed, last, in_gain, weights, gain, cos, sin, first, turns):
     rows, width = normed.shape
     vmem = pl.BlockSpec(memory_space=pltpu.VMEM)
+    if turns[1]:
+        out_specs = [pl.BlockSpec((rows, HD), lambda j: (0, j))]
+        out_shape = [jax.ShapeDtypeStruct((rows, 2 * HD), jnp.bfloat16)]
+    else:
+        out_specs = [pl.BlockSpec((rows, HD), lambda j: (0, 0))] * 2
+        out_shape = [jax.ShapeDtypeStruct((rows, HD), jnp.bfloat16)] * 2
     return pl.pallas_call(
-        lambda *refs: project_kernel(turned_heads, *refs),
+        lambda *refs: project_kernel(turns, *refs),
         grid=(2,),
         in_specs=[
+            pl.BlockSpec(memory_space=pltpu.SMEM),
+            vmem,
+            vmem,
             vmem,
             pl.BlockSpec((width, HD), lambda j: (0, j + first)),
             vmem,
             vmem,
             vmem,
         ],
-        out_specs=pl.BlockSpec((rows, HD), lambda j: (0, j)),
-        out_shape=jax.ShapeDtypeStruct((rows, 2 * HD), jnp.bfloat16),
+        out_specs=out_specs,
+        out_shape=out_shape,
+        scratch_shapes=[pltpu.VMEM(last.shape, jnp.bfloat16)],
         name="project",
-    )(normed, weights, gain, cos, sin)
-
-
-def attend_kernel(block_ref, q_ref, own_ref, back1_ref, back2_ref, out_ref):
-    held = (back2_ref, back1_ref, own_ref)
+    )(order, normed, last, in_gain, weights, gain, cos, sin)
+
+
+def part_of(ref, i, rows):
+    return ref[i * rows : (i + 1) * rows, :]
+
+
+def scores_of(q, k, place, block, query, key):
+    s = lax.dot_general(q, k, NT, preferred_element_type=jnp.float32)
+    a, i = place
+    if i - a == 4:
+        return jnp.where(key <= query, s, -1e30)
+    if i >= 4:
+        return s
+    there = 2 * block + (i - 4) >= 0
+    if i == a:
+        return jnp.where((key > query) & there, s, -1e30)
+    return jnp.where(there, s, -1e30)
+
+
+def row_max(scores):
+    top = jnp.max(scores[0], axis=1, keepdims=True)
+    for s in scores[1:]:
+        top = jnp.maximum(top, jnp.max(s, axis=1, keepdims=True))
+    return top
+
+
+def attend_kernel(block_ref, q_ref, *refs):
+    keys, vals, out_ref = refs[2::-1], refs[5:2:-1], refs[6]
     rows = q_ref.shape[0] // 2
-    block = block_ref[0]
     query = lax.broadcasted_iota(jnp.int32, (rows, rows), 0)
     key = lax.broadcasted_iota(jnp.int32, (rows, rows), 1)
     for a in range(2):
-        pieces = [
-            held[i // 2][(i % 2) * rows : (i % 2 + 1) * rows, :] for i in range(a, a + 5)
-        ]
+        at = slice(a * rows, (a + 1) * rows)
+        pieces = range(a, a + 5)
         for g in range(GROUP):
-            q = q_ref[a * rows : (a + 1) * rows, g * HD : (g + 1) * HD]
-            scores = []
-            for k, piece in enumerate(pieces):
-                s = lax.dot_general(q, piece[:, :HD], NT, preferred_element_type=jnp.float32)
-                there = 2 * block + (a + k - 4) >= 0
-                if k == 4:
-                    s = jnp.where(key <= query, s, -1e30)
-                elif k == 0:
-                    s = jnp.where((key > query) & there, s, -1e30)
-                elif a + k < 4:
-                    s = jnp.where(there, s, -1e30)
-                scores.append(s)
-            top = jnp.max(scores[0], axis=1, keepdims=True)
-            for s in scores[1:]:
-                top = jnp.maximum(top, jnp.max(s, axis=1, keepdims=True))
-            total, mixed = 0.0, 0.0
-            for s, piece in zip(scores, pieces):
-                e = jnp.exp(s - top)
-                total = total + jnp.sum(e, axis=1, keepdims=True)
-                mixed = mixed + jnp.dot(
-                    e.astype(jnp.bfloat16), piece[:, HD:], preferred_element_type=jnp.float32
+            wide = slice(g * HD, (g + 1) * HD)
+            q = q_ref[at, wide]
+            scores = [
+                scores_of(q, part_of(keys[i // 2], i % 2, rows), (a, i), block_ref[0], query, key)
+                for i in pieces
+            ]
+            top = row_max(scores)
+            terms = [jnp.exp(s - top) for s in scores]
+            total = sum(jnp.sum(e, axis=1, keepdims=True) for e in terms)
+            share = 1.0 / total
+            mixed = sum(
+                jnp.dot(
+                    (e * share).astype(jnp.bfloat16),
+                    part_of(vals[i // 2], i % 2, rows),
+                    preferred_element_type=jnp.float32,
                 )
-            mixed = (mixed / total).astype(jnp.bfloat16)
+                for e, i in zip(terms, pieces)
+            ).astype(jnp.bfloat16)
             for x in range(4):
-                out_ref[2 * x + a, :, g * HD : (g + 1) * HD] = mixed
-
-
-def attend(block, q, held):
+                out_ref[2 * x + a, :, wide] = mixed
+
+
+def attend(block, q, keys, vals):
     rows, wide = q.shape
     vmem = pl.BlockSpec(memory_space=pltpu.VMEM)
     return pl.pallas_call(
         attend_kernel,
-        in_specs=[pl.BlockSpec(memory_space=pltpu.SMEM)] + [vmem] * 4,
+        in_specs=[pl.BlockSpec(memory_space=pltpu.SMEM)] + [vmem] * 7,
         out_specs=vmem,
         out_shape=jax.ShapeDtypeStruct((8, rows // 2, wide), jnp.bfloat16),
         name="attend",
-    )(block, q, *held)
-
-
-def sums_kernel(mixed_ref, w_ref, gains_ref, h_ref, out_ref, sums_ref):
+    )(block, q, *keys, *vals)
+
+
+def sums_kernel(mixed_ref, w_ref, gains_ref, h_ref, branch_ref, out_ref, sums_ref):
     o = pl.program_id(0)
 
     @pl.when(o == 0)
@@ -191,21 +242,10 @@
             NT,
             preferred_element_type=jnp.float32,
         )
-    gains = gains_ref[0]
-    post, final, head = gains[:, 0:1], gains[:, 1:2], gains[:, 2:3]
-    read = final * head
+    branch_ref[0] = branch
     hidden = h_ref[0].astype(jnp.float32)
-    scaled = branch * post
-    for k, term in enumerate(
-        (
-            branch * branch,
-            scaled * scaled,
-            hidden * scaled,
-            scaled * read,
-            hidden * read,
-            hidden * hidden,
-        )
-    ):
+    scaled = branch * gains_ref[0, :, 0:1]
+    for k, term in enumerate((branch * branch, scaled * scaled, hidden * scaled, hidden * hidden)):
         sums_ref[k : k + 1, :] += jnp.sum(term, axis=0, keepdims=True)
 
     @pl.when(o == pl.num_programs(0) - 1)
@@ -226,11 +266,47 @@
             pl.BlockSpec((1, depth, 3), lambda o: (o, 0, 0)),
             pl.BlockSpec((1, depth, rows), lambda o: (o, 0, 0)),
         ],
-        out_specs=pl.BlockSpec((copies, 8, rows), lambda o: (0, 0, 0)),
-        out_shape=jax.ShapeDtypeStruct((copies, 8, rows), jnp.float32),
+        out_specs=[
+            pl.BlockSpec((1, depth, rows), lambda o: (o, 0, 0)),
+            pl.BlockSpec((copies, 8, rows), lambda o: (0, 0, 0)),
+        ],
+        out_shape=[
+            jax.ShapeDtypeStruct((parts, depth, rows), jnp.float32),
+            jax.ShapeDtypeStruct((copies, 8, rows), jnp.float32),
+        ],
         scratch_shapes=[pltpu.VMEM((8, rows), jnp.float32)],
         name="token_sums",
     )(mixed, weights, gains, h_share)
+
+
+def values_kernel(sums_ref, branch_ref, gains_ref, h_ref, out_ref):
+    sums = sum(sums_ref[x] for x in range(sums_ref.shape[0]))
+    branch_sq, scaled_sq, cross, hidden_sq = (sums[k : k + 1] for k in range(4))
+    parts, depth, _ = h_ref.shape
+    width = 4 * parts * depth
+    scale = lax.rsqrt(branch_sq / width + NORM_EPS)
+    residual_sq = hidden_sq + scale * (2.0 * cross + scale * scaled_sq)
+    last_scale = lax.rsqrt(jnp.maximum(residual_sq, 0.0) / width + NORM_EPS)
+    value = 0.0
+    for o in range(parts):
+        post, final, head = (gains_ref[o, :, k : k + 1] for k in range(3))
+        residual = h_ref[o].astype(jnp.float32) + branch_ref[o] * scale * post
+        residual = residual.astype(jnp.bfloat16).astype(jnp.float32)
+        last = (residual * last_scale * final).astype(jnp.bfloat16).astype(jnp.float32)
+        value = value + jnp.sum(last * head, axis=0, keepdims=True)
+    for k in range(out_ref.shape[0]):
+        out_ref[k] = value
+
+
+def partial_values(sums, branch, gains, h_share, copies):
+    vmem = pl.BlockSpec(memory_space=pltpu.VMEM)
+    return pl.pallas_call(
+        values_kernel,
+        in_specs=[vmem] * 4,
+        out_specs=vmem,
+        out_shape=jax.ShapeDtypeStruct((copies, 1, h_share.shape[2]), jnp.float32),
+        name="partial_values",
+    )(sums, branch, gains, h_share)
 
 
 def local(
@@ -294,7 +370,8 @@
 
     mine = lax.dynamic_index_in_dim(hidden, lax.axis_index("core"), 0, keepdims=False)
     near = moved(mine, beside(0, 1))
-    far = moved(mine, beside(1, 0)), moved(mine, beside(1, 1))
+    far = [moved(mine, beside(1, 0))]
+    far.append(moved(mine, beside(1, 1)))
     pieces = (mine, near, *far)
     order = jnp.stack(
         [
@@ -304,7 +381,7 @@
             2 - 2 * parity + 1 - half,
         ]
     )
-    normed = normed_rows(order, in_full, pieces)
+    normed = normed_rows(order, in_full, pieces[:3])
     h_share = jnp.concatenate(
         [jnp.where(half == 0, mine, near), jnp.where(half == 0, near, mine)], axis=0
     )
@@ -318,21 +395,19 @@
     cos = jnp.concatenate([cos, cos], axis=1)
     sin = jnp.concatenate([-sin, sin], axis=1)
 
-    held = [project(normed, weights, key_gain[None], cos, sin, 2, 1)]
+    shared = (order, normed, pieces[3], in_full, weights)
+    key, val = project(*shared, key_gain[None], cos, sin, 2, (True, False))
+    keys, vals = [key], [val]
     for _ in range(2):
-        held.append(moved(held[-1], block_before))
-    q = project(normed, weights, (query_gain * QUERY_SCALE)[None], cos, sin, 0, 2)
-    mixed = exchanged(attend(block[None], q, held), OCTANT)
-
-    sums = exchanged(token_sums(mixed, out_weights, out_gains, h_share, 16), OCTANT + ("core",))
-    sums = sums.reshape(4, 2, 2, 8, rows).sum(axis=0)
-    branch_sq, scaled_sq, cross, read_branch, read_hidden, hidden_sq = (
-        sums[:, :, k] for k in range(6)
-    )
-    scale = lax.rsqrt(branch_sq / width + NORM_EPS)
-    residual_sq = hidden_sq + scale * (2.0 * cross + scale * scaled_sq)
-    residual_sq = jnp.maximum(residual_sq, 0.0)
-    values = (read_hidden + scale * read_branch) * lax.rsqrt(residual_sq / width + NORM_EPS)
+        keys.append(moved(keys[-1], block_before))
+        vals.append(moved(vals[-1], block_before))
+    (q,) = project(*shared, (query_gain * QUERY_SCALE)[None], cos, sin, 0, (True, True))
+    mixed = exchanged(attend(block[None], q, keys, vals), OCTANT)
+
+    branch, sums = token_sums(mixed, out_weights, out_gains, h_share, 4)
+    sums = exchanged(sums, ("xh", "xl"))
+    values = partial_values(sums, branch, out_gains, h_share, 16)
+    values = exchanged(values, OCTANT + ("core",)).reshape(4, 2, 2, rows).sum(axis=0)
     pos = pos.reshape(2, 1, rows)
     values = jnp.where(pos < lengths[None, :, None], values, 0.0)
     reward = jnp.sum(jnp.where(pos == reward_pos[None, :, None], values, 0.0), axis=(0, 2))

time: 206 us -> 214 us (1.039)
  waiting for transfers between devices: 58.7 us -> 43.2 us
  blocking collectives: 21.4 us -> 29.8 us
  starting transfers between devices: 70.5 us -> 77.9 us
  Pallas kernels: 24.2 us -> 29.3 us
    ppermute x7 -> x9, waiting for transfers between devices: 19.4 us -> 5.97 us  [moved(): return lax.ppermute(array, AXES, pairs_of(source_of))]
    ppermute x7 -> x9, starting transfers between devices: 28 us -> 40.2 us  [moved(): return lax.ppermute(array, AXES, pairs_of(source_of))]
    all_to_all x1 -> x2, blocking collectives: 21.4 us -> 29.8 us  [exchanged(): return lax.all_to_all(tiles, axes, 0, 0, tiled=True)]
    all_to_all x2, starting transfers between devices: 31.9 us -> 26.5 us  [told_to_all(): lax.all_to_all(jnp.broadcast_to(array[None], (n, *array.shape)), axes, 0,...]
    pallas_call x2 -> x3, Pallas kernels: 9.81 us -> 14.7 us  [the longest x2 12.4 us: project(): pl.pallas_call(lambda *refs: project_kernel(turns, *refs), grid=(2,), in_...]
    all_gather x1, waiting for transfers between devices: 3.72 us -> 0.01 us  [local(): lax.all_gather(octet[:, 4 * HD:], ('z', 'core'), axis=0, tiled=True)]
    all_to_all x2, waiting for transfers between devices: 14.4 us -> 16.5 us  [exchanged(): return lax.all_to_all(tiles, axes, 0, 0, tiled=True)]
  transfers between devices with their start and end apart: 13 -> 15, of which waited for: 9 -> 6; matrix products, arithmetic and copies ran while one was open for 5% -> 5% of each run, Pallas kernels for 9% -> 10%
where the time goes in v3:
time: 214 us; the launch traced here: 213 us
  starting transfers between devices  77.9 us (36%)
  waiting for transfers between devices  43.2 us (20%)
  blocking collectives  29.8 us (14%)
  Pallas kernels  29.3 us (14%)
  between operations  14.4 us (7%)
  local copies, waits for them, and re-layouts  12.2 us (6%)
  other arithmetic  5.97 us (3%)
    ppermute x9, starting transfers between devices, moved(): return lax.ppermute(array, AXES, pairs_of(source_of))  40.2 us
    all_to_all x2, blocking collectives, exchanged(): return lax.all_to_all(tiles, axes, 0, 0, tiled=True)  29.8 us
    all_to_all x2, starting transfers between devices, told_to_all(): lax.all_to_all(jnp.broadcast_to(array[None], (n, *array.shape)), axes, 0,...  26.5 us
    all_to_all x2, waiting for transfers between devices, told_to_all(): lax.all_to_all(jnp.broadcast_to(array[None], (n, *array.shape)), axes, 0,...  17.2 us
    all_to_all x2, waiting for transfers between devices, exchanged(): return lax.all_to_all(tiles, axes, 0, 0, tiled=True)  16.5 us
    pallas_call x2, Pallas kernels, project(): pl.pallas_call(lambda *refs: project_kernel(turns, *refs), grid=(2,), in_...  12.4 us
    all_to_all x2, starting transfers between devices, exchanged(): return lax.all_to_all(tiles, axes, 0, 0, tiled=True)  11.1 us
    ppermute x9, waiting for transfers between devices, moved(): return lax.ppermute(array, AXES, pairs_of(source_of))  5.97 us
  transfers between devices with their start and end apart: 15, of which 6 were waited for; matrix products, arithmetic and copies ran while one was open for 5% of the time, Pallas kernels for 10%

profile of v3, /device:TPU:1, one launch (start us, length us, event | category | flops | bytes accessed | tf_op | source)
XLA Modules:
  0.0 212.8 jit_solution(11130954295312830850)
XLA Ops:
  9.4 4.5 %collective-permute-start = (bf16[2,22,512]{2,1,0:T(8,128)(2,1)S(1)}, bf16[2,22,512]{2,1,0:T(8,128)(2,1)S(1)}, u32[]{:S(2)}, u32[]{:S(2)}) collective-permute-start(bf16[2,22,512]{2,1,0:T(8,128)(2,1)S(1)} %pad_maximum_fusion.3), channel_id=1, source_target_pairs={{0,0},{128,1},{1,2},{129,3},{2,4},{130,5},{3,6},{131,7},{4,8},{132... | collective-permute-start | bytes 135176 | tf_op jit(solution)/shard_map/ppermute | solution.py:56
  15.4 3.3 %collective-permute-start.1 = (bf16[22,512]{1,0:T(8,128)(2,1)S(1)}, bf16[22,512]{1,0:T(8,128)(2,1)S(1)}, u32[]{:S(2)}, u32[]{:S(2)}) collective-permute-start(bf16[22,512]{1,0:T(8,128)(2,1)S(1)} %pad_maximum_fusion.6), channel_id=1, source_target_pairs={{0,0},{32,1},{1,2},{33,3},{2,4},{34,5},{3,6},{35,7},{4,8},{36,9},{... | collective-permute-start | bytes 67592 | tf_op jit(solution)/shard_map/ppermute | solution.py:56
  18.8 5.9 %collective-permute-done.1 = bf16[22,512]{1,0:T(8,128)(2,1)S(1)} collective-permute-done((bf16[22,512]{1,0:T(8,128)(2,1)S(1)}, bf16[22,512]{1,0:T(8,128)(2,1)S(1)}, u32[]{:S(2)}, u32[]{:S(2)}) %collective-permute-start.1) | collective-permute-done | bytes 22560 | tf_op jit(solution)/shard_map/ppermute | solution.py:56
  24.8 21.4 %all_to_all.31 = bf16[8,22,1024]{2,1,0:T(8,128)(2,1)S(1)} all-to-all(bf16[8,22,1024]{2,1,0:T(8,128)(2,1)S(1)} %pad_maximum_fusion), channel_id=1, replica_groups=mesh['xh'=2,'core'=2,'z'=8,'yy'=4,'p'=2,'xl'=2] {'yy','p'}, dimensions={0} | all-to-all | bytes 720896 | tf_op jit(solution)/shard_map/all_to_all | solution.py:65
  52.6 3.8 %collective-permute-start.4 = (bf16[128,2688]{1,0:T(8,128)(2,1)S(1)}, bf16[128,2688]{1,0:T(8,128)(2,1)S(1)}, u32[]{:S(2)}, u32[]{:S(2)}) collective-permute-start(bf16[128,2688]{1,0:T(8,128)(2,1)S(1)} %dynamic-slice_bitcast_fusion.refs_0_), channel_id=1, source_target_pairs={{3,0},{2,1},{1,2},{0,3},{7,4},{6,5},{5,6},{4,7},{11,8},{10,9},{9,1... | collective-permute-start | bytes 2064392 | tf_op jit(solution)/shard_map/ppermute | solution.py:56
  59.5 18.2 %all-to-all-start.1 = ((bf16[16,4,256]{2,1,0:T(4,128)(2,1)}), bf16[16,4,256]{2,1,0:T(4,128)(2,1)S(1)}, u32[]{:S(2)}, u32[]{:S(2)}) async-start(bf16[16,4,256]{2,1,0:T(4,128)(2,1)} %broadcast_in_dim.44), calls=%async_computation.1 | async-start | bytes 65536 | tf_op jit(solution)/shard_map/all_to_all | solution.py:61
  78.4 6.8 %all-to-all-done.1 = bf16[16,4,256]{2,1,0:T(4,128)(2,1)S(1)} async-done(((bf16[16,4,256]{2,1,0:T(4,128)(2,1)}), bf16[16,4,256]{2,1,0:T(4,128)(2,1)S(1)}, u32[]{:S(2)}, u32[]{:S(2)}) %all-to-all-start.1) | async-done | bytes 32800 | tf_op jit(solution)/shard_map/all_to_all | solution.py:61
  87.7 4.2 %norm.1.refs_1_ = bf16[512,2688]{1,0:T(8,128)(2,1)} custom-call(s32[4]{0:T(128)} %pad_add_fusion.order_ref.refs_0_, f32[1,2688]{1,0:T(1,128)} %reshape_squeeze.3.gain_ref.refs_3_, bf16[128,2688]{1,0:T(8,128)(2,1)} %copy-done.3, bf16[128,2688]{1,0:T(8,128)(2,1)} %copy-done.1, bf16[128,2688]{1,0:T(8,128)(2,1)} %copy-done.7), custom_call_target="tpu_custom_call" | custom-call | tf_op jit(solution)/shard_map/norm/pallas_call | solution.py:88
  91.9 2.8 %all-gather.3.cloned.1.call-done.refs_4_ = bf16[2688,512]{1,0:T(8,128)(2,1)} async-done(((bf16[168,512]{1,0:T(8,128)(2,1)}), bf16[2688,512]{1,0:T(8,128)(2,1)}) %all-gather.3.cloned.1.call-update) | async-done | bytes 2752528 | tf_op jit(solution)/shard_map/all_gather | solution.py:363
  94.8 5.9 %project.3 = (bf16[512,128]{1,0:T(8,128)(2,1)}, bf16[512,128]{1,0:T(8,128)(2,1)}) custom-call(s32[4]{0:T(128)} %pad_add_fusion.order_ref.refs_0_, bf16[512,2688]{1,0:T(8,128)(2,1)} %norm.1.refs_1_, bf16[128,2688]{1,0:T(8,128)(2,1)} %copy-done.4, f32[1,2688]{1,0:T(1,128)} %reshape_squeeze.3.gain_ref.refs_3_, ...), custom_call_target="tpu_custom_call" | custom-call | tf_op jit(solution)/shard_map/project/pallas_call | solution.py:141
  100.7 3.9 %collective-permute-start.5 = (bf16[512,128]{1,0:T(8,128)(2,1)}, bf16[512,128]{1,0:T(8,128)(2,1)S(1)}, u32[]{:S(2)}, u32[]{:S(2)}) collective-permute-start(bf16[512,128]{1,0:T(8,128)(2,1)} %get-tuple-element.6.refs_0_), channel_id=1, source_target_pairs={{0,4},{1,5},{2,6},{3,7},{4,8},{5,9},{6,10},{7,11},{8,12},{9,13},{1... | collective-permute-start | bytes 393224 | tf_op jit(solution)/shard_map/ppermute | solution.py:56
  104.6 5.6 %collective-permute-start.7 = (bf16[512,128]{1,0:T(8,128)(2,1)}, bf16[512,128]{1,0:T(8,128)(2,1)S(1)}, u32[]{:S(2)}, u32[]{:S(2)}) collective-permute-start(bf16[512,128]{1,0:T(8,128)(2,1)} %get-tuple-element.7.refs_3_), channel_id=1, source_target_pairs={{0,4},{1,5},{2,6},{3,7},{4,8},{5,9},{6,10},{7,11},{8,12},{9,13},{1... | collective-permute-start | bytes 393224 | tf_op jit(solution)/shard_map/ppermute | solution.py:56
  110.3 8.3 %collective-permute-start.6 = (bf16[512,128]{1,0:T(8,128)(2,1)S(1)}, bf16[512,128]{1,0:T(8,128)(2,1)S(1)}, u32[]{:S(2)}, u32[]{:S(2)}) collective-permute-start(bf16[512,128]{1,0:T(8,128)(2,1)S(1)} %collective-permute-done.5.refs_1_), channel_id=1, source_target_pairs={{0,4},{1,5},{2,6},{3,7},{4,8},{5,9},{6,10},{7,11},{8,12},{9,13},{1... | collective-permute-start | bytes 393224 | tf_op jit(solution)/shard_map/ppermute | solution.py:56
  118.6 6.1 %collective-permute-start.8 = (bf16[512,128]{1,0:T(8,128)(2,1)S(1)}, bf16[512,128]{1,0:T(8,128)(2,1)S(1)}, u32[]{:S(2)}, u32[]{:S(2)}) collective-permute-start(bf16[512,128]{1,0:T(8,128)(2,1)S(1)} %collective-permute-done.7.refs_4_), channel_id=1, source_target_pairs={{0,4},{1,5},{2,6},{3,7},{4,8},{5,9},{6,10},{7,11},{8,12},{9,13},{1... | collective-permute-start | bytes 393224 | tf_op jit(solution)/shard_map/ppermute | solution.py:56
  125.2 6.5 %project.2.q_ref = bf16[512,256]{1,0:T(8,128)(2,1)} custom-call(s32[4]{0:T(128)} %pad_add_fusion.order_ref.refs_0_, bf16[512,2688]{1,0:T(8,128)(2,1)} %norm.1.refs_1_, bf16[128,2688]{1,0:T(8,128)(2,1)} %copy-done.4, f32[1,2688]{1,0:T(1,128)} %reshape_squeeze.3.gain_ref.refs_3_, bf16[2688,512]{1,0:T(8,128)(2,1)} %all-gather.3.cloned.1.call-done.refs_4_, ...), custom_call_target="tpu_custom_call" | custom-call | tf_op jit(solution)/shard_map/project/pallas_call | solution.py:141
  132.4 5.3 %attend.1 = bf16[8,256,256]{2,1,0:T(8,128)(2,1)} custom-call(s32[1]{0:T(128)} %bitcast.block_ref, bf16[512,256]{1,0:T(8,128)(2,1)} %project.2.q_ref, bf16[512,128]{1,0:T(8,128)(2,1)} %get-tuple-element.6.refs_0_, bf16[512,128]{1,0:T(8,128)(2,1)} %copy-done.9, bf16[512,128]{1,0:T(8,128)(2,1)} %copy-done.11, bf16[512,128]{1,0:T(8,128)(2,1)} %get-tuple-element.7.refs_3_, ...), custom_call_target="tpu_custom_call" | custom-call | tf_op jit(solution)/shard_map/attend/pallas_call | solution.py:219
  137.7 3.9 %all-to-all-start.2 = ((bf16[8,256,256]{2,1,0:T(8,128)(2,1)}), bf16[8,256,256]{2,1,0:T(8,128)(2,1)S(1)}, u32[]{:S(2)}, u32[]{:S(2)}) async-start(bf16[8,256,256]{2,1,0:T(8,128)(2,1)} %attend.1), calls=%async_computation.2 | async-start | bytes 2097152 | tf_op jit(solution)/shard_map/all_to_all | solution.py:65
  144.6 10.7 %all-to-all-done.2.mixed_ref = bf16[8,256,256]{2,1,0:T(8,128)(2,1)S(1)} async-done(((bf16[8,256,256]{2,1,0:T(8,128)(2,1)}), bf16[8,256,256]{2,1,0:T(8,128)(2,1)S(1)}, u32[]{:S(2)}, u32[]{:S(2)}) %all-to-all-start.2) | async-done | bytes 1048608 | tf_op jit(solution)/shard_map/all_to_all | solution.py:65
  156.3 5.0 %token_sums.1 = (f32[4,168,256]{2,1,0:T(8,128)}, f32[4,8,256]{2,1,0:T(8,128)}) custom-call(bf16[8,256,256]{2,1,0:T(8,128)(2,1)} %copy-done, bf16[4,4,168,512]{3,2,1,0:T(8,128)(2,1)} %bitcast.30, f32[4,168,3]{2,1,0:T(8,128)} %bitcast.28, bf16[4,168,256]{2,1,0:T(8,128)(2,1)} %bitcast.26), custom_call_target="tpu_custom_call" | custom-call | tf_op jit(solution)/shard_map/token_sums/pallas_call | solution.py:260
  161.3 8.4 %all_to_all.32.sums_ref = f32[4,8,256]{2,1,0:T(8,128)} all-to-all(f32[4,8,256]{2,1,0:T(8,128)} %get-tuple-element.8), channel_id=1, replica_groups=mesh['xh'=2,'core'=2,'z'=8,'yy'=4,'p'=2,'xl'=2] {'xh','xl'}, dimensions={0} | all-to-all | bytes 65536 | tf_op jit(solution)/shard_map/all_to_all | solution.py:65
  172.0 7.2 %all-to-all-start.4 = ((f32[16,1,256]{2,1,0:T(1,128)}), f32[16,1,256]{2,1,0:T(1,128)S(1)}, u32[]{:S(2)}, u32[]{:S(2)}) async-start(f32[16,1,256]{2,1,0:T(1,128)} %partial_values.1), calls=%async_computation.4 | async-start | bytes 32768 | tf_op jit(solution)/shard_map/all_to_all | solution.py:65
  179.3 5.8 %all-to-all-done.4 = f32[16,1,256]{2,1,0:T(1,128)S(1)} async-done(((f32[16,1,256]{2,1,0:T(1,128)}), f32[16,1,256]{2,1,0:T(1,128)S(1)}, u32[]{:S(2)}, u32[]{:S(2)}) %all-to-all-start.4) | async-done | bytes 16416 | tf_op jit(solution)/shard_map/all_to_all | solution.py:65
  186.0 8.4 %all-to-all-start.5 = ((f32[32,1,2]{2,1,0:T(1,128)}), f32[32,1,2]{2,1,0:T(1,128)S(1)}, u32[]{:S(2)}, u32[]{:S(2)}) async-start(f32[32,1,2]{2,1,0:T(1,128)} %broadcast_in_dim.48), calls=%async_computation.5 | async-start | bytes 32768 | tf_op jit(solution)/shard_map/all_to_all | solution.py:61
  195.0 10.4 %all-to-all-done.5 = f32[32,1,2]{2,1,0:T(1,128)S(1)} async-done(((f32[32,1,2]{2,1,0:T(1,128)}), f32[32,1,2]{2,1,0:T(1,128)S(1)}, u32[]{:S(2)}, u32[]{:S(2)}) %all-to-all-start.5) | async-done | bytes 288 | tf_op jit(solution)/shard_map/all_to_all | solution.py:61
  (92 shorter events, 26.0 us)
Async XLA Ops:
  7.2 87.6 %all-gather.3.cloned.1.call-start = ((), (), s32[]{:S(2)}) async-start(), calls=%async_computation.6 | async-start | bytes 2924544 | tf_op jit(solution)/shard_map/all_gather | solution.py:363
  9.4 15.3 %collective-permute-start = (bf16[2,22,512]{2,1,0:T(8,128)(2,1)S(1)}, bf16[2,22,512]{2,1,0:T(8,128)(2,1)S(1)}, u32[]{:S(2)}, u32[]{:S(2)}) collective-permute-start(bf16[2,22,512]{2,1,0:T(8,128)(2,1)S(1)} %pad_maximum_fusion.3), channel_id=1, source_target_pairs={{0,0},{128,1},{1,2},{129,3},{2,4},{130,5},{3,6},{131,7},{4,8},{132... | collective-permute-start | bytes 135176 | tf_op jit(solution)/shard_map/ppermute | solution.py:56
  15.4 9.3 %collective-permute-start.1 = (bf16[22,512]{1,0:T(8,128)(2,1)S(1)}, bf16[22,512]{1,0:T(8,128)(2,1)S(1)}, u32[]{:S(2)}, u32[]{:S(2)}) collective-permute-start(bf16[22,512]{1,0:T(8,128)(2,1)S(1)} %pad_maximum_fusion.6), channel_id=1, source_target_pairs={{0,0},{32,1},{1,2},{33,3},{2,4},{34,5},{3,6},{35,7},{4,8},{36,9},{... | collective-permute-start | bytes 67592 | tf_op jit(solution)/shard_map/ppermute | solution.py:56
  24.8 23.1 %copy-start.5 = (bf16[2,128,2688]{2,1,0:T(8,128)(2,1)S(1)}, bf16[2,128,2688]{2,1,0:T(8,128)(2,1)}, u32[]{:S(2)}) copy-start(bf16[2,128,2688]{2,1,0:T(8,128)(2,1)} %param.13) | copy-start | bytes 4128772
  47.2 97.4 %all-gather.5.cloned.1.call-start = ((), (), s32[]{:S(2)}) async-start(), calls=%async_computation.7 | async-start | bytes 2924544 | tf_op jit(solution)/shard_map/all_gather | solution.py:364
  48.0 38.0 %copy-start.3 = (bf16[128,2688]{1,0:T(8,128)(2,1)}, bf16[128,2688]{1,0:T(8,128)(2,1)S(1)}, u32[]{:S(2)}) copy-start(bf16[128,2688]{1,0:T(8,128)(2,1)S(1)} %dynamic-slice_bitcast_fusion.refs_0_) | copy-start | bytes 2064388
  48.0 37.9 %collective-permute-start.2 = (bf16[128,2688]{1,0:T(8,128)(2,1)S(1)}, bf16[128,2688]{1,0:T(8,128)(2,1)S(1)}, u32[]{:S(2)}, u32[]{:S(2)}) collective-permute-start(bf16[128,2688]{1,0:T(8,128)(2,1)S(1)} %dynamic-slice_bitcast_fusion.refs_0_), channel_id=1, source_target_pairs={{1,0},{0,1},{3,2},{2,3},{5,4},{4,5},{7,6},{6,7},{9,8},{8,9},{11,10... | collective-permute-start | bytes 2064392 | tf_op jit(solution)/shard_map/ppermute | solution.py:56
  50.7 35.2 %collective-permute-start.3 = (bf16[128,2688]{1,0:T(8,128)(2,1)S(1)}, bf16[128,2688]{1,0:T(8,128)(2,1)S(1)}, u32[]{:S(2)}, u32[]{:S(2)}) collective-permute-start(bf16[128,2688]{1,0:T(8,128)(2,1)S(1)} %dynamic-slice_bitcast_fusion.refs_0_), channel_id=1, source_target_pairs={{2,0},{3,1},{0,2},{1,3},{6,4},{7,5},{4,6},{5,7},{10,8},{11,9},{8,1... | collective-permute-start | bytes 2064392 | tf_op jit(solution)/shard_map/ppermute | solution.py:56
  52.6 39.3 %collective-permute-start.4 = (bf16[128,2688]{1,0:T(8,128)(2,1)S(1)}, bf16[128,2688]{1,0:T(8,128)(2,1)S(1)}, u32[]{:S(2)}, u32[]{:S(2)}) collective-permute-start(bf16[128,2688]{1,0:T(8,128)(2,1)S(1)} %dynamic-slice_bitcast_fusion.refs_0_), channel_id=1, source_target_pairs={{3,0},{2,1},{1,2},{0,3},{7,4},{6,5},{5,6},{4,7},{11,8},{10,9},{9,1... | collective-permute-start | bytes 2064392 | tf_op jit(solution)/shard_map/ppermute | solution.py:56
  59.5 25.6 %all-to-all-start.1 = ((bf16[16,4,256]{2,1,0:T(4,128)(2,1)}), bf16[16,4,256]{2,1,0:T(4,128)(2,1)S(1)}, u32[]{:S(2)}, u32[]{:S(2)}) async-start(bf16[16,4,256]{2,1,0:T(4,128)(2,1)} %broadcast_in_dim.44), calls=%async_computation.1 | async-start | bytes 65536 | tf_op jit(solution)/shard_map/all_to_all | solution.py:61
  85.2 15.5 %copy-start.8 = (f32[16,4,168]{2,1,0:T(4,128)}, f32[16,4,168]{2,1,0:T(4,128)S(1)}, u32[]{:S(2)}) copy-start(f32[16,4,168]{2,1,0:T(4,128)S(1)} %slice_convert_fusion) | copy-start | bytes 129028
  94.7 30.0 %copy-start.15 = (f32[128]{0:T(128)S(1)}, f32[128]{0:T(128)}, u32[]{:S(2)}) copy-start(f32[128]{0:T(128)} %param.20) | copy-start | bytes 1540
  100.7 9.6 %collective-permute-start.5 = (bf16[512,128]{1,0:T(8,128)(2,1)}, bf16[512,128]{1,0:T(8,128)(2,1)S(1)}, u32[]{:S(2)}, u32[]{:S(2)}) collective-permute-start(bf16[512,128]{1,0:T(8,128)(2,1)} %get-tuple-element.6.refs_0_), channel_id=1, source_target_pairs={{0,4},{1,5},{2,6},{3,7},{4,8},{5,9},{6,10},{7,11},{8,12},{9,13},{1... | collective-permute-start | bytes 393224 | tf_op jit(solution)/shard_map/ppermute | solution.py:56
  104.6 14.0 %collective-permute-start.7 = (bf16[512,128]{1,0:T(8,128)(2,1)}, bf16[512,128]{1,0:T(8,128)(2,1)S(1)}, u32[]{:S(2)}, u32[]{:S(2)}) collective-permute-start(bf16[512,128]{1,0:T(8,128)(2,1)} %get-tuple-element.7.refs_3_), channel_id=1, source_target_pairs={{0,4},{1,5},{2,6},{3,7},{4,8},{5,9},{6,10},{7,11},{8,12},{9,13},{1... | collective-permute-start | bytes 393224 | tf_op jit(solution)/shard_map/ppermute | solution.py:56
  110.3 21.5 %copy-start.9 = (bf16[512,128]{1,0:T(8,128)(2,1)}, bf16[512,128]{1,0:T(8,128)(2,1)S(1)}, u32[]{:S(2)}) copy-start(bf16[512,128]{1,0:T(8,128)(2,1)S(1)} %collective-permute-done.5.refs_1_) | copy-start | bytes 393220
  110.3 21.5 %collective-permute-start.6 = (bf16[512,128]{1,0:T(8,128)(2,1)S(1)}, bf16[512,128]{1,0:T(8,128)(2,1)S(1)}, u32[]{:S(2)}, u32[]{:S(2)}) collective-permute-start(bf16[512,128]{1,0:T(8,128)(2,1)S(1)} %collective-permute-done.5.refs_1_), channel_id=1, source_target_pairs={{0,4},{1,5},{2,6},{3,7},{4,8},{5,9},{6,10},{7,11},{8,12},{9,13},{1... | collective-permute-start | bytes 393224 | tf_op jit(solution)/shard_map/ppermute | solution.py:56
  118.6 13.1 %copy-start.10 = (bf16[512,128]{1,0:T(8,128)(2,1)}, bf16[512,128]{1,0:T(8,128)(2,1)S(1)}, u32[]{:S(2)}) copy-start(bf16[512,128]{1,0:T(8,128)(2,1)S(1)} %collective-permute-done.7.refs_4_) | copy-start | bytes 393220
  118.6 13.2 %collective-permute-start.8 = (bf16[512,128]{1,0:T(8,128)(2,1)S(1)}, bf16[512,128]{1,0:T(8,128)(2,1)S(1)}, u32[]{:S(2)}, u32[]{:S(2)}) collective-permute-start(bf16[512,128]{1,0:T(8,128)(2,1)S(1)} %collective-permute-done.7.refs_4_), channel_id=1, source_target_pairs={{0,4},{1,5},{2,6},{3,7},{4,8},{5,9},{6,10},{7,11},{8,12},{9,13},{1... | collective-permute-start | bytes 393224 | tf_op jit(solution)/shard_map/ppermute | solution.py:56
  137.7 3.9 %copy-start.6 = (bf16[2,128,2688]{2,1,0:T(8,128)(2,1)S(1)}, bf16[2,128,2688]{2,1,0:T(8,128)(2,1)}, u32[]{:S(2)}) copy-start(bf16[2,128,2688]{2,1,0:T(8,128)(2,1)} %param.13) | copy-start | bytes 4128772
  137.7 17.6 %all-to-all-start.2 = ((bf16[8,256,256]{2,1,0:T(8,128)(2,1)}), bf16[8,256,256]{2,1,0:T(8,128)(2,1)S(1)}, u32[]{:S(2)}, u32[]{:S(2)}) async-start(bf16[8,256,256]{2,1,0:T(8,128)(2,1)} %attend.1), calls=%async_computation.2 | async-start | bytes 2097152 | tf_op jit(solution)/shard_map/all_to_all | solution.py:65
  161.3 23.8 %copy-start.13 = (s32[2]{0:T(128)S(1)}, s32[2]{0:T(128)}, u32[]{:S(2)}) copy-start(s32[2]{0:T(128)} %param.15) | copy-start | bytes 28
  161.3 23.8 %copy-start.14 = (s32[2]{0:T(128)S(1)}, s32[2]{0:T(128)}, u32[]{:S(2)}) copy-start(s32[2]{0:T(128)} %param.14) | copy-start | bytes 28
  172.0 13.0 %all-to-all-start.4 = ((f32[16,1,256]{2,1,0:T(1,128)}), f32[16,1,256]{2,1,0:T(1,128)S(1)}, u32[]{:S(2)}, u32[]{:S(2)}) async-start(f32[16,1,256]{2,1,0:T(1,128)} %partial_values.1), calls=%async_computation.4 | async-start | bytes 32768 | tf_op jit(solution)/shard_map/all_to_all | solution.py:65
  186.0 19.4 %all-to-all-start.5 = ((f32[32,1,2]{2,1,0:T(1,128)}), f32[32,1,2]{2,1,0:T(1,128)S(1)}, u32[]{:S(2)}, u32[]{:S(2)}) async-start(f32[32,1,2]{2,1,0:T(1,128)} %broadcast_in_dim.48), calls=%async_computation.5 | async-start | bytes 32768 | tf_op jit(solution)/shard_map/all_to_all | solution.py:61
  (7 other events, 10.8 us)
Sparse Core Ops, SparseCore 0:
  47.3 47.4 all-gather.2
  96.9 46.2 all-gather.4

commit v4 on v3

--- a/solution.py
+++ b/solution.py
@@ -225,7 +225,7 @@
     )(block, q, *keys, *vals)
 
 
-def sums_kernel(mixed_ref, w_ref, gains_ref, h_ref, branch_ref, out_ref, sums_ref):
+def sums_kernel(mixed_ref, w_ref, gains_ref, h_ref, out_ref, sums_ref):
     o = pl.program_id(0)
 
     @pl.when(o == 0)
@@ -242,10 +242,21 @@
             NT,
             preferred_element_type=jnp.float32,
         )
-    branch_ref[0] = branch
+    gains = gains_ref[0]
+    post, final, head = gains[:, 0:1], gains[:, 1:2], gains[:, 2:3]
+    read = final * head
     hidden = h_ref[0].astype(jnp.float32)
-    scaled = branch * gains_ref[0, :, 0:1]
-    for k, term in enumerate((branch * branch, scaled * scaled, hidden * scaled, hidden * hidden)):
+    scaled = branch * post
+    for k, term in enumerate(
+        (
+            branch * branch,
+            scaled * scaled,
+            hidden * scaled,
+            scaled * read,
+            hidden * read,
+            hidden * hidden,
+        )
+    ):
         sums_ref[k : k + 1, :] += jnp.sum(term, axis=0, keepdims=True)
 
     @pl.when(o == pl.num_programs(0) - 1)
@@ -266,47 +277,11 @@
             pl.BlockSpec((1, depth, 3), lambda o: (o, 0, 0)),
             pl.BlockSpec((1, depth, rows), lambda o: (o, 0, 0)),
         ],
-        out_specs=[
-            pl.BlockSpec((1, depth, rows), lambda o: (o, 0, 0)),
-            pl.BlockSpec((copies, 8, rows), lambda o: (0, 0, 0)),
-        ],
-        out_shape=[
-            jax.ShapeDtypeStruct((parts, depth, rows), jnp.float32),
-            jax.ShapeDtypeStruct((copies, 8, rows), jnp.float32),
-        ],
+        out_specs=pl.BlockSpec((copies, 8, rows), lambda o: (0, 0, 0)),
+        out_shape=jax.ShapeDtypeStruct((copies, 8, rows), jnp.float32),
         scratch_shapes=[pltpu.VMEM((8, rows), jnp.float32)],
         name="token_sums",
     )(mixed, weights, gains, h_share)
-
-
-def values_kernel(sums_ref, branch_ref, gains_ref, h_ref, out_ref):
-    sums = sum(sums_ref[x] for x in range(sums_ref.shape[0]))
-    branch_sq, scaled_sq, cross, hidden_sq = (sums[k : k + 1] for k in range(4))
-    parts, depth, _ = h_ref.shape
-    width = 4 * parts * depth
-    scale = lax.rsqrt(branch_sq / width + NORM_EPS)
-    residual_sq = hidden_sq + scale * (2.0 * cross + scale * scaled_sq)
-    last_scale = lax.rsqrt(jnp.maximum(residual_sq, 0.0) / width + NORM_EPS)
-    value = 0.0
-    for o in range(parts):
-        post, final, head = (gains_ref[o, :, k : k + 1] for k in range(3))
-        residual = h_ref[o].astype(jnp.float32) + branch_ref[o] * scale * post
-        residual = residual.astype(jnp.bfloat16).astype(jnp.float32)
-        last = (residual * last_scale * final).astype(jnp.bfloat16).astype(jnp.float32)
-        value = value + jnp.sum(last * head, axis=0, keepdims=True)
-    for k in range(out_ref.shape[0]):
-        out_ref[k] = value
-
-
-def partial_values(sums, branch, gains, h_share, copies):
-    vmem = pl.BlockSpec(memory_space=pltpu.VMEM)
-    return pl.pallas_call(
-        values_kernel,
-        in_specs=[vmem] * 4,
-        out_specs=vmem,
-        out_shape=jax.ShapeDtypeStruct((copies, 1, h_share.shape[2]), jnp.float32),
-        name="partial_values",
-    )(sums, branch, gains, h_share)
 
 
 def local(
@@ -389,7 +364,7 @@
     h_share = h_share.T.reshape(4, octet_rows, rows)
 
     pos = block * 2 * rows + jnp.arange(2 * rows, dtype=jnp.int32)
-    frequency = ROPE_BASE ** (-jnp.arange(HD // 2, dtype=jnp.float32) * 2.0 / HD)
+    frequency = (ROPE_BASE ** (-np.arange(HD // 2) * 2.0 / HD)).astype(np.float32)
     angles = pos.astype(jnp.float32)[:, None] * frequency[None, :]
     cos, sin = jnp.cos(angles), jnp.sin(angles)
     cos = jnp.concatenate([cos, cos], axis=1)
@@ -404,10 +379,15 @@
     (q,) = project(*shared, (query_gain * QUERY_SCALE)[None], cos, sin, 0, (True, True))
     mixed = exchanged(attend(block[None], q, keys, vals), OCTANT)
 
-    branch, sums = token_sums(mixed, out_weights, out_gains, h_share, 4)
-    sums = exchanged(sums, ("xh", "xl"))
-    values = partial_values(sums, branch, out_gains, h_share, 16)
-    values = exchanged(values, OCTANT + ("core",)).reshape(4, 2, 2, rows).sum(axis=0)
+    sums = exchanged(token_sums(mixed, out_weights, out_gains, h_share, 16), OCTANT + ("core",))
+    sums = sums.reshape(4, 2, 2, 8, rows).sum(axis=0)
+    branch_sq, scaled_sq, cross, read_branch, read_hidden, hidden_sq = (
+        sums[:, :, k] for k in range(6)
+    )
+    scale = lax.rsqrt(branch_sq / width + NORM_EPS)
+    residual_sq = hidden_sq + scale * (2.0 * cross + scale * scaled_sq)
+    residual_sq = jnp.maximum(residual_sq, 0.0)
+    values = (read_hidden + scale * read_branch) * lax.rsqrt(residual_sq / width + NORM_EPS)
     pos = pos.reshape(2, 1, rows)
     values = jnp.where(pos < lengths[None, :, None], values, 0.0)
     reward = jnp.sum(jnp.where(pos == reward_pos[None, :, None], values, 0.0), axis=(0, 2))

time: 214 us -> 203 us (0.949)
  blocking collectives: 29.8 us -> 21.4 us
  Pallas kernels: 29.3 us -> 26.9 us
    all_to_all x2 -> x1, blocking collectives: 29.8 us -> 21.4 us  [exchanged(): return lax.all_to_all(tiles, axes, 0, 0, tiled=True)]
    pallas_call x1 -> x0, Pallas kernels: 2.33 us -> none  [partial_values(): pl.pallas_call(values_kernel, in_specs=[vmem] * 4, out_specs=vmem, out_sh...]
  transfers between devices with their start and end apart: 15 -> 15, of which waited for: 6 -> 7; matrix products, arithmetic and copies ran while one was open for 5% -> 5% of each run, Pallas kernels for 10% -> 11%
where the time goes in v4:
time: 203 us; the launch traced here: 202 us
  starting transfers between devices  77.6 us (38%)
  waiting for transfers between devices  44.3 us (22%)
  Pallas kernels  26.9 us (13%)
  blocking collectives  21.4 us (11%)
  between operations  14.4 us (7%)
  local copies, waits for them, and re-layouts  11.5 us (6%)
  other arithmetic  5.87 us (3%)
    ppermute x9, starting transfers between devices, moved(): return lax.ppermute(array, AXES, pairs_of(source_of))  40.1 us
    all_to_all x2, starting transfers between devices, told_to_all(): lax.all_to_all(jnp.broadcast_to(array[None], (n, *array.shape)), axes, 0,...  27.5 us
    all_to_all x1, blocking collectives, exchanged(): return lax.all_to_all(tiles, axes, 0, 0, tiled=True)  21.4 us
    all_to_all x2, waiting for transfers between devices, exchanged(): return lax.all_to_all(tiles, axes, 0, 0, tiled=True)  17.6 us
    all_to_all x2, waiting for transfers between devices, told_to_all(): lax.all_to_all(jnp.broadcast_to(array[None], (n, *array.shape)), axes, 0,...  17.2 us
    pallas_call x2, Pallas kernels, project(): pl.pallas_call(lambda *refs: project_kernel(turns, *refs), grid=(2,), in_...  12.4 us
    all_to_all x2, starting transfers between devices, exchanged(): return lax.all_to_all(tiles, axes, 0, 0, tiled=True)  9.93 us
    ppermute x9, waiting for transfers between devices, moved(): return lax.ppermute(array, AXES, pairs_of(source_of))  5.97 us
  transfers between devices with their start and end apart: 15, of which 7 were waited for; matrix products, arithmetic and copies ran while one was open for 5% of the time, Pallas kernels for 11%

profile of v4, /device:TPU:1, one launch (start us, length us, event | category | flops | bytes accessed | tf_op | source)
XLA Modules:
  0.0 202.2 jit_solution(9222278240297725047)
XLA Ops:
  9.4 4.5 %collective-permute-start = (bf16[2,22,512]{2,1,0:T(8,128)(2,1)S(1)}, bf16[2,22,512]{2,1,0:T(8,128)(2,1)S(1)}, u32[]{:S(2)}, u32[]{:S(2)}) collective-permute-start(bf16[2,22,512]{2,1,0:T(8,128)(2,1)S(1)} %pad_maximum_fusion.3), channel_id=1, source_target_pairs={{0,0},{128,1},{1,2},{129,3},{2,4},{130,5},{3,6},{131,7},{4,8},{132... | collective-permute-start | bytes 135176 | tf_op jit(solution)/shard_map/ppermute | solution.py:56
  15.4 3.3 %collective-permute-start.1 = (bf16[22,512]{1,0:T(8,128)(2,1)S(1)}, bf16[22,512]{1,0:T(8,128)(2,1)S(1)}, u32[]{:S(2)}, u32[]{:S(2)}) collective-permute-start(bf16[22,512]{1,0:T(8,128)(2,1)S(1)} %pad_maximum_fusion.6), channel_id=1, source_target_pairs={{0,0},{32,1},{1,2},{33,3},{2,4},{34,5},{3,6},{35,7},{4,8},{36,9},{... | collective-permute-start | bytes 67592 | tf_op jit(solution)/shard_map/ppermute | solution.py:56
  18.8 5.9 %collective-permute-done.1 = bf16[22,512]{1,0:T(8,128)(2,1)S(1)} collective-permute-done((bf16[22,512]{1,0:T(8,128)(2,1)S(1)}, bf16[22,512]{1,0:T(8,128)(2,1)S(1)}, u32[]{:S(2)}, u32[]{:S(2)}) %collective-permute-start.1) | collective-permute-done | bytes 22560 | tf_op jit(solution)/shard_map/ppermute | solution.py:56
  24.8 21.4 %all_to_all.26 = bf16[8,22,1024]{2,1,0:T(8,128)(2,1)S(1)} all-to-all(bf16[8,22,1024]{2,1,0:T(8,128)(2,1)S(1)} %pad_maximum_fusion), channel_id=1, replica_groups=mesh['xh'=2,'core'=2,'z'=8,'yy'=4,'p'=2,'xl'=2] {'yy','p'}, dimensions={0} | all-to-all | bytes 720896 | tf_op jit(solution)/shard_map/all_to_all | solution.py:65
  48.0 2.7 %collective-permute-start.2 = (bf16[128,2688]{1,0:T(8,128)(2,1)S(1)}, bf16[128,2688]{1,0:T(8,128)(2,1)S(1)}, u32[]{:S(2)}, u32[]{:S(2)}) collective-permute-start(bf16[128,2688]{1,0:T(8,128)(2,1)S(1)} %dynamic-slice_bitcast_fusion.refs_0_), channel_id=1, source_target_pairs={{1,0},{0,1},{3,2},{2,3},{5,4},{4,5},{7,6},{6,7},{9,8},{8,9},{11,10... | collective-permute-start | bytes 2064392 | tf_op jit(solution)/shard_map/ppermute | solution.py:56
  52.6 3.8 %collective-permute-start.4 = (bf16[128,2688]{1,0:T(8,128)(2,1)S(1)}, bf16[128,2688]{1,0:T(8,128)(2,1)S(1)}, u32[]{:S(2)}, u32[]{:S(2)}) collective-permute-start(bf16[128,2688]{1,0:T(8,128)(2,1)S(1)} %dynamic-slice_bitcast_fusion.refs_0_), channel_id=1, source_target_pairs={{3,0},{2,1},{1,2},{0,3},{7,4},{6,5},{5,6},{4,7},{11,8},{10,9},{9,1... | collective-permute-start | bytes 2064392 | tf_op jit(solution)/shard_map/ppermute | solution.py:56
  59.6 18.2 %all-to-all-start.1 = ((bf16[16,4,256]{2,1,0:T(4,128)(2,1)}), bf16[16,4,256]{2,1,0:T(4,128)(2,1)S(1)}, u32[]{:S(2)}, u32[]{:S(2)}) async-start(bf16[16,4,256]{2,1,0:T(4,128)(2,1)} %broadcast_in_dim.41), calls=%async_computation.1 | async-start | bytes 65536 | tf_op jit(solution)/shard_map/all_to_all | solution.py:61
  78.4 6.8 %all-to-all-done.1 = bf16[16,4,256]{2,1,0:T(4,128)(2,1)S(1)} async-done(((bf16[16,4,256]{2,1,0:T(4,128)(2,1)}), bf16[16,4,256]{2,1,0:T(4,128)(2,1)S(1)}, u32[]{:S(2)}, u32[]{:S(2)}) %all-to-all-start.1) | async-done | bytes 32800 | tf_op jit(solution)/shard_map/all_to_all | solution.py:61
  87.7 4.3 %norm.1.refs_1_ = bf16[512,2688]{1,0:T(8,128)(2,1)} custom-call(s32[4]{0:T(128)} %pad_add_fusion.order_ref.refs_0_, f32[1,2688]{1,0:T(1,128)} %reshape_squeeze.3.gain_ref.refs_3_, bf16[128,2688]{1,0:T(8,128)(2,1)} %copy-done.3, bf16[128,2688]{1,0:T(8,128)(2,1)} %copy-done.1, bf16[128,2688]{1,0:T(8,128)(2,1)} %copy-done.7), custom_call_target="tpu_custom_call" | custom-call | tf_op jit(solution)/shard_map/norm/pallas_call | solution.py:88
  92.0 2.8 %all-gather.3.cloned.1.call-done.refs_4_ = bf16[2688,512]{1,0:T(8,128)(2,1)} async-done(((bf16[168,512]{1,0:T(8,128)(2,1)}), bf16[2688,512]{1,0:T(8,128)(2,1)}) %all-gather.3.cloned.1.call-update) | async-done | bytes 2752528 | tf_op jit(solution)/shard_map/all_gather | solution.py:338
  94.8 5.9 %project.3 = (bf16[512,128]{1,0:T(8,128)(2,1)}, bf16[512,128]{1,0:T(8,128)(2,1)}) custom-call(s32[4]{0:T(128)} %pad_add_fusion.order_ref.refs_0_, bf16[512,2688]{1,0:T(8,128)(2,1)} %norm.1.refs_1_, bf16[128,2688]{1,0:T(8,128)(2,1)} %copy-done.4, f32[1,2688]{1,0:T(1,128)} %reshape_squeeze.3.gain_ref.refs_3_, ...), custom_call_target="tpu_custom_call" | custom-call | tf_op jit(solution)/shard_map/project/pallas_call | solution.py:141
  100.7 3.9 %collective-permute-start.5 = (bf16[512,128]{1,0:T(8,128)(2,1)}, bf16[512,128]{1,0:T(8,128)(2,1)S(1)}, u32[]{:S(2)}, u32[]{:S(2)}) collective-permute-start(bf16[512,128]{1,0:T(8,128)(2,1)} %get-tuple-element.4.refs_0_), channel_id=1, source_target_pairs={{0,4},{1,5},{2,6},{3,7},{4,8},{5,9},{6,10},{7,11},{8,12},{9,13},{1... | collective-permute-start | bytes 393224 | tf_op jit(solution)/shard_map/ppermute | solution.py:56
  104.6 5.6 %collective-permute-start.7 = (bf16[512,128]{1,0:T(8,128)(2,1)}, bf16[512,128]{1,0:T(8,128)(2,1)S(1)}, u32[]{:S(2)}, u32[]{:S(2)}) collective-permute-start(bf16[512,128]{1,0:T(8,128)(2,1)} %get-tuple-element.5.refs_3_), channel_id=1, source_target_pairs={{0,4},{1,5},{2,6},{3,7},{4,8},{5,9},{6,10},{7,11},{8,12},{9,13},{1... | collective-permute-start | bytes 393224 | tf_op jit(solution)/shard_map/ppermute | solution.py:56
  110.3 8.1 %collective-permute-start.6 = (bf16[512,128]{1,0:T(8,128)(2,1)S(1)}, bf16[512,128]{1,0:T(8,128)(2,1)S(1)}, u32[]{:S(2)}, u32[]{:S(2)}) collective-permute-start(bf16[512,128]{1,0:T(8,128)(2,1)S(1)} %collective-permute-done.5.refs_1_), channel_id=1, source_target_pairs={{0,4},{1,5},{2,6},{3,7},{4,8},{5,9},{6,10},{7,11},{8,12},{9,13},{1... | collective-permute-start | bytes 393224 | tf_op jit(solution)/shard_map/ppermute | solution.py:56
  118.4 6.3 %collective-permute-start.8 = (bf16[512,128]{1,0:T(8,128)(2,1)S(1)}, bf16[512,128]{1,0:T(8,128)(2,1)S(1)}, u32[]{:S(2)}, u32[]{:S(2)}) collective-permute-start(bf16[512,128]{1,0:T(8,128)(2,1)S(1)} %collective-permute-done.7.refs_4_), channel_id=1, source_target_pairs={{0,4},{1,5},{2,6},{3,7},{4,8},{5,9},{6,10},{7,11},{8,12},{9,13},{1... | collective-permute-start | bytes 393224 | tf_op jit(solution)/shard_map/ppermute | solution.py:56
  125.2 6.5 %project.2.q_ref = bf16[512,256]{1,0:T(8,128)(2,1)} custom-call(s32[4]{0:T(128)} %pad_add_fusion.order_ref.refs_0_, bf16[512,2688]{1,0:T(8,128)(2,1)} %norm.1.refs_1_, bf16[128,2688]{1,0:T(8,128)(2,1)} %copy-done.4, f32[1,2688]{1,0:T(1,128)} %reshape_squeeze.3.gain_ref.refs_3_, bf16[2688,512]{1,0:T(8,128)(2,1)} %all-gather.3.cloned.1.call-done.refs_4_, ...), custom_call_target="tpu_custom_call" | custom-call | tf_op jit(solution)/shard_map/project/pallas_call | solution.py:141
  132.3 5.3 %attend.1 = bf16[8,256,256]{2,1,0:T(8,128)(2,1)} custom-call(s32[1]{0:T(128)} %bitcast.block_ref, bf16[512,256]{1,0:T(8,128)(2,1)} %project.2.q_ref, bf16[512,128]{1,0:T(8,128)(2,1)} %get-tuple-element.4.refs_0_, bf16[512,128]{1,0:T(8,128)(2,1)} %copy-done.8, bf16[512,128]{1,0:T(8,128)(2,1)} %copy-done.10, bf16[512,128]{1,0:T(8,128)(2,1)} %get-tuple-element.5.refs_3_, ...), custom_call_target="tpu_custom_call" | custom-call | tf_op jit(solution)/shard_map/attend/pallas_call | solution.py:219
  137.6 3.7 %all-to-all-start.2 = ((bf16[8,256,256]{2,1,0:T(8,128)(2,1)}), bf16[8,256,256]{2,1,0:T(8,128)(2,1)S(1)}, u32[]{:S(2)}, u32[]{:S(2)}) async-start(bf16[8,256,256]{2,1,0:T(8,128)(2,1)} %attend.1), calls=%async_computation.2 | async-start | bytes 2097152 | tf_op jit(solution)/shard_map/all_to_all | solution.py:65
  143.7 11.4 %all-to-all-done.2.mixed_ref = bf16[8,256,256]{2,1,0:T(8,128)(2,1)S(1)} async-done(((bf16[8,256,256]{2,1,0:T(8,128)(2,1)}), bf16[8,256,256]{2,1,0:T(8,128)(2,1)S(1)}, u32[]{:S(2)}, u32[]{:S(2)}) %all-to-all-start.2) | async-done | bytes 1048608 | tf_op jit(solution)/shard_map/all_to_all | solution.py:65
  156.0 5.0 %token_sums.1 = f32[16,8,256]{2,1,0:T(8,128)} custom-call(bf16[8,256,256]{2,1,0:T(8,128)(2,1)} %copy-done, bf16[4,4,168,512]{3,2,1,0:T(8,128)(2,1)} %bitcast.73, f32[4,168,3]{2,1,0:T(8,128)} %bitcast.76, bf16[4,168,256]{2,1,0:T(8,128)(2,1)} %bitcast.75), custom_call_target="tpu_custom_call" | custom-call | tf_op jit(solution)/shard_map/token_sums/pallas_call | solution.py:271
  161.0 6.2 %all-to-all-start.3 = ((f32[16,8,256]{2,1,0:T(8,128)}), f32[16,8,256]{2,1,0:T(8,128)S(1)}, u32[]{:S(2)}, u32[]{:S(2)}) async-start(f32[16,8,256]{2,1,0:T(8,128)} %token_sums.1), calls=%async_computation.3 | async-start | bytes 262144 | tf_op jit(solution)/shard_map/all_to_all | solution.py:65
  167.3 6.2 %all-to-all-done.3 = f32[16,8,256]{2,1,0:T(8,128)S(1)} async-done(((f32[16,8,256]{2,1,0:T(8,128)}), f32[16,8,256]{2,1,0:T(8,128)S(1)}, u32[]{:S(2)}, u32[]{:S(2)}) %all-to-all-start.3) | async-done | bytes 131104 | tf_op jit(solution)/shard_map/all_to_all | solution.py:65
  174.3 9.4 %all-to-all-start.4 = ((f32[32,1,2]{2,1,0:T(1,128)}), f32[32,1,2]{2,1,0:T(1,128)S(1)}, u32[]{:S(2)}, u32[]{:S(2)}) async-start(f32[32,1,2]{2,1,0:T(1,128)} %broadcast_in_dim.44), calls=%async_computation.4 | async-start | bytes 32768 | tf_op jit(solution)/shard_map/all_to_all | solution.py:61
  184.4 10.4 %all-to-all-done.4 = f32[32,1,2]{2,1,0:T(1,128)S(1)} async-done(((f32[32,1,2]{2,1,0:T(1,128)}), f32[32,1,2]{2,1,0:T(1,128)S(1)}, u32[]{:S(2)}, u32[]{:S(2)}) %all-to-all-start.4) | async-done | bytes 288 | tf_op jit(solution)/shard_map/all_to_all | solution.py:61
  (88 shorter events, 20.2 us)
Async XLA Ops:
  7.2 87.6 %all-gather.3.cloned.1.call-start = ((), (), s32[]{:S(2)}) async-start(), calls=%async_computation.5 | async-start | bytes 2924544 | tf_op jit(solution)/shard_map/all_gather | solution.py:338
  9.4 15.3 %collective-permute-start = (bf16[2,22,512]{2,1,0:T(8,128)(2,1)S(1)}, bf16[2,22,512]{2,1,0:T(8,128)(2,1)S(1)}, u32[]{:S(2)}, u32[]{:S(2)}) collective-permute-start(bf16[2,22,512]{2,1,0:T(8,128)(2,1)S(1)} %pad_maximum_fusion.3), channel_id=1, source_target_pairs={{0,0},{128,1},{1,2},{129,3},{2,4},{130,5},{3,6},{131,7},{4,8},{132... | collective-permute-start | bytes 135176 | tf_op jit(solution)/shard_map/ppermute | solution.py:56
  15.4 9.3 %collective-permute-start.1 = (bf16[22,512]{1,0:T(8,128)(2,1)S(1)}, bf16[22,512]{1,0:T(8,128)(2,1)S(1)}, u32[]{:S(2)}, u32[]{:S(2)}) collective-permute-start(bf16[22,512]{1,0:T(8,128)(2,1)S(1)} %pad_maximum_fusion.6), channel_id=1, source_target_pairs={{0,0},{32,1},{1,2},{33,3},{2,4},{34,5},{3,6},{35,7},{4,8},{36,9},{... | collective-permute-start | bytes 67592 | tf_op jit(solution)/shard_map/ppermute | solution.py:56
  24.8 23.1 %copy-start.5 = (bf16[2,128,2688]{2,1,0:T(8,128)(2,1)S(1)}, bf16[2,128,2688]{2,1,0:T(8,128)(2,1)}, u32[]{:S(2)}) copy-start(bf16[2,128,2688]{2,1,0:T(8,128)(2,1)} %param.14) | copy-start | bytes 4128772
  46.4 10.1 %copy-start.14 = (f32[64]{0:T(128)S(1)}, f32[64]{0:T(128)}, u32[]{:S(2)}) copy-start(f32[64]{0:T(128)} %constant.103) | copy-start | bytes 772
  47.2 96.5 %all-gather.5.cloned.1.call-start = ((), (), s32[]{:S(2)}) async-start(), calls=%async_computation.6 | async-start | bytes 2924544 | tf_op jit(solution)/shard_map/all_gather | solution.py:339
  48.0 37.9 %copy-start.3 = (bf16[128,2688]{1,0:T(8,128)(2,1)}, bf16[128,2688]{1,0:T(8,128)(2,1)S(1)}, u32[]{:S(2)}) copy-start(bf16[128,2688]{1,0:T(8,128)(2,1)S(1)} %dynamic-slice_bitcast_fusion.refs_0_) | copy-start | bytes 2064388
  48.0 37.9 %collective-permute-start.2 = (bf16[128,2688]{1,0:T(8,128)(2,1)S(1)}, bf16[128,2688]{1,0:T(8,128)(2,1)S(1)}, u32[]{:S(2)}, u32[]{:S(2)}) collective-permute-start(bf16[128,2688]{1,0:T(8,128)(2,1)S(1)} %dynamic-slice_bitcast_fusion.refs_0_), channel_id=1, source_target_pairs={{1,0},{0,1},{3,2},{2,3},{5,4},{4,5},{7,6},{6,7},{9,8},{8,9},{11,10... | collective-permute-start | bytes 2064392 | tf_op jit(solution)/shard_map/ppermute | solution.py:56
  50.7 35.2 %collective-permute-start.3 = (bf16[128,2688]{1,0:T(8,128)(2,1)S(1)}, bf16[128,2688]{1,0:T(8,128)(2,1)S(1)}, u32[]{:S(2)}, u32[]{:S(2)}) collective-permute-start(bf16[128,2688]{1,0:T(8,128)(2,1)S(1)} %dynamic-slice_bitcast_fusion.refs_0_), channel_id=1, source_target_pairs={{2,0},{3,1},{0,2},{1,3},{6,4},{7,5},{4,6},{5,7},{10,8},{11,9},{8,1... | collective-permute-start | bytes 2064392 | tf_op jit(solution)/shard_map/ppermute | solution.py:56
  52.6 39.4 %collective-permute-start.4 = (bf16[128,2688]{1,0:T(8,128)(2,1)S(1)}, bf16[128,2688]{1,0:T(8,128)(2,1)S(1)}, u32[]{:S(2)}, u32[]{:S(2)}) collective-permute-start(bf16[128,2688]{1,0:T(8,128)(2,1)S(1)} %dynamic-slice_bitcast_fusion.refs_0_), channel_id=1, source_target_pairs={{3,0},{2,1},{1,2},{0,3},{7,4},{6,5},{5,6},{4,7},{11,8},{10,9},{9,1... | collective-permute-start | bytes 2064392 | tf_op jit(solution)/shard_map/ppermute | solution.py:56
  59.6 25.6 %all-to-all-start.1 = ((bf16[16,4,256]{2,1,0:T(4,128)(2,1)}), bf16[16,4,256]{2,1,0:T(4,128)(2,1)S(1)}, u32[]{:S(2)}, u32[]{:S(2)}) async-start(bf16[16,4,256]{2,1,0:T(4,128)(2,1)} %broadcast_in_dim.41), calls=%async_computation.1 | async-start | bytes 65536 | tf_op jit(solution)/shard_map/all_to_all | solution.py:61
  94.8 29.8 %copy-start.15 = (f32[128]{0:T(128)S(1)}, f32[128]{0:T(128)}, u32[]{:S(2)}) copy-start(f32[128]{0:T(128)} %param.21) | copy-start | bytes 1540
  100.7 9.6 %collective-permute-start.5 = (bf16[512,128]{1,0:T(8,128)(2,1)}, bf16[512,128]{1,0:T(8,128)(2,1)S(1)}, u32[]{:S(2)}, u32[]{:S(2)}) collective-permute-start(bf16[512,128]{1,0:T(8,128)(2,1)} %get-tuple-element.4.refs_0_), channel_id=1, source_target_pairs={{0,4},{1,5},{2,6},{3,7},{4,8},{5,9},{6,10},{7,11},{8,12},{9,13},{1... | collective-permute-start | bytes 393224 | tf_op jit(solution)/shard_map/ppermute | solution.py:56
  104.6 13.7 %collective-permute-start.7 = (bf16[512,128]{1,0:T(8,128)(2,1)}, bf16[512,128]{1,0:T(8,128)(2,1)S(1)}, u32[]{:S(2)}, u32[]{:S(2)}) collective-permute-start(bf16[512,128]{1,0:T(8,128)(2,1)} %get-tuple-element.5.refs_3_), channel_id=1, source_target_pairs={{0,4},{1,5},{2,6},{3,7},{4,8},{5,9},{6,10},{7,11},{8,12},{9,13},{1... | collective-permute-start | bytes 393224 | tf_op jit(solution)/shard_map/ppermute | solution.py:56
  110.3 21.3 %copy-start.8 = (bf16[512,128]{1,0:T(8,128)(2,1)}, bf16[512,128]{1,0:T(8,128)(2,1)S(1)}, u32[]{:S(2)}) copy-start(bf16[512,128]{1,0:T(8,128)(2,1)S(1)} %collective-permute-done.5.refs_1_) | copy-start | bytes 393220
  110.3 21.3 %collective-permute-start.6 = (bf16[512,128]{1,0:T(8,128)(2,1)S(1)}, bf16[512,128]{1,0:T(8,128)(2,1)S(1)}, u32[]{:S(2)}, u32[]{:S(2)}) collective-permute-start(bf16[512,128]{1,0:T(8,128)(2,1)S(1)} %collective-permute-done.5.refs_1_), channel_id=1, source_target_pairs={{0,4},{1,5},{2,6},{3,7},{4,8},{5,9},{6,10},{7,11},{8,12},{9,13},{1... | collective-permute-start | bytes 393224 | tf_op jit(solution)/shard_map/ppermute | solution.py:56
  118.4 13.3 %copy-start.9 = (bf16[512,128]{1,0:T(8,128)(2,1)}, bf16[512,128]{1,0:T(8,128)(2,1)S(1)}, u32[]{:S(2)}) copy-start(bf16[512,128]{1,0:T(8,128)(2,1)S(1)} %collective-permute-done.7.refs_4_) | copy-start | bytes 393220
  118.4 13.3 %collective-permute-start.8 = (bf16[512,128]{1,0:T(8,128)(2,1)S(1)}, bf16[512,128]{1,0:T(8,128)(2,1)S(1)}, u32[]{:S(2)}, u32[]{:S(2)}) collective-permute-start(bf16[512,128]{1,0:T(8,128)(2,1)S(1)} %collective-permute-done.7.refs_4_), channel_id=1, source_target_pairs={{0,4},{1,5},{2,6},{3,7},{4,8},{5,9},{6,10},{7,11},{8,12},{9,13},{1... | collective-permute-start | bytes 393224 | tf_op jit(solution)/shard_map/ppermute | solution.py:56
  137.6 3.7 %copy-start.6 = (bf16[2,128,2688]{2,1,0:T(8,128)(2,1)S(1)}, bf16[2,128,2688]{2,1,0:T(8,128)(2,1)}, u32[]{:S(2)}) copy-start(bf16[2,128,2688]{2,1,0:T(8,128)(2,1)} %param.14) | copy-start | bytes 4128772
  137.6 17.4 %all-to-all-start.2 = ((bf16[8,256,256]{2,1,0:T(8,128)(2,1)}), bf16[8,256,256]{2,1,0:T(8,128)(2,1)S(1)}, u32[]{:S(2)}, u32[]{:S(2)}) async-start(bf16[8,256,256]{2,1,0:T(8,128)(2,1)} %attend.1), calls=%async_computation.2 | async-start | bytes 2097152 | tf_op jit(solution)/shard_map/all_to_all | solution.py:65
  156.0 17.5 %copy-start.12 = (s32[2]{0:T(128)S(1)}, s32[2]{0:T(128)}, u32[]{:S(2)}) copy-start(s32[2]{0:T(128)} %param.16) | copy-start | bytes 28
  156.0 17.5 %copy-start.13 = (s32[2]{0:T(128)S(1)}, s32[2]{0:T(128)}, u32[]{:S(2)}) copy-start(s32[2]{0:T(128)} %param.15) | copy-start | bytes 28
  161.0 12.4 %all-to-all-start.3 = ((f32[16,8,256]{2,1,0:T(8,128)}), f32[16,8,256]{2,1,0:T(8,128)S(1)}, u32[]{:S(2)}, u32[]{:S(2)}) async-start(f32[16,8,256]{2,1,0:T(8,128)} %token_sums.1), calls=%async_computation.3 | async-start | bytes 262144 | tf_op jit(solution)/shard_map/all_to_all | solution.py:65
  174.3 20.4 %all-to-all-start.4 = ((f32[32,1,2]{2,1,0:T(1,128)}), f32[32,1,2]{2,1,0:T(1,128)S(1)}, u32[]{:S(2)}, u32[]{:S(2)}) async-start(f32[32,1,2]{2,1,0:T(1,128)} %broadcast_in_dim.44), calls=%async_computation.4 | async-start | bytes 32768 | tf_op jit(solution)/shard_map/all_to_all | solution.py:61
  (7 other events, 10.6 us)
Sparse Core Ops, SparseCore 0:
  47.3 47.4 all-gather.2
  96.9 46.7 all-gather.4

commit v5 on v2

--- a/solution.py
+++ b/solution.py
@@ -150,14 +150,16 @@
             top = jnp.max(scores[0], axis=1, keepdims=True)
             for s in scores[1:]:
                 top = jnp.maximum(top, jnp.max(s, axis=1, keepdims=True))
-            total, mixed = 0.0, 0.0
-            for s, piece in zip(scores, pieces):
-                e = jnp.exp(s - top)
-                total = total + jnp.sum(e, axis=1, keepdims=True)
+            terms = [jnp.exp(s - top) for s in scores]
+            share = 1.0 / sum(jnp.sum(e, axis=1, keepdims=True) for e in terms)
+            mixed = 0.0
+            for e, piece in zip(terms, pieces):
                 mixed = mixed + jnp.dot(
-                    e.astype(jnp.bfloat16), piece[:, HD:], preferred_element_type=jnp.float32
+                    (e * share).astype(jnp.bfloat16),
+                    piece[:, HD:],
+                    preferred_element_type=jnp.float32,
                 )
-            mixed = (mixed / total).astype(jnp.bfloat16)
+            mixed = mixed.astype(jnp.bfloat16)
             for x in range(4):
                 out_ref[2 * x + a, :, g * HD : (g + 1) * HD] = mixed
 
@@ -312,7 +314,7 @@
     h_share = h_share.T.reshape(4, octet_rows, rows)
 
     pos = block * 2 * rows + jnp.arange(2 * rows, dtype=jnp.int32)
-    frequency = ROPE_BASE ** (-jnp.arange(HD // 2, dtype=jnp.float32) * 2.0 / HD)
+    frequency = (ROPE_BASE ** (-np.arange(HD // 2) * 2.0 / HD)).astype(np.float32)
     angles = pos.astype(jnp.float32)[:, None] * frequency[None, :]
     cos, sin = jnp.cos(angles), jnp.sin(angles)
     cos = jnp.concatenate([cos, cos], axis=1)

time: 206 us -> 207 us (level)
  transfers between devices with their start and end apart: 13 -> 13, of which waited for: 9 -> 9; matrix products, arithmetic and copies ran while one was open for 5% -> 5% of each run, Pallas kernels for 9% -> 10%
where the time goes in v5:
time: 207 us; the launch traced here: 206 us
  starting transfers between devices  70.8 us (34%)
  waiting for transfers between devices  58.4 us (28%)
  Pallas kernels  24.8 us (12%)
  blocking collectives  21.4 us (10%)
  between operations  14.3 us (7%)
  local copies, waits for them, and re-layouts  10.6 us (5%)
  other arithmetic  5.88 us (3%)
    all_to_all x2, starting transfers between devices, told_to_all(): lax.all_to_all(jnp.broadcast_to(array[None], (n, *array.shape)), axes, 0,...  31.9 us
    ppermute x7, starting transfers between devices, moved(): return lax.ppermute(array, AXES, pairs_of(source_of))  28.1 us
    all_to_all x1, blocking collectives, exchanged(): return lax.all_to_all(tiles, axes, 0, 0, tiled=True)  21.4 us
    ppermute x7, waiting for transfers between devices, moved(): return lax.ppermute(array, AXES, pairs_of(source_of))  19.1 us
    all_to_all x2, waiting for transfers between devices, told_to_all(): lax.all_to_all(jnp.broadcast_to(array[None], (n, *array.shape)), axes, 0,...  17.2 us
    all_to_all x2, waiting for transfers between devices, exchanged(): return lax.all_to_all(tiles, axes, 0, 0, tiled=True)  15 us
    all_to_all x2, starting transfers between devices, exchanged(): return lax.all_to_all(tiles, axes, 0, 0, tiled=True)  10.7 us
    pallas_call x2, Pallas kernels, project(): pl.pallas_call(lambda *refs: project_kernel(turned_heads, *refs), grid=(2...  9.8 us
  transfers between devices with their start and end apart: 13, of which 9 were waited for; matrix products, arithmetic and copies ran while one was open for 5% of the time, Pallas kernels for 10%

profile of v5, /device:TPU:1, one launch (start us, length us, event | category | flops | bytes accessed | tf_op | source)
XLA Modules:
  0.0 206.3 jit_solution(17304390088013559286)
XLA Ops:
  9.4 4.5 %collective-permute-start = (bf16[2,22,512]{2,1,0:T(8,128)(2,1)S(1)}, bf16[2,22,512]{2,1,0:T(8,128)(2,1)S(1)}, u32[]{:S(2)}, u32[]{:S(2)}) collective-permute-start(bf16[2,22,512]{2,1,0:T(8,128)(2,1)S(1)} %pad_maximum_fusion.3), channel_id=1, source_target_pairs={{0,0},{128,1},{1,2},{129,3},{2,4},{130,5},{3,6},{131,7},{4,8},{132... | collective-permute-start | bytes 135176 | tf_op jit(solution)/shard_map/ppermute | solution.py:56
  15.4 3.3 %collective-permute-start.1 = (bf16[22,512]{1,0:T(8,128)(2,1)S(1)}, bf16[22,512]{1,0:T(8,128)(2,1)S(1)}, u32[]{:S(2)}, u32[]{:S(2)}) collective-permute-start(bf16[22,512]{1,0:T(8,128)(2,1)S(1)} %pad_maximum_fusion.6), channel_id=1, source_target_pairs={{0,0},{32,1},{1,2},{33,3},{2,4},{34,5},{3,6},{35,7},{4,8},{36,9},{... | collective-permute-start | bytes 67592 | tf_op jit(solution)/shard_map/ppermute | solution.py:56
  18.8 5.9 %collective-permute-done.1 = bf16[22,512]{1,0:T(8,128)(2,1)S(1)} collective-permute-done((bf16[22,512]{1,0:T(8,128)(2,1)S(1)}, bf16[22,512]{1,0:T(8,128)(2,1)S(1)}, u32[]{:S(2)}, u32[]{:S(2)}) %collective-permute-start.1) | collective-permute-done | bytes 22560 | tf_op jit(solution)/shard_map/ppermute | solution.py:56
  24.8 21.4 %all_to_all.26 = bf16[8,22,1024]{2,1,0:T(8,128)(2,1)S(1)} all-to-all(bf16[8,22,1024]{2,1,0:T(8,128)(2,1)S(1)} %pad_maximum_fusion), channel_id=1, replica_groups=mesh['xh'=2,'core'=2,'z'=8,'yy'=4,'p'=2,'xl'=2] {'yy','p'}, dimensions={0} | all-to-all | bytes 720896 | tf_op jit(solution)/shard_map/all_to_all | solution.py:65
  52.6 3.8 %collective-permute-start.4 = (bf16[128,2688]{1,0:T(8,128)(2,1)S(1)}, bf16[128,2688]{1,0:T(8,128)(2,1)}, u32[]{:S(2)}, u32[]{:S(2)}) collective-permute-start(bf16[128,2688]{1,0:T(8,128)(2,1)S(1)} %dynamic-slice_bitcast_fusion.refs_0_), channel_id=1, source_target_pairs={{3,0},{2,1},{1,2},{0,3},{7,4},{6,5},{5,6},{4,7},{11,8},{10,9},{9,1... | collective-permute-start | bytes 2064392 | tf_op jit(solution)/shard_map/ppermute | solution.py:56
  59.6 18.2 %all-to-all-start.1 = ((bf16[16,4,256]{2,1,0:T(4,128)(2,1)}), bf16[16,4,256]{2,1,0:T(4,128)(2,1)S(1)}, u32[]{:S(2)}, u32[]{:S(2)}) async-start(bf16[16,4,256]{2,1,0:T(4,128)(2,1)} %broadcast_in_dim.41), calls=%async_computation.1 | async-start | bytes 65536 | tf_op jit(solution)/shard_map/all_to_all | solution.py:61
  78.4 6.8 %all-to-all-done.1 = bf16[16,4,256]{2,1,0:T(4,128)(2,1)S(1)} async-done(((bf16[16,4,256]{2,1,0:T(4,128)(2,1)}), bf16[16,4,256]{2,1,0:T(4,128)(2,1)S(1)}, u32[]{:S(2)}, u32[]{:S(2)}) %all-to-all-start.1) | async-done | bytes 32800 | tf_op jit(solution)/shard_map/all_to_all | solution.py:61
  86.8 4.8 %norm.1.refs_0_ = bf16[512,2688]{1,0:T(8,128)(2,1)} custom-call(s32[4]{0:T(128)} %pad_add_fusion.order_ref, f32[1,2688]{1,0:T(1,128)} %reshape_squeeze.3.gain_ref, bf16[128,2688]{1,0:T(8,128)(2,1)} %copy-done.3, bf16[128,2688]{1,0:T(8,128)(2,1)} %copy-done.1, bf16[128,2688]{1,0:T(8,128)(2,1)} %collective-permute-done.3.refs_2_, ...), custom_call_target="tpu_custom_call" | custom-call | tf_op jit(solution)/shard_map/norm/pallas_call | solution.py:80
  91.6 3.3 %all-gather.3.cloned.1.call-done.refs_1_ = bf16[2688,512]{1,0:T(8,128)(2,1)} async-done(((bf16[168,512]{1,0:T(8,128)(2,1)}), bf16[2688,512]{1,0:T(8,128)(2,1)}) %all-gather.3.cloned.1.call-update) | async-done | bytes 2752528 | tf_op jit(solution)/shard_map/all_gather | solution.py:289
  94.9 4.8 %project.3.own_ref = bf16[512,256]{1,0:T(8,128)(2,1)} custom-call(bf16[512,2688]{1,0:T(8,128)(2,1)} %norm.1.refs_0_, bf16[2688,512]{1,0:T(8,128)(2,1)} %all-gather.3.cloned.1.call-done.refs_1_, f32[1,128]{1,0:T(1,128)} %bitcast.80, f32[512,128]{1,0:T(8,128)} %get-tuple-element.31.refs_3_, f32[512,128]{1,0:T(8,128)} %get-tuple-element.32.refs_4_), custom_call_target="tpu_custom_call" | custom-call | tf_op jit(solution)/shard_map/project/pallas_call | solution.py:111
  99.7 3.9 %collective-permute-start.5 = (bf16[512,256]{1,0:T(8,128)(2,1)}, bf16[512,256]{1,0:T(8,128)(2,1)S(1)}, u32[]{:S(2)}, u32[]{:S(2)}) collective-permute-start(bf16[512,256]{1,0:T(8,128)(2,1)} %project.3.own_ref), channel_id=1, source_target_pairs={{0,4},{1,5},{2,6},{3,7},{4,8},{5,9},{6,10},{7,11},{8,12},{9,13},{1... | collective-permute-start | bytes 786440 | tf_op jit(solution)/shard_map/ppermute | solution.py:56
  103.6 9.3 %collective-permute-done.5.back1_ref = bf16[512,256]{1,0:T(8,128)(2,1)S(1)} collective-permute-done((bf16[512,256]{1,0:T(8,128)(2,1)}, bf16[512,256]{1,0:T(8,128)(2,1)S(1)}, u32[]{:S(2)}, u32[]{:S(2)}) %collective-permute-start.5) | collective-permute-done | bytes 262176 | tf_op jit(solution)/shard_map/ppermute | solution.py:56
  112.9 8.1 %collective-permute-start.6 = (bf16[512,256]{1,0:T(8,128)(2,1)S(1)}, bf16[512,256]{1,0:T(8,128)(2,1)S(1)}, u32[]{:S(2)}, u32[]{:S(2)}) collective-permute-start(bf16[512,256]{1,0:T(8,128)(2,1)S(1)} %collective-permute-done.5.back1_ref), channel_id=1, source_target_pairs={{0,4},{1,5},{2,6},{3,7},{4,8},{5,9},{6,10},{7,11},{8,12},{9,13},{1... | collective-permute-start | bytes 786440 | tf_op jit(solution)/shard_map/ppermute | solution.py:56
  121.5 5.0 %project.2.q_ref = bf16[512,256]{1,0:T(8,128)(2,1)} custom-call(bf16[512,2688]{1,0:T(8,128)(2,1)} %norm.1.refs_0_, bf16[2688,512]{1,0:T(8,128)(2,1)} %all-gather.3.cloned.1.call-done.refs_1_, f32[1,128]{1,0:T(1,128)} %multiply_bitcast_fusion.refs_2_, f32[512,128]{1,0:T(8,128)} %get-tuple-element.31.refs_3_, f32[512,128]{1,0:T(8,128)} %get-tuple-element.32.refs_4_), custom_call_target="tpu_custom_call" | custom-call | tf_op jit(solution)/shard_map/project/pallas_call | solution.py:111
  126.5 3.8 %collective-permute-done.6.back2_ref = bf16[512,256]{1,0:T(8,128)(2,1)S(1)} collective-permute-done((bf16[512,256]{1,0:T(8,128)(2,1)S(1)}, bf16[512,256]{1,0:T(8,128)(2,1)S(1)}, u32[]{:S(2)}, u32[]{:S(2)}) %collective-permute-start.6) | collective-permute-done | bytes 262176 | tf_op jit(solution)/shard_map/ppermute | solution.py:56
  131.0 5.2 %attend.1 = bf16[8,256,256]{2,1,0:T(8,128)(2,1)} custom-call(s32[1]{0:T(128)} %bitcast.block_ref, bf16[512,256]{1,0:T(8,128)(2,1)} %project.2.q_ref, bf16[512,256]{1,0:T(8,128)(2,1)} %project.3.own_ref, bf16[512,256]{1,0:T(8,128)(2,1)} %copy-done.5, bf16[512,256]{1,0:T(8,128)(2,1)} %copy-done.6), custom_call_target="tpu_custom_call" | custom-call | tf_op jit(solution)/shard_map/attend/pallas_call | solution.py:170
  136.3 4.8 %all-to-all-start.2 = ((bf16[8,256,256]{2,1,0:T(8,128)(2,1)}), bf16[8,256,256]{2,1,0:T(8,128)(2,1)S(1)}, u32[]{:S(2)}, u32[]{:S(2)}) async-start(bf16[8,256,256]{2,1,0:T(8,128)(2,1)} %attend.1), calls=%async_computation.2 | async-start | bytes 2097152 | tf_op jit(solution)/shard_map/all_to_all | solution.py:65
  143.3 3.1 %all-gather.5.cloned.1.call-done = bf16[2688,512]{1,0:T(8,128)(2,1)} async-done(((bf16[168,512]{1,0:T(8,128)(2,1)}), bf16[2688,512]{1,0:T(8,128)(2,1)}) %all-gather.5.cloned.1.call-update) | async-done | bytes 2752528 | tf_op jit(solution)/shard_map/all_gather | solution.py:290
  146.4 8.8 %all-to-all-done.2.mixed_ref = bf16[8,256,256]{2,1,0:T(8,128)(2,1)S(1)} async-done(((bf16[8,256,256]{2,1,0:T(8,128)(2,1)}), bf16[8,256,256]{2,1,0:T(8,128)(2,1)S(1)}, u32[]{:S(2)}, u32[]{:S(2)}) %all-to-all-start.2) | async-done | bytes 1048608 | tf_op jit(solution)/shard_map/all_to_all | solution.py:65
  156.2 5.0 %token_sums.1 = f32[16,8,256]{2,1,0:T(8,128)} custom-call(bf16[8,256,256]{2,1,0:T(8,128)(2,1)} %copy-done, bf16[4,4,168,512]{3,2,1,0:T(8,128)(2,1)} %bitcast.73, f32[4,168,3]{2,1,0:T(8,128)} %bitcast.76, bf16[4,168,256]{2,1,0:T(8,128)(2,1)} %bitcast.75), custom_call_target="tpu_custom_call" | custom-call | tf_op jit(solution)/shard_map/token_sums/pallas_call | solution.py:222
  161.2 5.8 %all-to-all-start.3 = ((f32[16,8,256]{2,1,0:T(8,128)}), f32[16,8,256]{2,1,0:T(8,128)S(1)}, u32[]{:S(2)}, u32[]{:S(2)}) async-start(f32[16,8,256]{2,1,0:T(8,128)} %token_sums.1), calls=%async_computation.3 | async-start | bytes 262144 | tf_op jit(solution)/shard_map/all_to_all | solution.py:65
  167.0 6.2 %all-to-all-done.3 = f32[16,8,256]{2,1,0:T(8,128)S(1)} async-done(((f32[16,8,256]{2,1,0:T(8,128)}), f32[16,8,256]{2,1,0:T(8,128)S(1)}, u32[]{:S(2)}, u32[]{:S(2)}) %all-to-all-start.3) | async-done | bytes 131104 | tf_op jit(solution)/shard_map/all_to_all | solution.py:65
  174.1 13.8 %all-to-all-start.4 = ((f32[32,1,2]{2,1,0:T(1,128)}), f32[32,1,2]{2,1,0:T(1,128)S(1)}, u32[]{:S(2)}, u32[]{:S(2)}) async-start(f32[32,1,2]{2,1,0:T(1,128)} %broadcast_in_dim.44), calls=%async_computation.4 | async-start | bytes 32768 | tf_op jit(solution)/shard_map/all_to_all | solution.py:61
  188.5 10.4 %all-to-all-done.4 = f32[32,1,2]{2,1,0:T(1,128)S(1)} async-done(((f32[32,1,2]{2,1,0:T(1,128)}), f32[32,1,2]{2,1,0:T(1,128)S(1)}, u32[]{:S(2)}, u32[]{:S(2)}) %all-to-all-start.4) | async-done | bytes 288 | tf_op jit(solution)/shard_map/all_to_all | solution.py:61
  (74 shorter events, 21.9 us)
Async XLA Ops:
  7.2 87.7 %all-gather.3.cloned.1.call-start = ((), (), s32[]{:S(2)}) async-start(), calls=%async_computation.5 | async-start | bytes 2924544 | tf_op jit(solution)/shard_map/all_gather | solution.py:289
  9.4 15.3 %collective-permute-start = (bf16[2,22,512]{2,1,0:T(8,128)(2,1)S(1)}, bf16[2,22,512]{2,1,0:T(8,128)(2,1)S(1)}, u32[]{:S(2)}, u32[]{:S(2)}) collective-permute-start(bf16[2,22,512]{2,1,0:T(8,128)(2,1)S(1)} %pad_maximum_fusion.3), channel_id=1, source_target_pairs={{0,0},{128,1},{1,2},{129,3},{2,4},{130,5},{3,6},{131,7},{4,8},{132... | collective-permute-start | bytes 135176 | tf_op jit(solution)/shard_map/ppermute | solution.py:56
  15.4 9.3 %collective-permute-start.1 = (bf16[22,512]{1,0:T(8,128)(2,1)S(1)}, bf16[22,512]{1,0:T(8,128)(2,1)S(1)}, u32[]{:S(2)}, u32[]{:S(2)}) collective-permute-start(bf16[22,512]{1,0:T(8,128)(2,1)S(1)} %pad_maximum_fusion.6), channel_id=1, source_target_pairs={{0,0},{32,1},{1,2},{33,3},{2,4},{34,5},{3,6},{35,7},{4,8},{36,9},{... | collective-permute-start | bytes 67592 | tf_op jit(solution)/shard_map/ppermute | solution.py:56
  24.8 23.1 %copy-start.4 = (bf16[2,128,2688]{2,1,0:T(8,128)(2,1)S(1)}, bf16[2,128,2688]{2,1,0:T(8,128)(2,1)}, u32[]{:S(2)}) copy-start(bf16[2,128,2688]{2,1,0:T(8,128)(2,1)} %param.14) | copy-start | bytes 4128772
  46.4 10.1 %copy-start.9 = (f32[64]{0:T(128)S(1)}, f32[64]{0:T(128)}, u32[]{:S(2)}) copy-start(f32[64]{0:T(128)} %constant.103) | copy-start | bytes 772
  47.2 99.2 %all-gather.5.cloned.1.call-start = ((), (), s32[]{:S(2)}) async-start(), calls=%async_computation.6 | async-start | bytes 2924544 | tf_op jit(solution)/shard_map/all_gather | solution.py:290
  48.0 37.9 %copy-start.3 = (bf16[128,2688]{1,0:T(8,128)(2,1)}, bf16[128,2688]{1,0:T(8,128)(2,1)S(1)}, u32[]{:S(2)}) copy-start(bf16[128,2688]{1,0:T(8,128)(2,1)S(1)} %dynamic-slice_bitcast_fusion.refs_0_) | copy-start | bytes 2064388
  48.0 37.9 %collective-permute-start.2 = (bf16[128,2688]{1,0:T(8,128)(2,1)S(1)}, bf16[128,2688]{1,0:T(8,128)(2,1)S(1)}, u32[]{:S(2)}, u32[]{:S(2)}) collective-permute-start(bf16[128,2688]{1,0:T(8,128)(2,1)S(1)} %dynamic-slice_bitcast_fusion.refs_0_), channel_id=1, source_target_pairs={{1,0},{0,1},{3,2},{2,3},{5,4},{4,5},{7,6},{6,7},{9,8},{8,9},{11,10... | collective-permute-start | bytes 2064392 | tf_op jit(solution)/shard_map/ppermute | solution.py:56
  50.7 35.2 %collective-permute-start.3 = (bf16[128,2688]{1,0:T(8,128)(2,1)S(1)}, bf16[128,2688]{1,0:T(8,128)(2,1)}, u32[]{:S(2)}, u32[]{:S(2)}) collective-permute-start(bf16[128,2688]{1,0:T(8,128)(2,1)S(1)} %dynamic-slice_bitcast_fusion.refs_0_), channel_id=1, source_target_pairs={{2,0},{3,1},{0,2},{1,3},{6,4},{7,5},{4,6},{5,7},{10,8},{11,9},{8,1... | collective-permute-start | bytes 2064392 | tf_op jit(solution)/shard_map/ppermute | solution.py:56
  52.6 33.3 %collective-permute-start.4 = (bf16[128,2688]{1,0:T(8,128)(2,1)S(1)}, bf16[128,2688]{1,0:T(8,128)(2,1)}, u32[]{:S(2)}, u32[]{:S(2)}) collective-permute-start(bf16[128,2688]{1,0:T(8,128)(2,1)S(1)} %dynamic-slice_bitcast_fusion.refs_0_), channel_id=1, source_target_pairs={{3,0},{2,1},{1,2},{0,3},{7,4},{6,5},{5,6},{4,7},{11,8},{10,9},{9,1... | collective-permute-start | bytes 2064392 | tf_op jit(solution)/shard_map/ppermute | solution.py:56
  59.6 25.6 %all-to-all-start.1 = ((bf16[16,4,256]{2,1,0:T(4,128)(2,1)}), bf16[16,4,256]{2,1,0:T(4,128)(2,1)S(1)}, u32[]{:S(2)}, u32[]{:S(2)}) async-start(bf16[16,4,256]{2,1,0:T(4,128)(2,1)} %broadcast_in_dim.41), calls=%async_computation.1 | async-start | bytes 65536 | tf_op jit(solution)/shard_map/all_to_all | solution.py:61
  85.9 0.9 copy-start.1
  94.9 26.1 %copy-start.10 = (f32[128]{0:T(128)S(1)}, f32[128]{0:T(128)}, u32[]{:S(2)}) copy-start(f32[128]{0:T(128)} %param.21) | copy-start | bytes 1540
  99.7 13.2 %collective-permute-start.5 = (bf16[512,256]{1,0:T(8,128)(2,1)}, bf16[512,256]{1,0:T(8,128)(2,1)S(1)}, u32[]{:S(2)}, u32[]{:S(2)}) collective-permute-start(bf16[512,256]{1,0:T(8,128)(2,1)} %project.3.own_ref), channel_id=1, source_target_pairs={{0,4},{1,5},{2,6},{3,7},{4,8},{5,9},{6,10},{7,11},{8,12},{9,13},{1... | collective-permute-start | bytes 786440 | tf_op jit(solution)/shard_map/ppermute | solution.py:56
  112.9 13.6 %copy-start.5 = (bf16[512,256]{1,0:T(8,128)(2,1)}, bf16[512,256]{1,0:T(8,128)(2,1)S(1)}, u32[]{:S(2)}) copy-start(bf16[512,256]{1,0:T(8,128)(2,1)S(1)} %collective-permute-done.5.back1_ref) | copy-start | bytes 786436
  112.9 17.4 %collective-permute-start.6 = (bf16[512,256]{1,0:T(8,128)(2,1)S(1)}, bf16[512,256]{1,0:T(8,128)(2,1)S(1)}, u32[]{:S(2)}, u32[]{:S(2)}) collective-permute-start(bf16[512,256]{1,0:T(8,128)(2,1)S(1)} %collective-permute-done.5.back1_ref), channel_id=1, source_target_pairs={{0,4},{1,5},{2,6},{3,7},{4,8},{5,9},{6,10},{7,11},{8,12},{9,13},{1... | collective-permute-start | bytes 786440 | tf_op jit(solution)/shard_map/ppermute | solution.py:56
  130.3 0.7 copy-start.6
  136.3 4.8 %copy-start.2 = (bf16[128,2688]{1,0:T(8,128)(2,1)S(1)}, bf16[128,2688]{1,0:T(8,128)(2,1)}, u32[]{:S(2)}) copy-start(bf16[128,2688]{1,0:T(8,128)(2,1)} %copy-done.1) | copy-start | bytes 2064388
  136.3 18.9 %all-to-all-start.2 = ((bf16[8,256,256]{2,1,0:T(8,128)(2,1)}), bf16[8,256,256]{2,1,0:T(8,128)(2,1)S(1)}, u32[]{:S(2)}, u32[]{:S(2)}) async-start(bf16[8,256,256]{2,1,0:T(8,128)(2,1)} %attend.1), calls=%async_computation.2 | async-start | bytes 2097152 | tf_op jit(solution)/shard_map/all_to_all | solution.py:65
  155.2 1.0 copy-start
  156.2 17.1 %copy-start.7 = (s32[2]{0:T(128)S(1)}, s32[2]{0:T(128)}, u32[]{:S(2)}) copy-start(s32[2]{0:T(128)} %param.16) | copy-start | bytes 28
  156.2 17.1 %copy-start.8 = (s32[2]{0:T(128)S(1)}, s32[2]{0:T(128)}, u32[]{:S(2)}) copy-start(s32[2]{0:T(128)} %param.15) | copy-start | bytes 28
  161.2 12.0 %all-to-all-start.3 = ((f32[16,8,256]{2,1,0:T(8,128)}), f32[16,8,256]{2,1,0:T(8,128)S(1)}, u32[]{:S(2)}, u32[]{:S(2)}) async-start(f32[16,8,256]{2,1,0:T(8,128)} %token_sums.1), calls=%async_computation.3 | async-start | bytes 262144 | tf_op jit(solution)/shard_map/all_to_all | solution.py:65
  174.1 24.8 %all-to-all-start.4 = ((f32[32,1,2]{2,1,0:T(1,128)}), f32[32,1,2]{2,1,0:T(1,128)S(1)}, u32[]{:S(2)}, u32[]{:S(2)}) async-start(f32[32,1,2]{2,1,0:T(1,128)} %broadcast_in_dim.44), calls=%async_computation.4 | async-start | bytes 32768 | tf_op jit(solution)/shard_map/all_to_all | solution.py:61
Sparse Core Ops, SparseCore 0:
  47.3 47.5 all-gather.2
  97.0 49.3 all-gather.4
